TPU v7x, 32 devices: a 4x4x1 block of a 4x4x8 slice. The times are simulated.
32 devices in a mesh: dp: 1 (over z), ty: 4 (over y), tx: 8 (over x, core).
Axes of the slice: x: 4, y: 4, z: 1, core: 2. Of those that a mesh axis runs over, the one named last changes fastest.
The devices are a block of a 4x4x8 slice.
Arguments:
- x_in: bfloat16 [4, 1024, 4096], P(('dp', 'ty'), None, 'tx')
- w_q: bfloat16 [4096, 4096], P('tx', 'ty')
- w_k: bfloat16 [4096, 4096], P('tx', 'ty')
- w_v: bfloat16 [4096, 4096], P('tx', 'ty')
- w_o: bfloat16 [4096, 4096], P('ty', 'tx')
- w_gate: bfloat16 [4096, 11008], P('tx', 'ty')
- w_up: bfloat16 [4096, 11008], P('tx', 'ty')
- w_down: bfloat16 [11008, 4096], P('ty', 'tx')
Outputs:
- output: bfloat16 [4, 1024, 4096], P(('dp', 'ty'), None, 'tx')
All inputs are finite; a program needn't handle non-finite values.
Results may differ from a plain program's by a relative error of at most 0.02.
Values are sent between devices in bfloat16 or wider.
A program may use at most 768 MiB of HBM per device.

v0:
```python
import jax
import jax.numpy as jnp
from jax import lax
from jax.sharding import PartitionSpec as P, NamedSharding

HEAD_DIM = 128
EPS = 1e-5
THETA = 10000.0


def rotary(heads_bf):
    seq_len = heads_bf.shape[1]
    half_dim = HEAD_DIM // 2
    inv_freq = THETA ** (-2.0 * jnp.arange(half_dim, dtype=jnp.float32) / HEAD_DIM)
    angles = jnp.arange(seq_len, dtype=jnp.float32)[:, None] * inv_freq[None, :]
    cos_t = jnp.cos(angles)[:, None, :]
    sin_t = jnp.sin(angles)[:, None, :]
    values = heads_bf.astype(jnp.float32)
    lower_half = values[..., :half_dim]
    upper_half = values[..., half_dim:]
    return jnp.concatenate([lower_half * cos_t - upper_half * sin_t, upper_half * cos_t + lower_half * sin_t], axis=-1).astype(jnp.bfloat16)


def causal_attention(q_heads, k_heads, v_heads):
    seq_len = q_heads.shape[1]
    q_block = min(seq_len, 128)
    key_pos = jnp.arange(seq_len)
    scale_qk = HEAD_DIM ** -0.5

    def one_block(block_idx, out_acc):
        q_start = block_idx * q_block
        q_blk = lax.dynamic_slice_in_dim(q_heads, q_start, q_block, axis=1)
        scores = jnp.einsum("nqhd,nkhd->nhqk", q_blk, k_heads, preferred_element_type=jnp.float32) * scale_qk
        q_pos = q_start + jnp.arange(q_block)
        allowed = q_pos[:, None] >= key_pos[None, :]
        scores = jnp.where(allowed, scores, -1e30)
        prob_blk = jax.nn.softmax(scores, axis=-1).astype(jnp.bfloat16)
        blk_out = jnp.einsum("nhqk,nkhd->nqhd", prob_blk, v_heads, preferred_element_type=jnp.float32).astype(jnp.bfloat16)
        return lax.dynamic_update_slice_in_dim(out_acc, blk_out, q_start, axis=1)

    return lax.fori_loop(0, seq_len // q_block, one_block, jnp.zeros_like(q_heads))


def norm_sharded(values_bf, full_width):
    values = values_bf.astype(jnp.float32)
    moments = jnp.stack([jnp.sum(values, axis=-1), jnp.sum(values * values, axis=-1)], axis=-1)
    moments = lax.psum(moments, "tx")
    mean_val = moments[..., 0:1] / full_width
    var_val = moments[..., 1:2] / full_width - mean_val * mean_val
    return ((values - mean_val) * lax.rsqrt(var_val + EPS)).astype(jnp.bfloat16)


def project(rows_bf, weight):
    return jnp.einsum("...c,ch->...h", rows_bf, weight, preferred_element_type=jnp.float32).astype(jnp.bfloat16)


def solution(mesh):
    tx_count = mesh.shape["tx"]
    act_spec = P(("dp", "ty"), None, "tx")
    col_spec = P("tx", "ty")
    row_spec = P("ty", "tx")

    def layer_fn(x_blk, w_q, w_k, w_v, w_o, w_gate, w_up, w_down):
        full_width = x_blk.shape[-1] * tx_count
        normed_all = lax.all_gather(norm_sharded(x_blk, full_width), "ty", axis=0, tiled=True)
        q_sum, k_sum, v_sum = lax.psum((project(normed_all, w_q), project(normed_all, w_k), project(normed_all, w_v)), "tx")
        n_seqs, seq_len, local_cols = q_sum.shape
        head_shape = (n_seqs, seq_len, local_cols // HEAD_DIM, HEAD_DIM)
        attn_heads = causal_attention(rotary(q_sum.reshape(head_shape)), rotary(k_sum.reshape(head_shape)), v_sum.reshape(head_shape))
        attn_out = lax.psum_scatter(project(attn_heads.reshape(q_sum.shape), w_o), "ty", scatter_dimension=0, tiled=True)
        resid_h = (x_blk.astype(jnp.float32) + attn_out.astype(jnp.float32)).astype(jnp.bfloat16)
        normed_mlp = lax.all_gather(norm_sharded(resid_h, full_width), "ty", axis=0, tiled=True)
        gate_sum, up_sum = lax.psum((project(normed_mlp, w_gate), project(normed_mlp, w_up)), "tx")
        act_val = (jax.nn.silu(gate_sum.astype(jnp.float32)) * up_sum.astype(jnp.float32)).astype(jnp.bfloat16)
        mlp_out = lax.psum_scatter(project(act_val, w_down), "ty", scatter_dimension=0, tiled=True)
        return (resid_h.astype(jnp.float32) + mlp_out.astype(jnp.float32)).astype(jnp.bfloat16)

    return jax.shard_map(layer_fn, mesh=mesh, in_specs=(act_spec, col_spec, col_spec, col_spec, row_spec, col_spec, col_spec, row_spec), out_specs=act_spec, check_vma=False)
```

profile of v0, /device:TPU:97, one launch (start us, length us, event | category | flops | bytes accessed | tf_op | source)
XLA Modules:
  0.0 1539.0 jit_solution(17645382246313382992)
XLA Ops:
  8.3 14.1 psum.49
  25.1 47.9 %all-gather.3.cloned.1.call-done = bf16[4,1024,512]{2,1,0:T(8,128)(2,1)} async-done(((bf16[1,1024,512]{2,1,0:T(8,128)(2,1)}), bf16[4,1024,512]{2,1,0:T(8,128)(2,1)}) %all-gather.3.cloned.1.call-update) | async-done | bytes 4194320 | tf_op jit(solution)/shard_map/all_gather | solution.py:65
  73.0 10.3 convolution_convert_fusion.2
  83.2 11.6 copy.28
  94.9 10.3 convolution_convert_fusion.3
  105.1 11.3 copy.26
  116.5 10.3 convolution_convert_fusion.4
  126.7 11.3 copy.24
  141.4 253.8 %all-reduce.7.cloned.1.call-done = (bf16[4,1024,8,128]{3,1,2,0:T(8,128)(2,1)}, bf16[4,1024,8,128]{3,1,2,0:T(8,128)(2,1)}, bf16[4,1024,8,128]{3,1,2,0:T(8,128)(2,1)}) async-done(((bf16[4,1024,8,128]{3,1,2,0:T(8,128)(2,1)}, bf16[4,1024,8,128]{3,1,2,0:T(8,128)(2,1)}, bf16[4,1024,8,128]{3,1,2,0:T(8,128)(2,1)}), (bf16[4,1024,8,128]{3,1,2,0:T(8,128)(2,1)}, bf16[4,1024,8,128]{3,1,2,0:T(8,128)(2,1)}, ...) | async-done | bytes 25165840 | tf_op jit(solution)/shard_map/psum | solution.py:66
  395.2 11.1 convert_element_type.91
  406.3 11.2 convert_element_type.94
  417.5 34.3 %subtract_convert_fusion = (bf16[4,1024,8,64]{3,1,2,0:T(8,128)(2,1)}, bf16[4,1024,8,64]{3,1,2,0:T(8,128)(2,1)}, bf16[4,1024,8,64]{3,1,2,0:T(8,128)(2,1)}, bf16[4,1024,8,64]{3,1,2,0:T(8,128)(2,1)}) fusion(f32[4,1024,8,128]{3,1,2,0:T(8,128)} %convert_element_type.94, f32[1024,64]{1,0:T(8,128)} %get-tuple-element.160, f32[1024,64]{1,0:T(8,128)S(1)} %get-tuple-element.159, ...), kind=kLoop, calls=%fused_computation.31 | loop fusion | flops 33554432 | bytes 50855936 | tf_op jit(solution)/shard_map/convert.2
  451.7 19.0 %pad_maximum_fusion = (bf16[4,1024,8,128]{3,1,2,0:T(8,128)(2,1)}, bf16[4,1024,8,128]{3,1,2,0:T(8,128)(2,1)}) fusion(bf16[4,1024,8,64]{3,1,2,0:T(8,128)(2,1)} %get-tuple-element.153, bf16[4,1024,8,64]{3,1,2,0:T(8,128)(2,1)} %get-tuple-element.154, bf16[4,1024,8,64]{3,1,2,0:T(8,128)(2,1)} %get-tuple-element.150, bf16[4,1024,8,64]{3,1,2,0:T(8,128)(2,1)} %get-tuple-element.149), kind=kLoop, calls=%fused_computation.34 | loop fusion | flops 33554432 | bytes 33554432 | tf_op jit(solution)/shard_map/concatenate | solution.py:21
  470.7 4.3 broadcast_in_dim.35.clone
  475.0 389.2 %while.14 = (s32[]{:T(128)}, bf16[4,1024,8,128]{1,3,2,0:T(8,128)(2,1)}, bf16[4,1024,8,128]{3,1,2,0:T(8,128)(2,1)}, bf16[4,1024,8,128]{3,1,2,0:T(8,128)(2,1)}, bf...) while((s32[]{:T(128)}, ...), condition=%wide.region_9.10_spmd.clone, body=%wide.region_6.9_spmd.clone.sunk | while | flops 2181694464 | bytes 90473616 | solution.py:41
  475.3 11.8 fusion.66
  487.1 20.4 %fusion.67 = (f32[4,8,128]{2,1,0:T(8,128)S(1)}, f32[4,8,128,1024]{3,2,1,0:T(8,128)}) fusion(f32[4,8,128,1024]{3,2,1,0:T(8,128)} %fusion.66, pred[128,1024]{1,0:T(8,128)(4,1)S(1)} %iota_compare_fusion.2), kind=kOutput, calls=%fused_computation.79.clone.1 | output fusion | flops 25166848 | bytes 33701888 | tf_op jit(solution)/shard_map/while/body/eval_jaxpr/sub | solution.py:37
  507.5 11.6 fusion.68
  524.0 11.8 fusion.66
  535.8 20.4 %fusion.67 = (f32[4,8,128]{2,1,0:T(8,128)S(1)}, f32[4,8,128,1024]{3,2,1,0:T(8,128)}) fusion(f32[4,8,128,1024]{3,2,1,0:T(8,128)} %fusion.66, pred[128,1024]{1,0:T(8,128)(4,1)S(1)} %iota_compare_fusion.2), kind=kOutput, calls=%fused_computation.79.clone.1 | output fusion | flops 25166848 | bytes 33701888 | tf_op jit(solution)/shard_map/while/body/eval_jaxpr/sub | solution.py:37
  556.2 11.6 fusion.68
  572.6 11.8 fusion.66
  584.4 20.4 %fusion.67 = (f32[4,8,128]{2,1,0:T(8,128)S(1)}, f32[4,8,128,1024]{3,2,1,0:T(8,128)}) fusion(f32[4,8,128,1024]{3,2,1,0:T(8,128)} %fusion.66, pred[128,1024]{1,0:T(8,128)(4,1)S(1)} %iota_compare_fusion.2), kind=kOutput, calls=%fused_computation.79.clone.1 | output fusion | flops 25166848 | bytes 33701888 | tf_op jit(solution)/shard_map/while/body/eval_jaxpr/sub | solution.py:37
  604.8 11.6 fusion.68
  621.2 11.8 fusion.66
  633.0 20.4 %fusion.67 = (f32[4,8,128]{2,1,0:T(8,128)S(1)}, f32[4,8,128,1024]{3,2,1,0:T(8,128)}) fusion(f32[4,8,128,1024]{3,2,1,0:T(8,128)} %fusion.66, pred[128,1024]{1,0:T(8,128)(4,1)S(1)} %iota_compare_fusion.2), kind=kOutput, calls=%fused_computation.79.clone.1 | output fusion | flops 25166848 | bytes 33701888 | tf_op jit(solution)/shard_map/while/body/eval_jaxpr/sub | solution.py:37
  653.4 11.6 fusion.68
  669.8 11.8 fusion.66
  681.6 20.4 %fusion.67 = (f32[4,8,128]{2,1,0:T(8,128)S(1)}, f32[4,8,128,1024]{3,2,1,0:T(8,128)}) fusion(f32[4,8,128,1024]{3,2,1,0:T(8,128)} %fusion.66, pred[128,1024]{1,0:T(8,128)(4,1)S(1)} %iota_compare_fusion.2), kind=kOutput, calls=%fused_computation.79.clone.1 | output fusion | flops 25166848 | bytes 33701888 | tf_op jit(solution)/shard_map/while/body/eval_jaxpr/sub | solution.py:37
  702.0 11.6 fusion.68
  718.4 11.8 fusion.66
  730.2 20.4 %fusion.67 = (f32[4,8,128]{2,1,0:T(8,128)S(1)}, f32[4,8,128,1024]{3,2,1,0:T(8,128)}) fusion(f32[4,8,128,1024]{3,2,1,0:T(8,128)} %fusion.66, pred[128,1024]{1,0:T(8,128)(4,1)S(1)} %iota_compare_fusion.2), kind=kOutput, calls=%fused_computation.79.clone.1 | output fusion | flops 25166848 | bytes 33701888 | tf_op jit(solution)/shard_map/while/body/eval_jaxpr/sub | solution.py:37
  750.6 11.6 fusion.68
  767.0 11.8 fusion.66
  778.8 20.4 %fusion.67 = (f32[4,8,128]{2,1,0:T(8,128)S(1)}, f32[4,8,128,1024]{3,2,1,0:T(8,128)}) fusion(f32[4,8,128,1024]{3,2,1,0:T(8,128)} %fusion.66, pred[128,1024]{1,0:T(8,128)(4,1)S(1)} %iota_compare_fusion.2), kind=kOutput, calls=%fused_computation.79.clone.1 | output fusion | flops 25166848 | bytes 33701888 | tf_op jit(solution)/shard_map/while/body/eval_jaxpr/sub | solution.py:37
  799.2 11.6 fusion.68
  815.6 11.8 fusion.66
  827.4 20.4 %fusion.67 = (f32[4,8,128]{2,1,0:T(8,128)S(1)}, f32[4,8,128,1024]{3,2,1,0:T(8,128)}) fusion(f32[4,8,128,1024]{3,2,1,0:T(8,128)} %fusion.66, pred[128,1024]{1,0:T(8,128)(4,1)S(1)} %iota_compare_fusion.2), kind=kOutput, calls=%fused_computation.79.clone.1 | output fusion | flops 25166848 | bytes 33701888 | tf_op jit(solution)/shard_map/while/body/eval_jaxpr/sub | solution.py:37
  847.7 11.6 fusion.68
  864.2 10.1 convolution_convert_fusion.5
  874.5 44.3 %reduce-scatter.3.cloned.1.call-done = bf16[1,1024,512]{2,1,0:T(8,128)(2,1)} async-done(((bf16[4,1024,512]{2,1,0:T(8,128)(2,1)}), bf16[1,1024,512]{2,1,0:T(8,128)(2,1)}) %reduce-scatter.3.cloned.1.call-update) | async-done | bytes 1048592 | tf_op jit(solution)/shard_map/reduce_scatter | solution.py:70
  921.6 13.0 psum.53
  937.3 44.5 %all-gather.5.cloned.1.call-done = bf16[4,1024,512]{2,1,0:T(8,128)(2,1)} async-done(((bf16[1,1024,512]{2,1,0:T(8,128)(2,1)}), bf16[4,1024,512]{2,1,0:T(8,128)(2,1)}) %all-gather.5.cloned.1.call-update) | async-done | bytes 4194320 | tf_op jit(solution)/shard_map/all_gather | solution.py:72
  981.8 17.9 %convolution_convert_fusion = bf16[4,1024,2752]{1,2,0:T(8,128)(2,1)} fusion(bf16[4,1024,512]{2,1,0:T(8,128)(2,1)} %all-gather.5.cloned.1.call-done, bf16[512,2752]{0,1:T(8,128)(2,1)S(1)} %copy-done), kind=kOutput, calls=%fused_computation.28 | convolution fusion | flops 11553996800 | bytes 29556736 | tf_op jit(solution)/shard_map/...c,ch->...h/dot_general | solution.py:54
  999.7 19.1 %convolution_convert_fusion.1 = bf16[4,1024,2752]{1,2,0:T(8,128)(2,1)} fusion(bf16[4,1024,512]{2,1,0:T(8,128)(2,1)} %all-gather.5.cloned.1.call-done, bf16[512,2752]{0,1:T(8,128)(2,1)} %param.15), kind=kOutput, calls=%fused_computation.29 | convolution fusion | flops 11553996800 | bytes 29556736 | tf_op jit(solution)/shard_map/...c,ch->...h/dot_general | solution.py:54
  1018.9 443.9 %all-reduce.5.cloned.1.call-done = (bf16[4,1024,2752]{1,2,0:T(8,128)(2,1)}, bf16[4,1024,2752]{1,2,0:T(8,128)(2,1)}) async-done(((bf16[4,1024,2752]{1,2,0:T(8,128)(2,1)}, bf16[4,1024,2752]{1,2,0:T(8,128)(2,1)}), (bf16[4,1024,2752]{1,2,0:T(8,128)(2,1)}, bf16[4,1024,2752]{1,2,0:T(8,128)(2,1)})) %all-reduce.5.cloned.1.call-update) | async-done | bytes 45088784 | tf_op jit(solution)/shard_map/psum | solution.py:73
  1462.9 21.7 %fusion.25 = bf16[4,1024,512]{2,1,0:T(8,128)(2,1)} fusion(bf16[2752,512]{1,0:T(8,128)(2,1)} %param.17, bf16[4,1024,2752]{1,2,0:T(8,128)(2,1)} %get-tuple-element.141, bf16[4,1024,2752]{1,2,0:T(8,128)(2,1)} %get-tuple-element.142), kind=kOutput, calls=%fused_computation.50 | convolution fusion | flops 11634999296 | bytes 52101120 | tf_op jit(solution)/shard_map/...c,ch->...h/dot_general | solution.py:54
  1484.6 44.4 %reduce-scatter.5.cloned.1.call-done = bf16[1,1024,512]{2,1,0:T(8,128)(2,1)} async-done(((bf16[4,1024,512]{2,1,0:T(8,128)(2,1)}), bf16[1,1024,512]{2,1,0:T(8,128)(2,1)}) %reduce-scatter.5.cloned.1.call-update) | async-done | bytes 1048592 | tf_op jit(solution)/shard_map/reduce_scatter | solution.py:75
  (57 shorter events, 55.0 us)
Async XLA Ops:
  6.5 975.2 %copy-start = (bf16[512,2752]{0,1:T(8,128)(2,1)S(1)}, bf16[512,2752]{0,1:T(8,128)(2,1)}, u32[]{:S(2)}) copy-start(bf16[512,2752]{0,1:T(8,128)(2,1)} %param.16) | copy-start | bytes 8454148
  6.6 66.4 %all-gather.3.cloned.1.call-start = ((), (), s32[]{:S(2)}) async-start(), calls=%async_computation.2 | async-start | bytes 5242880 | tf_op jit(solution)/shard_map/all_gather | solution.py:65
  25.0 370.2 %all-reduce.7.cloned.1.call-start = ((), (), s32[]{:S(2)}) async-start(), calls=%async_computation.7 | async-start | bytes 50331648 | tf_op jit(solution)/shard_map/psum | solution.py:66
  138.1 780.7 %reduce-scatter.3.cloned.1.call-start = ((), (), s32[]{:S(2)}) async-start(), calls=%async_computation.3 | async-start | bytes 5242880 | tf_op jit(solution)/shard_map/reduce_scatter | solution.py:70
  874.4 107.4 %all-gather.5.cloned.1.call-start = ((), (), s32[]{:S(2)}) async-start(), calls=%async_computation.4 | async-start | bytes 5242880 | tf_op jit(solution)/shard_map/all_gather | solution.py:72
  937.2 525.6 %all-reduce.5.cloned.1.call-start = ((), (), s32[]{:S(2)}) async-start(), calls=%async_computation.6 | async-start | bytes 90177536 | tf_op jit(solution)/shard_map/psum | solution.py:73
  1018.8 510.2 %reduce-scatter.5.cloned.1.call-start = ((), (), s32[]{:S(2)}) async-start(), calls=%async_computation.5 | async-start | bytes 5242880 | tf_op jit(solution)/shard_map/reduce_scatter | solution.py:75
Sparse Core Ops, SparseCore 0:
  25.1 47.7 all-gather.2
  138.2 256.9 all-reduce.6
  874.5 44.2 reduce-scatter.2
  937.3 44.4 all-gather.4
  1019.0 443.8 all-reduce.4
  1484.8 44.2 reduce-scatter.4
where the time goes:
time: 1550 us; the launch traced here: 1540 us
  waiting for transfers between devices  879 us (57%)
  matrix products  287 us (19%)
  other arithmetic  256 us (17%)
  local copies, waits for them, and re-layouts  76 us (5%)
  blocking collectives  27 us (2%)
    psum x1, waiting for transfers between devices, layer_fn(): lax.psum((project(normed_mlp, w_gate), project(normed_mlp, w_up)), 'tx')  444 us
    psum x1, waiting for transfers between devices, layer_fn(): lax.psum((project(normed_all, w_q), project(normed_all, w_k), project(nor...  254 us
    sub x8, other arithmetic, one_block(): prob_blk = jax.nn.softmax(scores, axis=-1).astype(jnp.bfloat16)  163 us
    dot_general x7, matrix products, project(): jnp.einsum('...c,ch->...h', rows_bf, weight, preferred_element_type=jnp.f...  99.6 us
    dot_general x8, matrix products, one_block(): jnp.einsum('nqhd,nkhd->nhqk', q_blk, k_heads, preferred_element_type=jnp....  94.3 us
    dot_general x8, matrix products, one_block(): jnp.einsum('nhqk,nkhd->nqhd', prob_blk, v_heads, preferred_element_type=j...  92.7 us
    all_gather x1, waiting for transfers between devices, layer_fn(): lax.all_gather(norm_sharded(x_blk, full_width), 'ty', axis=0, tiled=True)  47.9 us
    all_gather x1, waiting for transfers between devices, layer_fn(): lax.all_gather(norm_sharded(resid_h, full_width), 'ty', axis=0, tiled=True)  44.5 us
  transfers between devices with their start and end apart: 6, of which 6 were waited for; matrix products, arithmetic and copies ran while one was open for 0% of the time, Pallas kernels for 0%

commit v1 on v0

v1 whole, which is shorter than its diff:
```python
import functools

import jax
import jax.numpy as jnp
from jax import lax
from jax.experimental import pallas as pl
from jax.experimental.pallas import tpu as pltpu
from jax.sharding import PartitionSpec as P

HEAD_DIM = 128
EPS = 1e-5
THETA = 10000.0
MESH = pl.DeviceIdType.MESH
F32 = jnp.float32
BF16 = jnp.bfloat16
NX = 4
NJ = 4
NCH = 16
STAGES = 4
VMEM_LIMIT = 67_043_328


def rem(a, b):
    return lax.rem(a, jnp.int32(b))


def div(a, b):
    return lax.div(a, jnp.int32(b))


def al(v, m):
    return pl.multiple_of(v, m)


def remote(src, dst, ssem, rsem, dev):
    return pltpu.make_async_remote_copy(src_ref=src, dst_ref=dst, send_sem=ssem, recv_sem=rsem, device_id=dev, device_id_type=MESH)


def chunk_of(n):
    is_c = div(n, 12)
    is_a = div(15 - n, 12)
    is_b = 1 - is_a - is_c
    j = is_a * n + is_b * (div(n + 12, 2) - 8) + is_c * (n - 12)
    r = is_b * (3 - 2 * rem(n, 2)) + 2 * is_c
    return r, j


class Place:
    def __init__(self):
        tx, ty = lax.axis_index("tx"), lax.axis_index("ty")
        self.x, self.c, self.y = div(tx, 2), rem(tx, 2), ty
        x, c, y = self.x, self.c, self.y
        self.xr, self.xl, self.xo = rem(x + 1, NX), rem(x + 3, NX), rem(x + 2, NX)
        self.yu, self.yd, self.yo = rem(y + 1, NX), rem(y + 3, NX), rem(y + 2, NX)
        self.right = {"tx": self.xr * 2 + c, "ty": y}
        self.left = {"tx": self.xl * 2 + c, "ty": y}
        self.up = {"tx": tx, "ty": self.yu}
        self.down = {"tx": tx, "ty": self.yd}
        self.partner = {"tx": x * 2 + 1 - c, "ty": y}

    def barrier(self):
        sem = pltpu.get_barrier_semaphore()
        for dev in (self.right, self.left, self.up, self.down, self.partner):
            pl.semaphore_signal(sem, inc=1, device_id=dev, device_id_type=MESH)
        pl.semaphore_wait(sem, 5)


class Gather:
    def __init__(self, at, src, xg, kc, ch, sx, rx, sy, ry):
        self.at, self.src, self.xg, self.kc, self.ch, self.h = at, src, xg, kc, ch, ch // 2
        self.sx, self.rx, self.sy, self.ry = sx, rx, sy, ry

    def cols(self, x):
        return pl.ds(al(x * self.kc, 128), self.kc)

    def keep_own(self, j):
        self.xg[self.at.y, j, :, self.cols(self.at.x)] = self.src[j]

    def xcopy(self, kind, j):
        at, h, ch = self.at, self.h, self.ch
        if kind < 2:
            src, dst = self.src.at[j], self.xg.at[at.y, j, :, self.cols(at.x)]
        elif kind == 2:
            src = dst = self.xg.at[at.y, j, pl.ds(0, h), self.cols(at.xl)]
        else:
            src = dst = self.xg.at[at.y, j, pl.ds(h, ch - h), self.cols(at.xr)]
        return remote(src, dst, self.sx.at[kind, j], self.rx.at[kind, j], at.left if kind % 2 else at.right)

    def xwait(self, kind, j):
        at, h, ch = self.at, self.h, self.ch
        dst = (
            lambda: self.xg.at[at.y, j, :, self.cols(at.xl)],
            lambda: self.xg.at[at.y, j, :, self.cols(at.xr)],
            lambda: self.xg.at[at.y, j, pl.ds(0, h), self.cols(at.xo)],
            lambda: self.xg.at[at.y, j, pl.ds(h, ch - h), self.cols(at.xo)],
        )[kind]()
        remote(dst, dst, self.sx.at[kind, j], self.rx.at[kind, j], at.right).wait_recv()

    def ycopy(self, kind, j):
        at, h, ch = self.at, self.h, self.ch
        if kind < 2:
            ref = self.xg.at[at.y, j]
        elif kind == 2:
            ref = self.xg.at[at.yd, j, pl.ds(0, h)]
        else:
            ref = self.xg.at[at.yu, j, pl.ds(h, ch - h)]
        return remote(ref, ref, self.sy.at[kind, j], self.ry.at[kind, j], at.down if kind % 2 else at.up)

    def ywait(self, kind, j):
        at, h, ch = self.at, self.h, self.ch
        dst = (
            lambda: self.xg.at[at.yd, j],
            lambda: self.xg.at[at.yu, j],
            lambda: self.xg.at[at.yo, j, pl.ds(0, h)],
            lambda: self.xg.at[at.yo, j, pl.ds(h, ch - h)],
        )[kind]()
        remote(dst, dst, self.sy.at[kind, j], self.ry.at[kind, j], at.up).wait_recv()

    def full(self, j):
        self.xcopy(0, j).start()
        self.xcopy(1, j).start()

    def pass_on(self, j):
        self.xwait(0, j)
        self.xwait(1, j)
        self.xcopy(2, j).start()
        self.xcopy(3, j).start()

    def finish(self, j):
        self.xwait(2, j)
        self.xwait(3, j)
        self.xcopy(2, j).wait_send()
        self.xcopy(3, j).wait_send()
        width = self.xg.shape[-1]
        rows = 8

        def body(i, carry):
            at_rows = pl.ds(al(i * rows, rows), rows)
            v = self.xg[self.at.y, j, at_rows, :].astype(F32)
            mean = jnp.sum(v, axis=-1, keepdims=True) / width
            var = jnp.sum(v * v, axis=-1, keepdims=True) / width - mean * mean
            self.xg[self.at.y, j, at_rows, :] = ((v - mean) * lax.rsqrt(var + EPS)).astype(BF16)
            return carry

        lax.fori_loop(0, self.ch // rows, body, 0)
        self.ycopy(0, j).start()
        self.ycopy(1, j).start()

    def arrive(self, n):
        _, j = chunk_of(n)

        @pl.when(n < 12)
        def _():
            @pl.when(rem(n, 2) == 0)
            def _():
                self.ywait(0, j)
                self.ycopy(2, j).start()

            @pl.when(rem(n, 2) == 1)
            def _():
                self.ywait(1, j)
                self.ycopy(3, j).start()

        @pl.when(n >= 12)
        def _():
            self.ywait(2, j)
            self.ywait(3, j)

    def drain(self):
        for j in range(NJ):
            self.xcopy(0, j).wait_send()
            self.xcopy(1, j).wait_send()
            for kind in range(4):
                self.ycopy(kind, j).wait_send()


class Reduce:
    def __init__(self, at, zb, ya, yb, yfd, yfu, ss, rs):
        self.at, self.zb, self.ya, self.yb, self.yfd, self.yfu, self.ss, self.rs = at, zb, ya, yb, yfd, yfu, ss, rs
        self.ch = zb.shape[2]
        self.h = self.ch // 2

    def copy(self, kind, j):
        at, h, ch = self.at, self.h, self.ch
        src, dst = (
            lambda: (self.zb.at[2, j, pl.ds(0, h)], self.ya.at[j]),
            lambda: (self.zb.at[2, j, pl.ds(h, ch - h)], self.yb.at[j]),
            lambda: (self.zb.at[1, j], self.yfd.at[j]),
            lambda: (self.zb.at[3, j], self.yfu.at[j]),
        )[kind]()
        return remote(src, dst, self.ss.at[kind, j], self.rs.at[kind, j], at.down if kind % 2 else at.up)

    def wait(self, kind, j):
        self.copy(kind, j).wait_recv()

    def halves(self, j):
        self.copy(0, j).start()
        self.copy(1, j).start()

    def middle(self, j):
        h = self.h
        self.wait(0, j)
        self.zb[1, j, 0:h] = (self.zb[1, j, 0:h].astype(F32) + self.ya[j].astype(F32)).astype(BF16)
        self.copy(2, j).start()
        self.wait(1, j)
        self.zb[3, j, h:] = (self.zb[3, j, h:].astype(F32) + self.yb[j].astype(F32)).astype(BF16)
        self.copy(3, j).start()

    def total(self, j):
        self.wait(2, j)
        self.wait(3, j)
        return self.zb[0, j].astype(F32) + self.yfd[j].astype(F32) + self.yfu[j].astype(F32)

    def drain(self):
        for j in range(NJ):
            for kind in range(4):
                self.copy(kind, j).wait_send()


def attention_kernel(
    x_ref, cos_ref, sin_ref, wq, wk, wv, wo, wg_t, wu_t, wdn,
    h_ref, w_all,
    xc, xg, wb, wrel, wob, qkv, kvo, kvp, og, zb, ya, yb, yfd, yfu, own, drel_r, drel_l,
    sx, rx, sy, ry, sd, rd, swd, rwd, swo, rwo, swf, rwf, swp, rwp, lw, so, ro, skv, rkv, sog, rog, syr, ryr,
    lg, sw, rw, swx, rwx, swy, rwy, swz, rwz,
):
    at = Place()
    x, c, y = at.x, at.c, at.y
    ch, kc, h = xc.shape[1], xc.shape[2], xc.shape[1] // 2
    kd = wq.shape[0]
    hc = wb.shape[1] // 3
    fc = w_all.shape[1]
    f_r = drel_r.shape[1]
    gather = Gather(at, xc, xg, kc, ch, sx, rx, sy, ry)
    reduce = Reduce(at, zb, ya, yb, yfd, yfu, syr, ryr)
    weights = (wq, wk, wv)
    my_rows = lambda xx: al((2 * xx + c) * kd, 128)
    half_cols = lambda core: pl.ds(al(core * kd, 128), kd)

    def head_cols(xx):
        return pl.ds(al(xx * hc, 128), hc)

    def w_direct(d, i):
        to, dev = (at.xl, at.left) if d else (at.xr, at.right)
        return remote(weights[i].at[:, head_cols(to)], wb.at[pl.ds(my_rows(x), kd), pl.ds(i * hc, hc)], swd.at[d, i], rwd.at[d, i], dev)

    def w_direct_wait(d, i):
        dst = wb.at[pl.ds(my_rows(at.xr if d else at.xl), kd), pl.ds(i * hc, hc)]
        remote(dst, dst, swd.at[d, i], rwd.at[d, i], at.right).wait_recv()

    def w_opp(d, i):
        rows = pl.ds(d * (kd // 2), kd // 2)
        return remote(weights[i].at[rows, head_cols(at.xo)], wrel.at[d, :, pl.ds(i * hc, hc)], swo.at[d, i], rwo.at[d, i], at.left if d else at.right)

    def w_fwd(d):
        src_x = at.xr if d else at.xl
        dst = wb.at[pl.ds(al(my_rows(src_x) + d * (kd // 2), 128), kd // 2)]
        return remote(wrel.at[d], dst, swf.at[d], rwf.at[d], at.left if d else at.right)

    def w_fwd_wait(d):
        dst = wb.at[pl.ds(al(my_rows(at.xo) + d * (kd // 2), 128), kd // 2)]
        remote(dst, dst, swf.at[d], rwf.at[d], at.right).wait_recv()

    def w_own_pair(i):
        return remote(weights[i].at[:, head_cols(x)], wb.at[pl.ds(my_rows(x), kd), pl.ds(i * hc, hc)], swp.at[i], rwp.at[i], at.partner)

    def w_pair(k):
        src = wb.at[pl.ds(my_rows((at.xl, at.xr, at.xo)[k]), kd)]
        return remote(src, src, swp.at[3 + k], rwp.at[3 + k], at.partner)

    def w_pair_wait(k):
        other = lambda xx: al((2 * xx + 1 - c) * kd, 128)
        if k < 3:
            dst = wb.at[pl.ds(other(x), kd), pl.ds(k * hc, hc)]
        else:
            dst = wb.at[pl.ds(other((at.xl, at.xr, at.xo)[k - 3]), kd)]
        remote(dst, dst, swp.at[k], rwp.at[k], at.partner).wait_recv()

    def w_own_local(i):
        return pltpu.make_async_copy(weights[i].at[:, head_cols(x)], wb.at[pl.ds(my_rows(x), kd), pl.ds(i * hc, hc)], lw.at[i])

    wo_local = pltpu.make_async_copy(wo, wob.at[:, half_cols(c)], lw.at[3])
    wo_pair = remote(wo, wob.at[:, half_cols(c)], so.at[0], ro.at[0], at.partner)

    mlp_weights = (wg_t, wu_t, wdn)
    parts = ((0, f_r), (f_r, fc - f_r))

    def d_cols(xx, core):
        return pl.ds(al((2 * xx + core) * kd, 128), kd)

    def d_direct(m, d, p):
        to, dev = (at.xl, at.left) if d else (at.xr, at.right)
        off, size = parts[p]
        src = mlp_weights[m].at[pl.ds(al(to * fc + off, 8), size)]
        return remote(src, w_all.at[m, pl.ds(off, size), d_cols(x, c)], sw.at[m, d, p], rw.at[m, d, p], dev)

    def d_direct_wait(m, d, p):
        off, size = parts[p]
        dst = w_all.at[m, pl.ds(off, size), d_cols(at.xr if d else at.xl, c)]
        remote(dst, dst, sw.at[m, d, p], rw.at[m, d, p], at.right).wait_recv()

    def d_opp(m, d):
        off, size = parts[d]
        src = mlp_weights[m].at[pl.ds(al(at.xo * fc + off, 8), size)]
        return remote(src, (drel_r, drel_l)[d].at[m], swx.at[m, d], rwx.at[m, d], at.left if d else at.right)

    def d_fwd(m, d):
        off, size = parts[d]
        src_x = at.xr if d else at.xl
        dst = w_all.at[m, pl.ds(off, size), d_cols(src_x, c)]
        return remote((drel_r, drel_l)[d].at[m], dst, swy.at[m, d], rwy.at[m, d], at.left if d else at.right)

    def d_fwd_wait(m, d):
        off, size = parts[d]
        dst = w_all.at[m, pl.ds(off, size), d_cols(at.xo, c)]
        remote(dst, dst, swy.at[m, d], rwy.at[m, d], at.right).wait_recv()

    def d_in(m):
        return pltpu.make_async_copy(mlp_weights[m].at[pl.ds(al(x * fc, 8), fc)], own.at[m], lg.at[0, m])

    def d_out(m):
        return pltpu.make_async_copy(own.at[m], w_all.at[m, :, d_cols(x, c)], lg.at[1, m])

    def d_pair(m, k):
        dst = w_all.at[m, :, d_cols((at.xl, at.xr, at.xo, x)[k], c)]
        return remote(own.at[m] if k == 3 else dst, dst, swz.at[m, k], rwz.at[m, k], at.partner)

    def d_pair_wait(m, k):
        dst = w_all.at[m, :, d_cols((at.xl, at.xr, at.xo, x)[k], 1 - c)]
        remote(dst, dst, swz.at[m, k], rwz.at[m, k], at.partner).wait_recv()

    def d_pairs(m):
        for d in range(2):
            for p in range(2):
                d_direct_wait(m, d, p)
            d_pair(m, d).start()
        for d in range(2):
            d_fwd_wait(m, d)
        d_pair(m, 2).start()

    def d_turn(m):
        for d in range(2):
            d_opp(m, d).wait_recv()
            d_fwd(m, d).start()

    for i in range(3):
        w_own_local(i).start()
    wo_local.start()
    for m in range(3):
        d_in(m).start()

    def x_rows(j, core):
        return pl.ds(al((2 * j + core) * ch, 8), ch)

    def x_pair(j):
        return remote(x_ref.at[x_rows(j, 1 - c)], xc.at[j, :, half_cols(c)], sd.at[j], rd.at[j], at.partner)

    def x_pair_wait(j):
        dst = xc.at[j, :, half_cols(1 - c)]
        remote(dst, dst, sd.at[j], rd.at[j], at.partner).wait_recv()

    for j in range(NJ):
        xc[j, :, half_cols(c)] = x_ref[x_rows(j, c), :]
    at.barrier()
    for j in range(NJ):
        x_pair(j).start()
    for i in range(3):
        w_own_pair(i).start()
    wo_pair.start()
    for j in range(2):
        x_pair_wait(j)
        gather.full(j)
        gather.keep_own(j)
    gather.pass_on(0)
    for j in range(2, NJ):
        x_pair_wait(j)
        gather.full(j)
        gather.keep_own(j)
        gather.pass_on(j - 1)
        gather.finish(j - 2)
    for d in range(2):
        for i in range(3):
            w_opp(d, i).start()
    gather.pass_on(NJ - 1)
    for d in range(2):
        for i in range(3):
            w_direct(d, i).start()
    gather.finish(NJ - 2)
    gather.finish(NJ - 1)
    for d in range(2):
        for i in range(3):
            w_opp(d, i).wait_recv()
        w_fwd(d).start()
    for m in range(3):
        d_in(m).wait()
        d_out(m).start()
        d_pair(m, 3).start()
    for i in range(3):
        w_own_local(i).wait()
    wo_local.wait()
    for d in range(2):
        for i in range(3):
            w_direct_wait(d, i)
        w_pair(d).start()
    for d in range(2):
        w_fwd_wait(d)
    w_pair(2).start()
    for k in range(6):
        w_pair_wait(k)
    wo_pair.wait_recv()

    def kv_copy(s, j, n):
        return remote(kvo.at[s, j], kvp.at[s, j], skv.at[n], rkv.at[n], at.partner)

    def og_copy(kind, n):
        cols = lambda xx: pl.ds(al(xx * hc, 128), hc)
        if kind < 2:
            ref = og.at[n, :, cols(x)]
        elif kind == 2:
            ref = og.at[n, pl.ds(0, h), cols(at.xl)]
        else:
            ref = og.at[n, pl.ds(h, ch - h), cols(at.xr)]
        return remote(ref, ref, sog.at[kind, n], rog.at[kind, n], at.left if kind % 2 else at.right)

    def og_wait(kind, n):
        cols = lambda xx: pl.ds(al(xx * hc, 128), hc)
        dst = (
            lambda: og.at[n, :, cols(at.xl)],
            lambda: og.at[n, :, cols(at.xr)],
            lambda: og.at[n, pl.ds(0, h), cols(at.xo)],
            lambda: og.at[n, pl.ds(h, ch - h), cols(at.xo)],
        )[kind]()
        remote(dst, dst, sog.at[kind, n], rog.at[kind, n], at.right).wait_recv()

    def project(n):
        r, j = chunk_of(n)
        s = rem(y + r, NX)

        def body(i, carry):
            cols = pl.ds(al(i * hc, 128), hc)
            qkv[rem(n, 2), :, cols] = jnp.dot(xg[s, j], wb[:, cols], preferred_element_type=F32).astype(BF16)
            return carry

        lax.fori_loop(0, 3, body, 0)
        rows = pl.ds(al((2 * j + c) * ch, 8), ch)
        cos_t, sin_t = cos_ref[rows, :], sin_ref[rows, :]

        def turned(col):
            v = qkv[rem(n, 2), :, col : col + HEAD_DIM].astype(F32)
            return (v * cos_t + pltpu.roll(v, HEAD_DIM // 2, axis=1) * sin_t).astype(BF16)

        for col in range(0, hc, HEAD_DIM):
            qkv[rem(n, 2), :, col : col + HEAD_DIM] = turned(col)
        for col in range(0, hc, HEAD_DIM):
            kvo[s, j, :, col : col + HEAD_DIM] = turned(hc + col)
        kvo[s, j, :, hc:] = qkv[rem(n, 2), :, 2 * hc :]
        kv_copy(s, j, n).start()

    def attend(n):
        r, j = chunk_of(n)
        s = rem(y + r, NX)
        kv_copy(s, j, n).wait_recv()

        def one(jj):
            keys = (jj + 1) * ch
            iq = lax.broadcasted_iota(jnp.int32, (ch, keys), 0) + jj * ch
            ik = lax.broadcasted_iota(jnp.int32, (ch, keys), 1)
            own_ok = iq >= ik
            par_ok = ik < (jj + c) * ch
            contract = (((1,), (1,)), ((), ()))
            for head in range(hc // HEAD_DIM):
                lo = head * HEAD_DIM
                q = qkv[rem(n, 2), :, lo : lo + HEAD_DIM]
                k_own = kvo[s, 0 : jj + 1, :, lo : lo + HEAD_DIM].reshape(keys, HEAD_DIM)
                k_par = kvp[s, 0 : jj + 1, :, lo : lo + HEAD_DIM].reshape(keys, HEAD_DIM)
                s_own = lax.dot_general(q, k_own, contract, preferred_element_type=F32) * HEAD_DIM**-0.5
                s_par = lax.dot_general(q, k_par, contract, preferred_element_type=F32) * HEAD_DIM**-0.5
                s_own = jnp.where(own_ok, s_own, -1e30)
                s_par = jnp.where(par_ok, s_par, -1e30)
                top = jnp.maximum(jnp.max(s_own, axis=1, keepdims=True), jnp.max(s_par, axis=1, keepdims=True))
                e_own, e_par = jnp.exp(s_own - top), jnp.exp(s_par - top)
                inv = 1.0 / (jnp.sum(e_own, axis=1, keepdims=True) + jnp.sum(e_par, axis=1, keepdims=True))
                v_own = kvo[s, 0 : jj + 1, :, hc + lo : hc + lo + HEAD_DIM].reshape(keys, HEAD_DIM)
                v_par = kvp[s, 0 : jj + 1, :, hc + lo : hc + lo + HEAD_DIM].reshape(keys, HEAD_DIM)
                out = jnp.dot((e_own * inv).astype(BF16), v_own, preferred_element_type=F32)
                out += jnp.dot((e_par * inv).astype(BF16), v_par, preferred_element_type=F32)
                og[n, :, pl.ds(al(x * hc + lo, 128), HEAD_DIM)] = out.astype(BF16)

        for jj in range(NJ):
            pl.when(j == jj)(functools.partial(one, jj))
        og_copy(0, n).start()
        og_copy(1, n).start()

    def pass_o(n):
        og_wait(0, n)
        og_copy(2, n).start()
        og_wait(1, n)
        og_copy(3, n).start()

    def out_project(n):
        r, j = chunk_of(n)
        og_wait(2, n)
        og_wait(3, n)

        def body(i, carry):
            cols = pl.ds(al(i * 256, 128), 256)
            zb[r, j, :, cols] = jnp.dot(og[n], wob[:, cols], preferred_element_type=F32).astype(BF16)
            return carry

        lax.fori_loop(0, kc // 256, body, 0)

        @pl.when(n >= 12)
        def _():
            reduce.halves(j)

    events = {}
    for m in range(3):
        events[4 * m] = lambda m=m: [d_direct(m, d, 0).start() for d in range(2)]
        events[4 * m + 1] = lambda m=m: [d_opp(m, d).start() for d in range(2)]
        events[4 * m + 2] = lambda m=m: [d_direct(m, d, 1).start() for d in range(2)]
        events[4 * m + 3] = functools.partial(d_turn, m)
        events[(12, 15, 19)[m]] = functools.partial(d_pairs, m)

    def tick(n, carry):
        @pl.when(n < NCH)
        def _():
            @pl.when(n >= 4)
            def _():
                gather.arrive(n)

            project(n)

        @pl.when(jnp.logical_and(n >= 1, n < NCH + 1))
        def _():
            attend(n - 1)

        @pl.when(jnp.logical_and(n >= 2, n < NCH + 2))
        def _():
            pass_o(n - 2)

        @pl.when(jnp.logical_and(n >= 3, n < NCH + 3))
        def _():
            out_project(n - 3)

        @pl.when(jnp.logical_and(n >= 16, n < NCH + 4))
        def _():
            reduce.middle(n - 16)

        @pl.when(n >= 17)
        def _():
            j = n - 17
            attn = reduce.total(j).astype(BF16)
            h_ref[j] = (xc[j].astype(F32) + attn.astype(F32)).astype(BF16)

        for when, event in events.items():

            @pl.when(n == when)
            def _(event=event):
                event()

        return carry

    lax.fori_loop(0, NCH + 5, tick, 0)

    for m in range(3):
        for k in range(4):
            d_pair_wait(m, k)
        d_out(m).wait()
    for j in range(NJ):
        x_pair(j).wait_send()
    gather.drain()
    reduce.drain()
    wo_pair.wait_send()
    for k in range(3):
        w_own_pair(k).wait_send()
        w_pair(k).wait_send()
    for d in range(2):
        for i in range(3):
            w_direct(d, i).wait_send()
            w_opp(d, i).wait_send()
        w_fwd(d).wait_send()
    for m in range(3):
        for k in range(4):
            d_pair(m, k).wait_send()
        for d in range(2):
            for p in range(2):
                d_direct(m, d, p).wait_send()
            d_opp(m, d).wait_send()
            d_fwd(m, d).wait_send()

    def drain_chunk(n, carry):
        r, j = chunk_of(n)
        kv_copy(rem(y + r, NX), j, n).wait_send()
        for kind in range(4):
            og_copy(kind, n).wait_send()
        return carry

    lax.fori_loop(0, NCH, drain_chunk, 0)


def mlp_kernel(
    h_ref, w_hbm, y_ref,
    xg, wt, act, pp, rsa, rsb, rsl, rsr, zb, ya, yb, yfd, yfu, yst,
    sx, rx, sy, ry, sr, rr, syr, ryr, sd, rd, lw,
):
    at = Place()
    x, c, y = at.x, at.c, at.y
    ch, kc, h = h_ref.shape[1], h_ref.shape[2], h_ref.shape[1] // 2
    width = xg.shape[-1]
    kd = kc // 2
    fc, fp = w_hbm.shape[1], wt.shape[1]
    gather = Gather(at, h_ref, xg, kc, ch, sx, rx, sy, ry)
    reduce = Reduce(at, zb, ya, yb, yfd, yfu, syr, ryr)

    def w_in(m):
        return pltpu.make_async_copy(w_hbm.at[m], wt.at[m, pl.ds(0, fc)], lw.at[m])

    for m in range(3):
        w_in(m).start()
    for m in range(3):
        wt[m, fc:, :] = jnp.zeros((fp - fc, width), BF16)
    at.barrier()
    for j in range(2):
        gather.full(j)
    for j in range(NJ):
        gather.keep_own(j)
    gather.pass_on(0)

    def silu_mul(g, u):
        g, u = g.astype(BF16).astype(F32), u.astype(BF16).astype(F32)
        return g / (1.0 + jnp.exp(-g)) * u

    def compute(n):
        r, j = chunk_of(n)
        s = rem(y + r, NX)
        slot = rem(n, STAGES)

        def columns(i, carry):
            rows = pl.ds(al(i * 256, 8), 256)
            g = lax.dot_general(xg[s, j], wt[0, rows, :], (((1,), (1,)), ((), ())), preferred_element_type=F32)
            u = lax.dot_general(xg[s, j], wt[1, rows, :], (((1,), (1,)), ((), ())), preferred_element_type=F32)
            act[:, pl.ds(al(i * 256, 128), 256)] = silu_mul(g, u).astype(BF16)
            return carry

        lax.fori_loop(0, fp // 256, columns, 0)
        per = kc // 256

        def down(i, carry):
            q, k = div(i, per), rem(i, per)
            out = jnp.dot(act[...], wt[2, :, pl.ds(al(i * 256, 128), 256)], preferred_element_type=F32)
            pp[slot, q, :, pl.ds(al(k * 256, 128), 256)] = out.astype(BF16)
            return carry

        lax.fori_loop(0, width // 256, down, 0)

    def rs_copy(kind, n):
        slot = rem(n, STAGES)
        src, dst = (
            lambda: (pp.at[slot, at.xo, pl.ds(0, h)], rsa.at[n]),
            lambda: (pp.at[slot, at.xo, pl.ds(h, ch - h)], rsb.at[n]),
            lambda: (pp.at[slot, at.xr], rsl.at[n]),
            lambda: (pp.at[slot, at.xl], rsr.at[n]),
        )[kind]()
        return remote(src, dst, sr.at[kind, n], rr.at[kind, n], at.left if kind % 2 else at.right)

    def rs_second(n):
        slot = rem(n, STAGES)
        rs_copy(0, n).wait_recv()
        pp[slot, at.xr, 0:h] = (pp[slot, at.xr, 0:h].astype(F32) + rsa[n].astype(F32)).astype(BF16)
        rs_copy(2, n).start()
        rs_copy(1, n).wait_recv()
        pp[slot, at.xl, h:] = (pp[slot, at.xl, h:].astype(F32) + rsb[n].astype(F32)).astype(BF16)
        rs_copy(3, n).start()

    def rs_third(n):
        r, j = chunk_of(n)
        slot = rem(n, STAGES)
        rs_copy(2, n).wait_recv()
        rs_copy(3, n).wait_recv()
        zb[r, j] = (pp[slot, x].astype(F32) + rsl[n].astype(F32) + rsr[n].astype(F32)).astype(BF16)

        @pl.when(n >= 12)
        def _():
            reduce.halves(j)

    def rs_sent(n):
        for kind in range(4):
            rs_copy(kind, n).wait_send()

    def y_rows(j, core):
        return pl.ds(al((2 * j + core) * ch, 8), ch)

    def y_copy(j):
        return remote(yst.at[1 - c, j], y_ref.at[y_rows(j, c)], sd.at[j], rd.at[j], at.partner)

    def y_wait(j):
        dst = y_ref.at[y_rows(j, 1 - c)]
        remote(dst, dst, sd.at[j], rd.at[j], at.partner).wait_recv()

    def tick(n, carry):
        @pl.when(n < 2)
        def _():
            gather.full(n + 2)

        @pl.when(n < 3)
        def _():
            gather.pass_on(n + 1)

        @pl.when(n < 4)
        def _():
            gather.finish(n)

        @pl.when(n == 0)
        def _():
            for m in range(3):
                w_in(m).wait()

        @pl.when(n < NCH)
        def _():
            @pl.when(n >= 4)
            def _():
                gather.arrive(n)

            @pl.when(n >= STAGES)
            def _():
                rs_sent(n - STAGES)

            compute(n)
            rs_copy(0, n).start()
            rs_copy(1, n).start()

        @pl.when(jnp.logical_and(n >= 1, n < NCH + 1))
        def _():
            rs_second(n - 1)

        @pl.when(jnp.logical_and(n >= 2, n < NCH + 2))
        def _():
            rs_third(n - 2)

        @pl.when(jnp.logical_and(n >= 15, n < NCH + 3))
        def _():
            reduce.middle(n - 15)

        @pl.when(n >= 16)
        def _():
            j = n - 16
            mlp = reduce.total(j).astype(BF16)
            out = (h_ref[j].astype(F32) + mlp.astype(F32)).astype(BF16)
            yst[0, j] = out[:, :kd]
            yst[1, j] = out[:, kd:]
            y_copy(j).start()
            y_ref[y_rows(j, c), :] = yst[c, j]

        return carry

    lax.fori_loop(0, NCH + 4, tick, 0)
    for n in range(NCH - STAGES, NCH):
        rs_sent(n)
    gather.drain()
    reduce.drain()
    for j in range(NJ):
        y_copy(j).wait_send()
        y_wait(j)


def vmem(*shape, dtype=BF16):
    return pltpu.VMEM(shape, dtype)


def sems(*shape):
    return pltpu.SemaphoreType.DMA(shape)


def solution(mesh):
    assert mesh.shape["tx"] == 2 * NX and mesh.shape["ty"] == NX
    act_spec = P(("dp", "ty"), None, "tx")
    col_spec = P("tx", "ty")
    row_spec = P("ty", "tx")
    any_spec = pl.BlockSpec(memory_space=pl.ANY)
    vmem_spec = pl.BlockSpec(memory_space=pltpu.VMEM)

    def layer(x_blk, w_q, w_k, w_v, w_o, w_gate, w_up, w_down):
        _, seq, kd = x_blk.shape
        kc, width = 2 * kd, 2 * NX * kd
        ch = seq // (2 * NJ)
        h = ch // 2
        row_heads = w_q.shape[1]
        hc = row_heads // NX
        fc = w_down.shape[0] // NX
        assert hc % HEAD_DIM == 0
        fp = (fc + 255) // 256 * 256
        f_r = (fc // 2 + 15) // 16 * 16

        half = HEAD_DIM // 2
        inv_freq = THETA ** (-2.0 * jnp.arange(half, dtype=F32) / HEAD_DIM)
        angles = jnp.arange(seq, dtype=F32)[:, None] * inv_freq[None, :]
        cos_t, sin_t = jnp.cos(angles), jnp.sin(angles)
        cos_t = jnp.concatenate([cos_t, cos_t], axis=1)
        sin_t = jnp.concatenate([-sin_t, sin_t], axis=1)

        reduce_scratch = [vmem(NX, NJ, ch, kc), vmem(NJ, h, kc), vmem(NJ, ch - h, kc), vmem(NJ, ch, kc), vmem(NJ, ch, kc)]
        h_blk, w_all = pl.pallas_call(
            attention_kernel,
            out_shape=(
                jax.ShapeDtypeStruct((NJ, ch, kc), BF16),
                jax.ShapeDtypeStruct((3, fc, width), BF16),
            ),
            in_specs=[vmem_spec] * 3 + [any_spec] * 7,
            out_specs=(vmem_spec, any_spec),
            scratch_shapes=[
                vmem(NJ, ch, kc), vmem(NX, NJ, ch, width), vmem(width, 3 * hc), vmem(2, kd // 2, 3 * hc), vmem(row_heads, kc),
                vmem(2, ch, 3 * hc), vmem(NX, NJ, ch, 2 * hc), vmem(NX, NJ, ch, 2 * hc), vmem(NCH, ch, row_heads),
                *reduce_scratch,
                vmem(3, fc, kd), vmem(3, f_r, kd), vmem(3, fc - f_r, kd),
                sems(4, NJ), sems(4, NJ), sems(4, NJ), sems(4, NJ), sems(NJ), sems(NJ),
                sems(2, 3), sems(2, 3), sems(2, 3), sems(2, 3), sems(2), sems(2), sems(6), sems(6), sems(4), sems(1), sems(1),
                sems(NCH), sems(NCH), sems(4, NCH), sems(4, NCH), sems(4, NJ), sems(4, NJ),
                sems(2, 3), sems(3, 2, 2), sems(3, 2, 2), sems(3, 2), sems(3, 2), sems(3, 2), sems(3, 2), sems(3, 4), sems(3, 4),
            ],
            compiler_params=pltpu.CompilerParams(collective_id=0, has_side_effects=True, vmem_limit_bytes=VMEM_LIMIT),
            name="attention_part",
        )(x_blk[0], cos_t, sin_t, w_q, w_k, w_v, w_o, w_gate.T, w_up.T, w_down)

        y_blk = pl.pallas_call(
            mlp_kernel,
            out_shape=jax.ShapeDtypeStruct((seq, kd), BF16),
            in_specs=[vmem_spec, any_spec],
            out_specs=vmem_spec,
            scratch_shapes=[
                vmem(NX, NJ, ch, width), vmem(3, fp, width), vmem(ch, fp), vmem(STAGES, NX, ch, kc),
                vmem(NCH, h, kc), vmem(NCH, ch - h, kc), vmem(NCH, ch, kc), vmem(NCH, ch, kc),
                *reduce_scratch, vmem(2, NJ, ch, kd),
                sems(4, NJ), sems(4, NJ), sems(4, NJ), sems(4, NJ), sems(4, NCH), sems(4, NCH), sems(4, NJ), sems(4, NJ),
                sems(NJ), sems(NJ), sems(3),
            ],
            compiler_params=pltpu.CompilerParams(collective_id=1, has_side_effects=True, vmem_limit_bytes=VMEM_LIMIT),
            name="mlp_part",
        )(h_blk, w_all)
        return y_blk[None]

    return jax.shard_map(
        layer,
        mesh=mesh,
        in_specs=(act_spec, col_spec, col_spec, col_spec, row_spec, col_spec, col_spec, row_spec),
        out_specs=act_spec,
        check_vma=False,
    )
```

time: 1550 us -> 465 us (0.30)
  waiting for transfers between devices: 879 us -> 0 us
  Pallas kernels: 0 us -> 459 us
  matrix products: 287 us -> 0 us
  other arithmetic: 256 us -> 3.32 us
  local copies, waits for them, and re-layouts: 76 us -> 2.26 us
  blocking collectives: 27 us -> 0 us
    psum x2 -> x0, waiting for transfers between devices: 698 us -> none  [the longest x1 444 us: layer_fn(): lax.psum((project(normed_mlp, w_gate), project(normed_mlp, w_up)), 'tx')]
    pallas_call x0 -> x2, Pallas kernels: none -> 459 us  [the longest x1 252 us: layer(): pl.pallas_call(attention_kernel, out_shape=(jax.ShapeDtypeStruct((NJ, ch,...]
    dot_general x23 -> x0, matrix products: 287 us -> none  [the longest x7 99.6 us: project(): jnp.einsum('...c,ch->...h', rows_bf, weight, preferred_element_type=jnp.f...]
    sub x8 -> x0, other arithmetic: 163 us -> none  [one_block(): prob_blk = jax.nn.softmax(scores, axis=-1).astype(jnp.bfloat16)]
    all_gather x2 -> x0, waiting for transfers between devices: 92.4 us -> none  [the longest x1 47.9 us: layer_fn(): lax.all_gather(norm_sharded(x_blk, full_width), 'ty', axis=0, tiled=True)]
    reduce_scatter x2 -> x0, waiting for transfers between devices: 88.7 us -> none  [the longest x1 44.4 us: layer_fn(): lax.psum_scatter(project(act_val, w_down), 'ty', scatter_dimension=0, til...]
    dynamic_update_slice x16 -> x0, local copies, waits for them, and re-layouts: 37.4 us -> none  [one_block(): return lax.dynamic_update_slice_in_dim(out_acc, blk_out, q_start, axis=1)]
    another operation x3 -> x0, other arithmetic: 34.3 us -> none
  transfers between devices with their start and end apart: 6 -> 0, of which waited for: 6 -> 0; matrix products, arithmetic and copies ran while one was open for 0% -> 0% of each run, Pallas kernels for 0% -> 0%
where the time goes in v1:
time: 465 us
  Pallas kernels  459 us (99%)
    pallas_call x1, Pallas kernels, layer(): pl.pallas_call(attention_kernel, out_shape=(jax.ShapeDtypeStruct((NJ, ch,...  252 us
    pallas_call x1, Pallas kernels, layer(): pl.pallas_call(mlp_kernel, out_shape=jax.ShapeDtypeStruct((seq, kd), BF16...  207 us

profile of v1, /device:TPU:97, one launch (start us, length us, event | category | flops | bytes accessed | tf_op | source)
XLA Modules:
  0.0 465.1 jit_solution(17890264984855436051)
XLA Ops:
  0.0 2.0 fusion.2
  2.0 1.4 pad_maximum_fusion
  3.3 252.1 %attention_part.1 = (bf16[4,128,1024]{2,1,0:T(8,128)(2,1)}, bf16[3,688,4096]{2,1,0:T(8,128)(2,1)}) custom-call(bf16[1024,512]{1,0:T(8,128)(2,1)} %bitcast.7, f32[1024,128]{1,0:T(8,128)} %get-tuple-element.12.cos_ref, f32[1024,128]{1,0:T(8,128)} %get-tuple-element.13.sin_ref, bf16[512,1024]{1,0:T(8,128)(2,1)} %wq.1, bf16[512,1024]{1,0:T(8,128)(2,1)} %wk.1, ...), custom_call_target="tpu_custom_call" | custom-call | tf_op jit(solution)/shard_map/attention_part/pallas_call | solution.py:802
  255.4 207.4 %mlp_part.1 = bf16[1024,512]{1,0:T(8,128)(2,1)} custom-call(bf16[4,128,1024]{2,1,0:T(8,128)(2,1)} %get-tuple-element.7.h_ref, bf16[3,688,4096]{2,1,0:T(8,128)(2,1)} %get-tuple-element.8.w_hbm), custom_call_target="tpu_custom_call" | custom-call | tf_op jit(solution)/shard_map/mlp_part/pallas_call | solution.py:824
  462.8 2.3 copy.10
  (1 shorter events, 0.0 us)

commit v2 on v1

--- a/solution.py
+++ b/solution.py
@@ -43,6 +43,12 @@
     j = is_a * n + is_b * (div(n + 12, 2) - 8) + is_c * (n - 12)
     r = is_b * (3 - 2 * rem(n, 2)) + 2 * is_c
     return r, j
+
+
+def mlp_chunk_of(n):
+    r, j = chunk_of(n + 1)
+    own = div(n, NCH - 1) + div(17 - n, 15)
+    return (1 - own) * r, (1 - own) * j + div(17 - n, 15) * n + div(n, NCH - 1) * (NJ - 1)
 
 
 class Place:
@@ -66,112 +72,125 @@
 
 
 class Gather:
-    def __init__(self, at, src, xg, kc, ch, sx, rx, sy, ry):
+    def __init__(self, at, src, xg, kc, ch, sx, rx, sy, ry, syh, ryh):
         self.at, self.src, self.xg, self.kc, self.ch, self.h = at, src, xg, kc, ch, ch // 2
-        self.sx, self.rx, self.sy, self.ry = sx, rx, sy, ry
+        self.sx, self.rx, self.sy, self.ry, self.syh, self.ryh = sx, rx, sy, ry, syh, ryh
 
     def cols(self, x):
         return pl.ds(al(x * self.kc, 128), self.kc)
 
+    def unit(self, u):
+        return (0, u * self.h, self.h) if u < 2 else (u - 1, 0, self.ch)
+
     def keep_own(self, j):
         self.xg[self.at.y, j, :, self.cols(self.at.x)] = self.src[j]
 
-    def xcopy(self, kind, j):
-        at, h, ch = self.at, self.h, self.ch
+    def xcopy(self, kind, u):
+        at = self.at
+        j, lo, n = self.unit(u)
         if kind < 2:
-            src, dst = self.src.at[j], self.xg.at[at.y, j, :, self.cols(at.x)]
+            rows = pl.ds(lo, n)
+            src, dst = self.src.at[j, rows], self.xg.at[at.y, j, rows, self.cols(at.x)]
         elif kind == 2:
-            src = dst = self.xg.at[at.y, j, pl.ds(0, h), self.cols(at.xl)]
+            src = dst = self.xg.at[at.y, j, pl.ds(lo, n // 2), self.cols(at.xl)]
         else:
-            src = dst = self.xg.at[at.y, j, pl.ds(h, ch - h), self.cols(at.xr)]
-        return remote(src, dst, self.sx.at[kind, j], self.rx.at[kind, j], at.left if kind % 2 else at.right)
-
-    def xwait(self, kind, j):
-        at, h, ch = self.at, self.h, self.ch
+            src = dst = self.xg.at[at.y, j, pl.ds(lo + n // 2, n // 2), self.cols(at.xr)]
+        return remote(src, dst, self.sx.at[kind, u], self.rx.at[kind, u], at.left if kind % 2 else at.right)
+
+    def xwait(self, kind, u):
+        at = self.at
+        j, lo, n = self.unit(u)
         dst = (
-            lambda: self.xg.at[at.y, j, :, self.cols(at.xl)],
-            lambda: self.xg.at[at.y, j, :, self.cols(at.xr)],
-            lambda: self.xg.at[at.y, j, pl.ds(0, h), self.cols(at.xo)],
-            lambda: self.xg.at[at.y, j, pl.ds(h, ch - h), self.cols(at.xo)],
+            lambda: self.xg.at[at.y, j, pl.ds(lo, n), self.cols(at.xl)],
+            lambda: self.xg.at[at.y, j, pl.ds(lo, n), self.cols(at.xr)],
+            lambda: self.xg.at[at.y, j, pl.ds(lo, n // 2), self.cols(at.xo)],
+            lambda: self.xg.at[at.y, j, pl.ds(lo + n // 2, n // 2), self.cols(at.xo)],
         )[kind]()
-        remote(dst, dst, self.sx.at[kind, j], self.rx.at[kind, j], at.right).wait_recv()
-
-    def ycopy(self, kind, j):
-        at, h, ch = self.at, self.h, self.ch
-        if kind < 2:
-            ref = self.xg.at[at.y, j]
-        elif kind == 2:
-            ref = self.xg.at[at.yd, j, pl.ds(0, h)]
-        else:
-            ref = self.xg.at[at.yu, j, pl.ds(h, ch - h)]
-        return remote(ref, ref, self.sy.at[kind, j], self.ry.at[kind, j], at.down if kind % 2 else at.up)
-
-    def ywait(self, kind, j):
-        at, h, ch = self.at, self.h, self.ch
-        dst = (
-            lambda: self.xg.at[at.yd, j],
-            lambda: self.xg.at[at.yu, j],
-            lambda: self.xg.at[at.yo, j, pl.ds(0, h)],
-            lambda: self.xg.at[at.yo, j, pl.ds(h, ch - h)],
-        )[kind]()
-        remote(dst, dst, self.sy.at[kind, j], self.ry.at[kind, j], at.up).wait_recv()
-
-    def full(self, j):
-        self.xcopy(0, j).start()
-        self.xcopy(1, j).start()
-
-    def pass_on(self, j):
-        self.xwait(0, j)
-        self.xwait(1, j)
-        self.xcopy(2, j).start()
-        self.xcopy(3, j).start()
-
-    def finish(self, j):
-        self.xwait(2, j)
-        self.xwait(3, j)
-        self.xcopy(2, j).wait_send()
-        self.xcopy(3, j).wait_send()
+        remote(dst, dst, self.sx.at[kind, u], self.rx.at[kind, u], at.right).wait_recv()
+
+    def ycopy(self, d, u):
+        j, lo, n = self.unit(u)
+        ref = self.xg.at[self.at.y, j, pl.ds(lo, n)]
+        return remote(ref, ref, self.sy.at[d, u], self.ry.at[d, u], self.at.down if d else self.at.up)
+
+    def ywait(self, d, j):
+        at, h = self.at, self.h
+        s = at.yu if d else at.yd
+
+        @pl.when(j == 0)
+        def _():
+            for u in range(2):
+                dst = self.xg.at[s, 0, pl.ds(u * h, h)]
+                remote(dst, dst, self.sy.at[d, u], self.ry.at[d, u], at.up).wait_recv()
+
+        @pl.when(j > 0)
+        def _():
+            dst = self.xg.at[s, j]
+            remote(dst, dst, self.sy.at[d, j + 1], self.ry.at[d, j + 1], at.up).wait_recv()
+
+    def yhalf(self, d, j):
+        at, h = self.at, self.h
+        ref = self.xg.at[at.yu if d else at.yd, j, pl.ds(d * h, h)]
+        return remote(ref, ref, self.syh.at[d, j], self.ryh.at[d, j], at.down if d else at.up)
+
+    def yhalf_wait(self, d, j):
+        dst = self.xg.at[self.at.yo, j, pl.ds(d * self.h, self.h)]
+        remote(dst, dst, self.syh.at[d, j], self.ryh.at[d, j], self.at.up).wait_recv()
+
+    def full(self, u):
+        self.xcopy(0, u).start()
+        self.xcopy(1, u).start()
+
+    def pass_on(self, u):
+        self.xwait(0, u)
+        self.xcopy(2, u).start()
+        self.xwait(1, u)
+        self.xcopy(3, u).start()
+
+    def finish(self, u):
+        self.xwait(2, u)
+        self.xwait(3, u)
+        self.xcopy(2, u).wait_send()
+        self.xcopy(3, u).wait_send()
         width = self.xg.shape[-1]
+        j, lo, n = self.unit(u)
         rows = 8
 
         def body(i, carry):
-            at_rows = pl.ds(al(i * rows, rows), rows)
+            at_rows = pl.ds(al(lo + i * rows, rows), rows)
             v = self.xg[self.at.y, j, at_rows, :].astype(F32)
             mean = jnp.sum(v, axis=-1, keepdims=True) / width
             var = jnp.sum(v * v, axis=-1, keepdims=True) / width - mean * mean
             self.xg[self.at.y, j, at_rows, :] = ((v - mean) * lax.rsqrt(var + EPS)).astype(BF16)
             return carry
 
-        lax.fori_loop(0, self.ch // rows, body, 0)
-        self.ycopy(0, j).start()
-        self.ycopy(1, j).start()
-
-    def arrive(self, n):
-        _, j = chunk_of(n)
-
-        @pl.when(n < 12)
-        def _():
-            @pl.when(rem(n, 2) == 0)
-            def _():
-                self.ywait(0, j)
-                self.ycopy(2, j).start()
-
-            @pl.when(rem(n, 2) == 1)
-            def _():
-                self.ywait(1, j)
-                self.ycopy(3, j).start()
-
-        @pl.when(n >= 12)
-        def _():
-            self.ywait(2, j)
-            self.ywait(3, j)
+        lax.fori_loop(0, n // rows, body, 0)
+        self.ycopy(0, u).start()
+        self.ycopy(1, u).start()
+
+    def arrive(self, r, j):
+        @pl.when(r == 3)
+        def _():
+            self.ywait(0, j)
+            self.yhalf(0, j).start()
+
+        @pl.when(r == 1)
+        def _():
+            self.ywait(1, j)
+            self.yhalf(1, j).start()
+
+        @pl.when(r == 2)
+        def _():
+            self.yhalf_wait(0, j)
+            self.yhalf_wait(1, j)
 
     def drain(self):
-        for j in range(NJ):
-            self.xcopy(0, j).wait_send()
-            self.xcopy(1, j).wait_send()
-            for kind in range(4):
-                self.ycopy(kind, j).wait_send()
+        for d in range(2):
+            for u in range(NJ + 1):
+                self.xcopy(d, u).wait_send()
+                self.ycopy(d, u).wait_send()
+            for j in range(NJ):
+                self.yhalf(d, j).wait_send()
 
 
 class Reduce:
@@ -221,7 +240,7 @@
     x_ref, cos_ref, sin_ref, wq, wk, wv, wo, wg_t, wu_t, wdn,
     h_ref, w_all,
     xc, xg, wb, wrel, wob, qkv, kvo, kvp, og, zb, ya, yb, yfd, yfu, own, drel_r, drel_l,
-    sx, rx, sy, ry, sd, rd, swd, rwd, swo, rwo, swf, rwf, swp, rwp, lw, so, ro, skv, rkv, sog, rog, syr, ryr,
+    sx, rx, sy, ry, syh, ryh, sd, rd, swd, rwd, swo, rwo, swf, rwf, swp, rwp, lw, so, ro, skv, rkv, sog, rog, syr, ryr,
     lg, sw, rw, swx, rwx, swy, rwy, swz, rwz,
 ):
     at = Place()
@@ -231,7 +250,7 @@
     hc = wb.shape[1] // 3
     fc = w_all.shape[1]
     f_r = drel_r.shape[1]
-    gather = Gather(at, xc, xg, kc, ch, sx, rx, sy, ry)
+    gather = Gather(at, xc, xg, kc, ch, sx, rx, sy, ry, syh, ryh)
     reduce = Reduce(at, zb, ya, yb, yfd, yfu, syr, ryr)
     weights = (wq, wk, wv)
     my_rows = lambda xx: al((2 * xx + c) * kd, 128)
@@ -343,6 +362,19 @@
             d_opp(m, d).wait_recv()
             d_fwd(m, d).start()
 
+    events = {}
+    starts = (-1, 0, 3, 5, 7, 9, 11, 13, 15, 17, 17, 18)
+    for m in range(3):
+        steps = (
+            lambda m=m: [d_direct(m, d, 0).start() for d in range(2)],
+            lambda m=m: [d_opp(m, d).start() for d in range(2)],
+            lambda m=m: [d_direct(m, d, 1).start() for d in range(2)],
+            functools.partial(d_turn, m),
+        )
+        for k, step in enumerate(steps):
+            events.setdefault(starts[4 * m + k], []).append(step)
+        events.setdefault((14, 17, 20)[m], []).append(functools.partial(d_pairs, m))
+
     for i in range(3):
         w_own_local(i).start()
     wo_local.start()
@@ -367,30 +399,44 @@
     for i in range(3):
         w_own_pair(i).start()
     wo_pair.start()
-    for j in range(2):
-        x_pair_wait(j)
-        gather.full(j)
-        gather.keep_own(j)
+
+    def full(u):
+        j = max(u - 1, 0)
+        if u != 1:
+            x_pair_wait(j)
+        gather.full(u)
+
+    full(0)
+    full(1)
+    gather.keep_own(0)
     gather.pass_on(0)
-    for j in range(2, NJ):
-        x_pair_wait(j)
-        gather.full(j)
-        gather.keep_own(j)
-        gather.pass_on(j - 1)
-        gather.finish(j - 2)
+    full(2)
+    gather.pass_on(1)
+    gather.keep_own(1)
+    gather.finish(0)
+    gather.finish(1)
+    full(3)
+    gather.pass_on(2)
+    gather.keep_own(2)
+    gather.finish(2)
+    full(4)
+    gather.pass_on(3)
+    gather.keep_own(3)
     for d in range(2):
         for i in range(3):
             w_opp(d, i).start()
-    gather.pass_on(NJ - 1)
+    gather.finish(3)
+    gather.pass_on(4)
     for d in range(2):
         for i in range(3):
             w_direct(d, i).start()
-    gather.finish(NJ - 2)
-    gather.finish(NJ - 1)
+    gather.finish(4)
     for d in range(2):
         for i in range(3):
             w_opp(d, i).wait_recv()
         w_fwd(d).start()
+    for event in events.pop(-1):
+        event()
     for m in range(3):
         d_in(m).wait()
         d_out(m).start()
@@ -513,54 +559,47 @@
         def _():
             reduce.halves(j)
 
-    events = {}
-    for m in range(3):
-        events[4 * m] = lambda m=m: [d_direct(m, d, 0).start() for d in range(2)]
-        events[4 * m + 1] = lambda m=m: [d_opp(m, d).start() for d in range(2)]
-        events[4 * m + 2] = lambda m=m: [d_direct(m, d, 1).start() for d in range(2)]
-        events[4 * m + 3] = functools.partial(d_turn, m)
-        events[(12, 15, 19)[m]] = functools.partial(d_pairs, m)
-
     def tick(n, carry):
         @pl.when(n < NCH)
         def _():
             @pl.when(n >= 4)
             def _():
-                gather.arrive(n)
+                gather.arrive(*chunk_of(n))
 
             project(n)
 
-        @pl.when(jnp.logical_and(n >= 1, n < NCH + 1))
-        def _():
-            attend(n - 1)
-
         @pl.when(jnp.logical_and(n >= 2, n < NCH + 2))
         def _():
             pass_o(n - 2)
 
-        @pl.when(jnp.logical_and(n >= 3, n < NCH + 3))
-        def _():
-            out_project(n - 3)
-
-        @pl.when(jnp.logical_and(n >= 16, n < NCH + 4))
-        def _():
-            reduce.middle(n - 16)
-
-        @pl.when(n >= 17)
-        def _():
-            j = n - 17
+        @pl.when(jnp.logical_and(n >= 4, n < NCH + 4))
+        def _():
+            out_project(n - 4)
+
+        @pl.when(n < NCH)
+        def _():
+            attend(n)
+
+        @pl.when(jnp.logical_and(n >= 17, n < NCH + 5))
+        def _():
+            reduce.middle(n - 17)
+
+        @pl.when(n >= 18)
+        def _():
+            j = n - 18
             attn = reduce.total(j).astype(BF16)
             h_ref[j] = (xc[j].astype(F32) + attn.astype(F32)).astype(BF16)
 
-        for when, event in events.items():
+        for when, steps in events.items():
 
             @pl.when(n == when)
-            def _(event=event):
-                event()
+            def _(steps=steps):
+                for step in steps:
+                    step()
 
         return carry
 
-    lax.fori_loop(0, NCH + 5, tick, 0)
+    lax.fori_loop(0, NCH + 6, tick, 0)
 
     for m in range(3):
         for k in range(4):
@@ -601,7 +640,7 @@
 def mlp_kernel(
     h_ref, w_hbm, y_ref,
     xg, wt, act, pp, rsa, rsb, rsl, rsr, zb, ya, yb, yfd, yfu, yst,
-    sx, rx, sy, ry, sr, rr, syr, ryr, sd, rd, lw,
+    sx, rx, sy, ry, syh, ryh, sr, rr, syr, ryr, sd, rd, lw,
 ):
     at = Place()
     x, c, y = at.x, at.c, at.y
@@ -609,7 +648,7 @@
     width = xg.shape[-1]
     kd = kc // 2
     fc, fp = w_hbm.shape[1], wt.shape[1]
-    gather = Gather(at, h_ref, xg, kc, ch, sx, rx, sy, ry)
+    gather = Gather(at, h_ref, xg, kc, ch, sx, rx, sy, ry, syh, ryh)
     reduce = Reduce(at, zb, ya, yb, yfd, yfu, syr, ryr)
 
     def w_in(m):
@@ -620,18 +659,24 @@
     for m in range(3):
         wt[m, fc:, :] = jnp.zeros((fp - fc, width), BF16)
     at.barrier()
-    for j in range(2):
-        gather.full(j)
+    gather.full(0)
+    gather.full(1)
     for j in range(NJ):
         gather.keep_own(j)
     gather.pass_on(0)
+    gather.full(2)
+    gather.pass_on(1)
+    gather.finish(0)
+    gather.finish(1)
+    gather.full(3)
+    gather.pass_on(2)
 
     def silu_mul(g, u):
         g, u = g.astype(BF16).astype(F32), u.astype(BF16).astype(F32)
         return g / (1.0 + jnp.exp(-g)) * u
 
     def compute(n):
-        r, j = chunk_of(n)
+        r, j = mlp_chunk_of(n)
         s = rem(y + r, NX)
         slot = rem(n, STAGES)
 
@@ -673,13 +718,13 @@
         rs_copy(3, n).start()
 
     def rs_third(n):
-        r, j = chunk_of(n)
+        r, j = mlp_chunk_of(n)
         slot = rem(n, STAGES)
         rs_copy(2, n).wait_recv()
         rs_copy(3, n).wait_recv()
         zb[r, j] = (pp[slot, x].astype(F32) + rsl[n].astype(F32) + rsr[n].astype(F32)).astype(BF16)
 
-        @pl.when(n >= 12)
+        @pl.when(r == 2)
         def _():
             reduce.halves(j)
 
@@ -698,28 +743,31 @@
         remote(dst, dst, sd.at[j], rd.at[j], at.partner).wait_recv()
 
     def tick(n, carry):
-        @pl.when(n < 2)
-        def _():
-            gather.full(n + 2)
-
-        @pl.when(n < 3)
-        def _():
-            gather.pass_on(n + 1)
-
-        @pl.when(n < 4)
-        def _():
-            gather.finish(n)
-
         @pl.when(n == 0)
         def _():
             for m in range(3):
                 w_in(m).wait()
 
+        @pl.when(n == 1)
+        def _():
+            gather.finish(2)
+            gather.full(4)
+            gather.pass_on(3)
+
+        @pl.when(n == 2)
+        def _():
+            gather.finish(3)
+            gather.pass_on(4)
+
+        @pl.when(n == 3)
+        def _():
+            gather.finish(4)
+
         @pl.when(n < NCH)
         def _():
-            @pl.when(n >= 4)
+            @pl.when(jnp.logical_and(n >= 3, n < NCH - 1))
             def _():
-                gather.arrive(n)
+                gather.arrive(*mlp_chunk_of(n))
 
             @pl.when(n >= STAGES)
             def _():
@@ -737,13 +785,13 @@
         def _():
             rs_third(n - 2)
 
-        @pl.when(jnp.logical_and(n >= 15, n < NCH + 3))
-        def _():
-            reduce.middle(n - 15)
-
-        @pl.when(n >= 16)
-        def _():
-            j = n - 16
+        @pl.when(jnp.logical_and(n >= 14, n < NCH + 2))
+        def _():
+            reduce.middle(n - 14)
+
+        @pl.when(n >= 15)
+        def _():
+            j = n - 15
             mlp = reduce.total(j).astype(BF16)
             out = (h_ref[j].astype(F32) + mlp.astype(F32)).astype(BF16)
             yst[0, j] = out[:, :kd]
@@ -753,7 +801,7 @@
 
         return carry
 
-    lax.fori_loop(0, NCH + 4, tick, 0)
+    lax.fori_loop(0, NCH + 3, tick, 0)
     for n in range(NCH - STAGES, NCH):
         rs_sent(n)
     gather.drain()
@@ -798,6 +846,8 @@
         cos_t = jnp.concatenate([cos_t, cos_t], axis=1)
         sin_t = jnp.concatenate([-sin_t, sin_t], axis=1)
 
+        units = NJ + 1
+        gather_sems = [sems(4, units), sems(4, units), sems(2, units), sems(2, units), sems(2, NJ), sems(2, NJ)]
         reduce_scratch = [vmem(NX, NJ, ch, kc), vmem(NJ, h, kc), vmem(NJ, ch - h, kc), vmem(NJ, ch, kc), vmem(NJ, ch, kc)]
         h_blk, w_all = pl.pallas_call(
             attention_kernel,
@@ -812,7 +862,7 @@
                 vmem(2, ch, 3 * hc), vmem(NX, NJ, ch, 2 * hc), vmem(NX, NJ, ch, 2 * hc), vmem(NCH, ch, row_heads),
                 *reduce_scratch,
                 vmem(3, fc, kd), vmem(3, f_r, kd), vmem(3, fc - f_r, kd),
-                sems(4, NJ), sems(4, NJ), sems(4, NJ), sems(4, NJ), sems(NJ), sems(NJ),
+                *gather_sems, sems(NJ), sems(NJ),
                 sems(2, 3), sems(2, 3), sems(2, 3), sems(2, 3), sems(2), sems(2), sems(6), sems(6), sems(4), sems(1), sems(1),
                 sems(NCH), sems(NCH), sems(4, NCH), sems(4, NCH), sems(4, NJ), sems(4, NJ),
                 sems(2, 3), sems(3, 2, 2), sems(3, 2, 2), sems(3, 2), sems(3, 2), sems(3, 2), sems(3, 2), sems(3, 4), sems(3, 4),
@@ -830,7 +880,7 @@
                 vmem(NX, NJ, ch, width), vmem(3, fp, width), vmem(ch, fp), vmem(STAGES, NX, ch, kc),
                 vmem(NCH, h, kc), vmem(NCH, ch - h, kc), vmem(NCH, ch, kc), vmem(NCH, ch, kc),
                 *reduce_scratch, vmem(2, NJ, ch, kd),
-                sems(4, NJ), sems(4, NJ), sems(4, NJ), sems(4, NJ), sems(4, NCH), sems(4, NCH), sems(4, NJ), sems(4, NJ),
+                *gather_sems, sems(4, NCH), sems(4, NCH), sems(4, NJ), sems(4, NJ),
                 sems(NJ), sems(NJ), sems(3),
             ],
             compiler_params=pltpu.CompilerParams(collective_id=1, has_side_effects=True, vmem_limit_bytes=VMEM_LIMIT),

time: 465 us -> 426 us (0.916)
  Pallas kernels: 459 us -> 421 us
    pallas_call x1, Pallas kernels: 252 us -> 222 us  [layer(): pl.pallas_call(attention_kernel, out_shape=(jax.ShapeDtypeStruct((NJ, ch,...]
    pallas_call x1, Pallas kernels: 207 us -> 198 us  [layer(): pl.pallas_call(mlp_kernel, out_shape=jax.ShapeDtypeStruct((seq, kd), BF16...]
where the time goes in v2:
time: 426 us
  Pallas kernels  421 us (99%)
    pallas_call x1, Pallas kernels, layer(): pl.pallas_call(attention_kernel, out_shape=(jax.ShapeDtypeStruct((NJ, ch,...  222 us
    pallas_call x1, Pallas kernels, layer(): pl.pallas_call(mlp_kernel, out_shape=jax.ShapeDtypeStruct((seq, kd), BF16...  198 us

profile of v2, /device:TPU:97, one launch (start us, length us, event | category | flops | bytes accessed | tf_op | source)
XLA Modules:
  0.0 426.2 jit_solution(14494154158938535435)
XLA Ops:
  0.0 2.0 fusion.2
  2.0 1.4 pad_maximum_fusion
  3.3 222.0 %attention_part.1 = (bf16[4,128,1024]{2,1,0:T(8,128)(2,1)}, bf16[3,688,4096]{2,1,0:T(8,128)(2,1)}) custom-call(bf16[1024,512]{1,0:T(8,128)(2,1)} %bitcast.7, f32[1024,128]{1,0:T(8,128)} %get-tuple-element.12.cos_ref, f32[1024,128]{1,0:T(8,128)} %get-tuple-element.13.sin_ref, bf16[512,1024]{1,0:T(8,128)(2,1)} %wq.1, bf16[512,1024]{1,0:T(8,128)(2,1)} %wk.1, ...), custom_call_target="tpu_custom_call" | custom-call | tf_op jit(solution)/shard_map/attention_part/pallas_call | solution.py:852
  225.4 198.5 %mlp_part.1 = bf16[1024,512]{1,0:T(8,128)(2,1)} custom-call(bf16[4,128,1024]{2,1,0:T(8,128)(2,1)} %get-tuple-element.7.h_ref, bf16[3,688,4096]{2,1,0:T(8,128)(2,1)} %get-tuple-element.8.w_hbm), custom_call_target="tpu_custom_call" | custom-call | tf_op jit(solution)/shard_map/mlp_part/pallas_call | solution.py:874
  423.9 2.3 copy.10
  (1 shorter events, 0.0 us)

commit v3 on v2

--- a/solution.py
+++ b/solution.py
@@ -16,7 +16,6 @@
 NX = 4
 NJ = 4
 NCH = 16
-STAGES = 4
 VMEM_LIMIT = 67_043_328
 
 
@@ -45,10 +44,18 @@
     return r, j
 
 
-def mlp_chunk_of(n):
-    r, j = chunk_of(n + 1)
-    own = div(n, NCH - 1) + div(17 - n, 15)
-    return (1 - own) * r, (1 - own) * j + div(17 - n, 15) * n + div(n, NCH - 1) * (NJ - 1)
+MLP_STEPS = (
+    ("XF", 0, 1), ("XF", 0, 2), ("YR", 0), ("XF", 0, 0), ("XH", 0, 1), ("YRH", 0), ("XF", 0, 3), ("XH", 0, 2), ("XH", 0, 0),
+    ("N", 0, 1), ("XF", 2, 0), ("XH", 0, 3), ("N", 0, 2), ("G", 0, 1), ("N", 0, 0), ("G", 0, 0), ("N", 0, 3), ("G", 0, 2),
+    ("YH", 1), ("XH", 2, 0), ("P", 0, 1), ("P", 0, 0), ("XF", 1, 0), ("P", 0, 2), ("N", 2, 0), ("X", 0, 1), ("XF", 3, 0),
+    ("X", 0, 0), ("XF", 0, 4), ("YH", 2), ("G", 3, 1), ("G", 1, 1), ("XH", 3, 0), ("XH", 1, 0), ("X", 0, 2), ("XH", 0, 4),
+    ("P", 3, 1), ("P", 1, 1), ("N", 3, 0), ("G", 3, 0), ("N", 1, 0), ("G", 1, 0), ("N", 0, 4), ("G", 0, 3), ("G", 2, 0),
+    ("P", 3, 0), ("YH", 3), ("G", 1, 2), ("G", 3, 2), ("G", 2, 1), ("P", 1, 0), ("P", 0, 3), ("X", 1, 1), ("X", 3, 1),
+    ("P", 2, 0), ("X", 3, 0), ("P", 1, 2), ("P", 3, 2), ("P", 2, 1), ("YH", 4), ("G", 1, 3), ("G", 3, 3), ("X", 1, 0),
+    ("X", 2, 0), ("X", 0, 3), ("X", 3, 2), ("G", 2, 2), ("X", 2, 1), ("P", 1, 3), ("X", 1, 2), ("P", 3, 3), ("G", 2, 3),
+    ("M", 0), ("P", 2, 2), ("X", 1, 3), ("M", 1), ("X", 3, 3), ("P", 2, 3), ("T", 0), ("X", 2, 2), ("X", 2, 3), ("T", 1),
+    ("M", 2), ("M", 3), ("T", 2), ("T", 3),
+)
 
 
 class Place:
@@ -193,6 +200,132 @@
                 self.yhalf(d, j).wait_send()
 
 
+class Spread:
+    def __init__(self, at, src, xg, units, sx, rx, sy, ry, syh, ryh):
+        self.at, self.src, self.xg, self.units, self.kc = at, src, xg, units, src.shape[2]
+        self.sx, self.rx, self.sy, self.ry, self.syh, self.ryh = sx, rx, sy, ry, syh, ryh
+        pairs = [(r, u) for u, unit in enumerate(units) for r in ((0, 3, 1, 2) if unit[3] else (0,))]
+        self.index = {pair: i for i, pair in enumerate(pairs)}
+        self.seqs = (at.y, at.yu, at.yo, at.yd)
+
+    def cols(self, x):
+        return pl.ds(al(x * self.kc, 128), self.kc)
+
+    def keep_own(self):
+        for j in range(NJ):
+            self.xg[self.at.y, j, :, self.cols(self.at.x)] = self.src[j]
+
+    def xcopy(self, kind, r, u):
+        at, s = self.at, self.seqs[r]
+        j, lo, n, _ = self.units[u]
+        i = self.index[r, u]
+        if kind < 2:
+            dst = self.xg.at[s, j, pl.ds(lo, n), self.cols(at.x)]
+            src = self.src.at[j, pl.ds(lo, n)] if r == 0 else dst
+        elif kind == 2:
+            src = dst = self.xg.at[s, j, pl.ds(lo, n // 2), self.cols(at.xl)]
+        else:
+            src = dst = self.xg.at[s, j, pl.ds(lo + n // 2, n // 2), self.cols(at.xr)]
+        return remote(src, dst, self.sx.at[kind, i], self.rx.at[kind, i], at.left if kind % 2 else at.right)
+
+    def xwait(self, kind, r, u):
+        at = self.at
+        j, lo, n, _ = self.units[u]
+        i = self.index[r, u]
+        x = (at.xl, at.xr, at.xo, at.xo)[kind]
+        rows = (pl.ds(lo, n), pl.ds(lo, n), pl.ds(lo, n // 2), pl.ds(lo + n // 2, n // 2))[kind]
+        dst = self.xg.at[self.seqs[r], j, rows, self.cols(x)]
+        remote(dst, dst, self.sx.at[kind, i], self.rx.at[kind, i], at.right).wait_recv()
+
+    def yref(self, s, u, lo, n):
+        j, _, _, first = self.units[u]
+        rows = pl.ds(lo, n)
+        return self.xg.at[s, j, rows, self.cols(self.at.x)] if first else self.xg.at[s, j, rows]
+
+    def ycopy(self, d, u):
+        j, lo, n, first = self.units[u]
+        dst = self.yref(self.at.y, u, lo, n)
+        src = self.src.at[j, pl.ds(lo, n)] if first else dst
+        return remote(src, dst, self.sy.at[d, u], self.ry.at[d, u], self.at.down if d else self.at.up)
+
+    def ywait(self, d, u):
+        _, lo, n, _ = self.units[u]
+        dst = self.yref(self.at.yu if d else self.at.yd, u, lo, n)
+        remote(dst, dst, self.sy.at[d, u], self.ry.at[d, u], self.at.up).wait_recv()
+
+    def yhalf(self, d, u):
+        _, lo, n, _ = self.units[u]
+        ref = self.yref(self.at.yu if d else self.at.yd, u, lo + d * (n // 2), n // 2)
+        return remote(ref, ref, self.syh.at[d, u], self.ryh.at[d, u], self.at.down if d else self.at.up)
+
+    def yhalf_wait(self, d, u):
+        _, lo, n, _ = self.units[u]
+        dst = self.yref(self.at.yo, u, lo + d * (n // 2), n // 2)
+        remote(dst, dst, self.syh.at[d, u], self.ryh.at[d, u], self.at.up).wait_recv()
+
+    def YR(self, u):
+        for d in range(2):
+            self.ycopy(d, u).start()
+
+    def YH(self, u):
+        for d in range(2):
+            self.ywait(d, u)
+            self.yhalf(d, u).start()
+
+    YRH = YH
+
+    def XF(self, r, u):
+        if r == 2:
+            for d in range(2):
+                self.yhalf_wait(d, u)
+        for kind in range(2):
+            self.xcopy(kind, r, u).start()
+
+    def XH(self, r, u):
+        for kind in range(2):
+            self.xwait(kind, r, u)
+            self.xcopy(kind + 2, r, u).start()
+
+    def N(self, r, u):
+        j, lo, n, first = self.units[u]
+        for kind in (2, 3):
+            self.xwait(kind, r, u)
+            self.xcopy(kind, r, u).wait_send()
+        if r:
+            for kind in range(2):
+                self.xcopy(kind, r, u).wait_send()
+        if r % 2:
+            self.yhalf(0 if r == 3 else 1, u).wait_send()
+        width, rows, s = self.xg.shape[-1], 8, self.seqs[r]
+
+        def body(i, carry):
+            at_rows = pl.ds(al(lo + i * rows, rows), rows)
+            v = self.xg[s, j, at_rows, :].astype(F32)
+            mean = jnp.sum(v, axis=-1, keepdims=True) / width
+            var = jnp.sum(v * v, axis=-1, keepdims=True) / width - mean * mean
+            self.xg[s, j, at_rows, :] = ((v - mean) * lax.rsqrt(var + EPS)).astype(BF16)
+            return carry
+
+        lax.fori_loop(0, n // rows, body, 0)
+        if not first:
+            self.YR(u)
+
+    def chunk_wait(self, r, j):
+        if r == 2:
+            for u, unit in enumerate(self.units):
+                if unit[0] == j and not unit[3]:
+                    for d in range(2):
+                        self.yhalf_wait(d, u)
+
+    def drain(self):
+        for u, unit in enumerate(self.units):
+            for d in range(2):
+                self.xcopy(d, 0, u).wait_send()
+                self.ycopy(d, u).wait_send()
+                if not unit[3]:
+                    self.yhalf(d, u).wait_send()
+
+
 class Reduce:
     def __init__(self, at, zb, ya, yb, yfd, yfu, ss, rs):
         self.at, self.zb, self.ya, self.yb, self.yfd, self.yfu, self.ss, self.rs = at, zb, ya, yb, yfd, yfu, ss, rs
@@ -237,7 +370,7 @@
 
 
 def attention_kernel(
-    x_ref, cos_ref, sin_ref, wq, wk, wv, wo, wg_t, wu_t, wdn,
+    x_ref, cos_ref, sin_ref, wq, wk, wv, wo, wg_t, wu_t,
     h_ref, w_all,
     xc, xg, wb, wrel, wob, qkv, kvo, kvp, og, zb, ya, yb, yfd, yfu, own, drel_r, drel_l,
     sx, rx, sy, ry, syh, ryh, sd, rd, swd, rwd, swo, rwo, swf, rwf, swp, rwp, lw, so, ro, skv, rkv, sog, rog, syr, ryr,
@@ -301,7 +434,7 @@
     wo_local = pltpu.make_async_copy(wo, wob.at[:, half_cols(c)], lw.at[3])
     wo_pair = remote(wo, wob.at[:, half_cols(c)], so.at[0], ro.at[0], at.partner)
 
-    mlp_weights = (wg_t, wu_t, wdn)
+    mlp_weights = (wg_t, wu_t)
     parts = ((0, f_r), (f_r, fc - f_r))
 
     def d_cols(xx, core):
@@ -363,8 +496,8 @@
             d_fwd(m, d).start()
 
     events = {}
-    starts = (-1, 0, 3, 5, 7, 9, 11, 13, 15, 17, 17, 18)
-    for m in range(3):
+    starts = (-1, 0, 3, 6, 8, 10, 13, 15)
+    for m in range(2):
         steps = (
             lambda m=m: [d_direct(m, d, 0).start() for d in range(2)],
             lambda m=m: [d_opp(m, d).start() for d in range(2)],
@@ -373,12 +506,12 @@
         )
         for k, step in enumerate(steps):
             events.setdefault(starts[4 * m + k], []).append(step)
-        events.setdefault((14, 17, 20)[m], []).append(functools.partial(d_pairs, m))
+        events.setdefault((15, 19)[m], []).append(functools.partial(d_pairs, m))
 
     for i in range(3):
         w_own_local(i).start()
     wo_local.start()
-    for m in range(3):
+    for m in range(2):
         d_in(m).start()
 
     def x_rows(j, core):
@@ -437,7 +570,7 @@
         w_fwd(d).start()
     for event in events.pop(-1):
         event()
-    for m in range(3):
+    for m in range(2):
         d_in(m).wait()
         d_out(m).start()
         d_pair(m, 3).start()
@@ -601,7 +734,7 @@
 
     lax.fori_loop(0, NCH + 6, tick, 0)
 
-    for m in range(3):
+    for m in range(2):
         for k in range(4):
             d_pair_wait(m, k)
         d_out(m).wait()
@@ -618,7 +751,7 @@
             w_direct(d, i).wait_send()
             w_opp(d, i).wait_send()
         w_fwd(d).wait_send()
-    for m in range(3):
+    for m in range(2):
         for k in range(4):
             d_pair(m, k).wait_send()
         for d in range(2):
@@ -638,99 +771,101 @@
 
 
 def mlp_kernel(
-    h_ref, w_hbm, y_ref,
-    xg, wt, act, pp, rsa, rsb, rsl, rsr, zb, ya, yb, yfd, yfu, yst,
-    sx, rx, sy, ry, syh, ryh, sr, rr, syr, ryr, sd, rd, lw,
+    units, h_ref, w_hbm, wdn, y_ref,
+    xg, wt, wd, ag, zb, ya, yb, yfd, yfu, yst,
+    sx, rx, sy, ry, syh, ryh, sa, ra, syr, ryr, sd, rd, lw, lwd, swd, rwd,
 ):
     at = Place()
     x, c, y = at.x, at.c, at.y
     ch, kc, h = h_ref.shape[1], h_ref.shape[2], h_ref.shape[1] // 2
     width = xg.shape[-1]
     kd = kc // 2
-    fc, fp = w_hbm.shape[1], wt.shape[1]
-    gather = Gather(at, h_ref, xg, kc, ch, sx, rx, sy, ry, syh, ryh)
+    fc, tiles = w_hbm.shape[1], wt.shape[0]
+    fp = tiles * 128
+    gather = Spread(at, h_ref, xg, units, sx, rx, sy, ry, syh, ryh)
     reduce = Reduce(at, zb, ya, yb, yfd, yfu, syr, ryr)
 
-    def w_in(m):
-        return pltpu.make_async_copy(w_hbm.at[m], wt.at[m, pl.ds(0, fc)], lw.at[m])
-
-    for m in range(3):
-        w_in(m).start()
-    for m in range(3):
-        wt[m, fc:, :] = jnp.zeros((fp - fc, width), BF16)
+    def w_in(m, i):
+        n = min(128, fc - i * 128)
+        return pltpu.make_async_copy(w_hbm.at[m, pl.ds(i * 128, n)], wt.at[i, pl.ds(m * 128, n)], lw.at[m, i])
+
+    def d_own(q):
+        return pltpu.make_async_copy(wdn.at[pl.ds(q * fc, fc)], wd.at[pl.ds(q * fp, fc), pl.ds(al(c * kd, 128), kd)], lwd.at[q])
+
+    def d_pair(q):
+        dst = wd.at[pl.ds(q * fp, fc), pl.ds(al(c * kd, 128), kd)]
+        return remote(wdn.at[pl.ds(q * fc, fc)], dst, swd.at[q], rwd.at[q], at.partner)
+
+    def d_pair_wait(q):
+        dst = wd.at[pl.ds(q * fp, fc), pl.ds(al((1 - c) * kd, 128), kd)]
+        remote(dst, dst, swd.at[q], rwd.at[q], at.partner).wait_recv()
+
+    for m in range(2):
+        for i in range(tiles):
+            w_in(m, i).start()
+    for q in range(NX):
+        d_own(q).start()
+    rest = fc - (tiles - 1) * 128
+    if rest < 128:
+        for m in range(2):
+            wt[tiles - 1, m * 128 + rest : (m + 1) * 128, :] = jnp.zeros((128 - rest, width), BF16)
+        for q in range(NX):
+            wd[q * fp + fc : (q + 1) * fp, :] = jnp.zeros((fp - fc, kc), BF16)
     at.barrier()
-    gather.full(0)
-    gather.full(1)
-    for j in range(NJ):
-        gather.keep_own(j)
-    gather.pass_on(0)
-    gather.full(2)
-    gather.pass_on(1)
-    gather.finish(0)
-    gather.finish(1)
-    gather.full(3)
-    gather.pass_on(2)
-
-    def silu_mul(g, u):
-        g, u = g.astype(BF16).astype(F32), u.astype(BF16).astype(F32)
-        return g / (1.0 + jnp.exp(-g)) * u
-
-    def compute(n):
-        r, j = mlp_chunk_of(n)
-        s = rem(y + r, NX)
-        slot = rem(n, STAGES)
+    for q in range(NX):
+        d_pair(q).start()
+
+    def a_cols(xx):
+        return pl.ds(al(xx * fp, 128), fp)
+
+    def a_copy(kind, n):
+        if kind < 2:
+            ref = ag.at[n, :, a_cols(x)]
+        elif kind == 2:
+            ref = ag.at[n, pl.ds(0, h), a_cols(at.xl)]
+        else:
+            ref = ag.at[n, pl.ds(h, ch - h), a_cols(at.xr)]
+        return remote(ref, ref, sa.at[kind, n], ra.at[kind, n], at.left if kind % 2 else at.right)
+
+    def a_wait(kind, n):
+        xx = (at.xl, at.xr, at.xo, at.xo)[kind]
+        rows = (pl.ds(0, ch), pl.ds(0, ch), pl.ds(0, h), pl.ds(h, ch - h))[kind]
+        dst = ag.at[n, rows, a_cols(xx)]
+        remote(dst, dst, sa.at[kind, n], ra.at[kind, n], at.right).wait_recv()
+
+    def G(r, j):
+        gather.chunk_wait(r, j)
+        s, n = gather.seqs[r], r * NJ + j
 
         def columns(i, carry):
-            rows = pl.ds(al(i * 256, 8), 256)
-            g = lax.dot_general(xg[s, j], wt[0, rows, :], (((1,), (1,)), ((), ())), preferred_element_type=F32)
-            u = lax.dot_general(xg[s, j], wt[1, rows, :], (((1,), (1,)), ((), ())), preferred_element_type=F32)
-            act[:, pl.ds(al(i * 256, 128), 256)] = silu_mul(g, u).astype(BF16)
+            out = lax.dot_general(xg[s, j], wt[i], (((1,), (1,)), ((), ())), preferred_element_type=F32)
+            g, u = out[:, :128].astype(BF16).astype(F32), out[:, 128:].astype(BF16).astype(F32)
+            ag[n, :, pl.ds(al(x * fp + i * 128, 128), 128)] = (g / (1.0 + jnp.exp(-g)) * u).astype(BF16)
             return carry
 
-        lax.fori_loop(0, fp // 256, columns, 0)
-        per = kc // 256
-
-        def down(i, carry):
-            q, k = div(i, per), rem(i, per)
-            out = jnp.dot(act[...], wt[2, :, pl.ds(al(i * 256, 128), 256)], preferred_element_type=F32)
-            pp[slot, q, :, pl.ds(al(k * 256, 128), 256)] = out.astype(BF16)
+        lax.fori_loop(0, tiles, columns, 0)
+        for kind in range(2):
+            a_copy(kind, n).start()
+
+    def P(r, j):
+        n = r * NJ + j
+        for kind in range(2):
+            a_wait(kind, n)
+            a_copy(kind + 2, n).start()
+
+    def X(r, j):
+        n = r * NJ + j
+        for kind in (2, 3):
+            a_wait(kind, n)
+
+        def columns(i, carry):
+            cols = pl.ds(al(i * 256, 128), 256)
+            zb[r, j, :, cols] = jnp.dot(ag[n], wd[:, cols], preferred_element_type=F32).astype(BF16)
             return carry
 
-        lax.fori_loop(0, width // 256, down, 0)
-
-    def rs_copy(kind, n):
-        slot = rem(n, STAGES)
-        src, dst = (
-            lambda: (pp.at[slot, at.xo, pl.ds(0, h)], rsa.at[n]),
-            lambda: (pp.at[slot, at.xo, pl.ds(h, ch - h)], rsb.at[n]),
-            lambda: (pp.at[slot, at.xr], rsl.at[n]),
-            lambda: (pp.at[slot, at.xl], rsr.at[n]),
-        )[kind]()
-        return remote(src, dst, sr.at[kind, n], rr.at[kind, n], at.left if kind % 2 else at.right)
-
-    def rs_second(n):
-        slot = rem(n, STAGES)
-        rs_copy(0, n).wait_recv()
-        pp[slot, at.xr, 0:h] = (pp[slot, at.xr, 0:h].astype(F32) + rsa[n].astype(F32)).astype(BF16)
-        rs_copy(2, n).start()
-        rs_copy(1, n).wait_recv()
-        pp[slot, at.xl, h:] = (pp[slot, at.xl, h:].astype(F32) + rsb[n].astype(F32)).astype(BF16)
-        rs_copy(3, n).start()
-
-    def rs_third(n):
-        r, j = mlp_chunk_of(n)
-        slot = rem(n, STAGES)
-        rs_copy(2, n).wait_recv()
-        rs_copy(3, n).wait_recv()
-        zb[r, j] = (pp[slot, x].astype(F32) + rsl[n].astype(F32) + rsr[n].astype(F32)).astype(BF16)
-
-        @pl.when(r == 2)
-        def _():
+        lax.fori_loop(0, kc // 256, columns, 0)
+        if r == 2:
             reduce.halves(j)
-
-    def rs_sent(n):
-        for kind in range(4):
-            rs_copy(kind, n).wait_send()
 
     def y_rows(j, core):
         return pl.ds(al((2 * j + core) * ch, 8), ch)
@@ -742,70 +877,34 @@
         dst = y_ref.at[y_rows(j, 1 - c)]
         remote(dst, dst, sd.at[j], rd.at[j], at.partner).wait_recv()
 
-    def tick(n, carry):
-        @pl.when(n == 0)
-        def _():
-            for m in range(3):
-                w_in(m).wait()
-
-        @pl.when(n == 1)
-        def _():
-            gather.finish(2)
-            gather.full(4)
-            gather.pass_on(3)
-
-        @pl.when(n == 2)
-        def _():
-            gather.finish(3)
-            gather.pass_on(4)
-
-        @pl.when(n == 3)
-        def _():
-            gather.finish(4)
-
-        @pl.when(n < NCH)
-        def _():
-            @pl.when(jnp.logical_and(n >= 3, n < NCH - 1))
-            def _():
-                gather.arrive(*mlp_chunk_of(n))
-
-            @pl.when(n >= STAGES)
-            def _():
-                rs_sent(n - STAGES)
-
-            compute(n)
-            rs_copy(0, n).start()
-            rs_copy(1, n).start()
-
-        @pl.when(jnp.logical_and(n >= 1, n < NCH + 1))
-        def _():
-            rs_second(n - 1)
-
-        @pl.when(jnp.logical_and(n >= 2, n < NCH + 2))
-        def _():
-            rs_third(n - 2)
-
-        @pl.when(jnp.logical_and(n >= 14, n < NCH + 2))
-        def _():
-            reduce.middle(n - 14)
-
-        @pl.when(n >= 15)
-        def _():
-            j = n - 15
-            mlp = reduce.total(j).astype(BF16)
-            out = (h_ref[j].astype(F32) + mlp.astype(F32)).astype(BF16)
-            yst[0, j] = out[:, :kd]
-            yst[1, j] = out[:, kd:]
-            y_copy(j).start()
-            y_ref[y_rows(j, c), :] = yst[c, j]
-
-        return carry
-
-    lax.fori_loop(0, NCH + 3, tick, 0)
-    for n in range(NCH - STAGES, NCH):
-        rs_sent(n)
+    def T(j):
+        mlp = reduce.total(j).astype(BF16)
+        out = (h_ref[j].astype(F32) + mlp.astype(F32)).astype(BF16)
+        yst[0, j] = out[:, :kd]
+        yst[1, j] = out[:, kd:]
+        y_copy(j).start()
+        y_ref[y_rows(j, c), :] = yst[c, j]
+
+    ops = {"G": G, "P": P, "X": X, "M": reduce.middle, "T": T}
+    for name in ("YR", "YRH", "YH", "XF", "XH", "N"):
+        ops[name] = getattr(gather, name)
+    waits = {
+        "N": gather.keep_own,
+        "G": lambda: [w_in(m, i).wait() for m in range(2) for i in range(tiles)],
+        "X": lambda: [(d_own(q).wait(), d_pair_wait(q)) for q in range(NX)],
+    }
+    for step in MLP_STEPS:
+        if step[0] in waits:
+            waits.pop(step[0])()
+        ops[step[0]](*step[1:])
+
     gather.drain()
     reduce.drain()
+    for q in range(NX):
+        d_pair(q).wait_send()
+    for n in range(NCH):
+        for kind in range(4):
+            a_copy(kind, n).wait_send()
     for j in range(NJ):
         y_copy(j).wait_send()
         y_wait(j)
@@ -836,7 +935,7 @@
         hc = row_heads // NX
         fc = w_down.shape[0] // NX
         assert hc % HEAD_DIM == 0
-        fp = (fc + 255) // 256 * 256
+        tiles = (fc + 127) // 128
         f_r = (fc // 2 + 15) // 16 * 16
 
         half = HEAD_DIM // 2
@@ -853,39 +952,41 @@
             attention_kernel,
             out_shape=(
                 jax.ShapeDtypeStruct((NJ, ch, kc), BF16),
-                jax.ShapeDtypeStruct((3, fc, width), BF16),
+                jax.ShapeDtypeStruct((2, fc, width), BF16),
             ),
-            in_specs=[vmem_spec] * 3 + [any_spec] * 7,
+            in_specs=[vmem_spec] * 3 + [any_spec] * 6,
             out_specs=(vmem_spec, any_spec),
             scratch_shapes=[
                 vmem(NJ, ch, kc), vmem(NX, NJ, ch, width), vmem(width, 3 * hc), vmem(2, kd // 2, 3 * hc), vmem(row_heads, kc),
                 vmem(2, ch, 3 * hc), vmem(NX, NJ, ch, 2 * hc), vmem(NX, NJ, ch, 2 * hc), vmem(NCH, ch, row_heads),
                 *reduce_scratch,
-                vmem(3, fc, kd), vmem(3, f_r, kd), vmem(3, fc - f_r, kd),
+                vmem(2, fc, kd), vmem(2, f_r, kd), vmem(2, fc - f_r, kd),
                 *gather_sems, sems(NJ), sems(NJ),
                 sems(2, 3), sems(2, 3), sems(2, 3), sems(2, 3), sems(2), sems(2), sems(6), sems(6), sems(4), sems(1), sems(1),
                 sems(NCH), sems(NCH), sems(4, NCH), sems(4, NCH), sems(4, NJ), sems(4, NJ),
-                sems(2, 3), sems(3, 2, 2), sems(3, 2, 2), sems(3, 2), sems(3, 2), sems(3, 2), sems(3, 2), sems(3, 4), sems(3, 4),
+                sems(2, 2), sems(2, 2, 2), sems(2, 2, 2), sems(2, 2), sems(2, 2), sems(2, 2), sems(2, 2), sems(2, 4), sems(2, 4),
             ],
             compiler_params=pltpu.CompilerParams(collective_id=0, has_side_effects=True, vmem_limit_bytes=VMEM_LIMIT),
             name="attention_part",
-        )(x_blk[0], cos_t, sin_t, w_q, w_k, w_v, w_o, w_gate.T, w_up.T, w_down)
-
+        )(x_blk[0], cos_t, sin_t, w_q, w_k, w_v, w_o, w_gate.T, w_up.T)
+
+        units = ((0, 0, h, 1), (0, h, h, 0)) + tuple((j, 0, ch, 0) for j in range(1, NJ))
+        n_u, n_x = len(units), len(units) + 3
         y_blk = pl.pallas_call(
-            mlp_kernel,
+            functools.partial(mlp_kernel, units),
             out_shape=jax.ShapeDtypeStruct((seq, kd), BF16),
-            in_specs=[vmem_spec, any_spec],
+            in_specs=[vmem_spec, any_spec, any_spec],
             out_specs=vmem_spec,
             scratch_shapes=[
-                vmem(NX, NJ, ch, width), vmem(3, fp, width), vmem(ch, fp), vmem(STAGES, NX, ch, kc),
-                vmem(NCH, h, kc), vmem(NCH, ch - h, kc), vmem(NCH, ch, kc), vmem(NCH, ch, kc),
+                vmem(NX, NJ, ch, width), vmem(tiles, 256, width), vmem(NX * tiles * 128, kc), vmem(NCH, ch, NX * tiles * 128),
                 *reduce_scratch, vmem(2, NJ, ch, kd),
-                *gather_sems, sems(4, NCH), sems(4, NCH), sems(4, NJ), sems(4, NJ),
-                sems(NJ), sems(NJ), sems(3),
+                sems(4, n_x), sems(4, n_x), sems(2, n_u), sems(2, n_u), sems(2, n_u), sems(2, n_u),
+                sems(4, NCH), sems(4, NCH), sems(4, NJ), sems(4, NJ), sems(NJ), sems(NJ),
+                sems(2, tiles), sems(NX), sems(NX), sems(NX),
             ],
             compiler_params=pltpu.CompilerParams(collective_id=1, has_side_effects=True, vmem_limit_bytes=VMEM_LIMIT),
             name="mlp_part",
-        )(h_blk, w_all)
+        )(h_blk, w_all, w_down)
         return y_blk[None]
 
     return jax.shard_map(

time: 426 us -> 412 us (0.967)
  Pallas kernels: 421 us -> 407 us
    pallas_call x1, Pallas kernels: 222 us -> 212 us  [layer(): pl.pallas_call(attention_kernel, out_shape=(jax.ShapeDtypeStruct((NJ, ch,...]
where the time goes in v3:
time: 412 us
  Pallas kernels  407 us (99%)
    pallas_call x1, Pallas kernels, layer(): pl.pallas_call(attention_kernel, out_shape=(jax.ShapeDtypeStruct((NJ, ch,...  212 us
    pallas_call x1, Pallas kernels, layer(): pl.pallas_call(functools.partial(mlp_kernel, units), out_shape=jax.ShapeD...  194 us

profile of v3, /device:TPU:97, one launch (start us, length us, event | category | flops | bytes accessed | tf_op | source)
XLA Modules:
  0.0 412.2 jit_solution(14874357732057632121)
XLA Ops:
  0.0 2.0 fusion.2
  2.0 1.3 pad_maximum_fusion
  3.3 212.3 %attention_part.1 = (bf16[4,128,1024]{2,1,0:T(8,128)(2,1)}, bf16[2,688,4096]{2,1,0:T(8,128)(2,1)}) custom-call(bf16[1024,512]{1,0:T(8,128)(2,1)} %bitcast.7, f32[1024,128]{1,0:T(8,128)} %get-tuple-element.12.cos_ref, f32[1024,128]{1,0:T(8,128)} %get-tuple-element.13.sin_ref, bf16[512,1024]{1,0:T(8,128)(2,1)} %wq.1, bf16[512,1024]{1,0:T(8,128)(2,1)} %wk.1, ...), custom_call_target="tpu_custom_call" | custom-call | tf_op jit(solution)/shard_map/attention_part/pallas_call | solution.py:951
  215.6 194.4 %mlp_part.1 = bf16[1024,512]{1,0:T(8,128)(2,1)} custom-call(bf16[4,128,1024]{2,1,0:T(8,128)(2,1)} %get-tuple-element.7.h_ref, bf16[2,688,4096]{2,1,0:T(8,128)(2,1)} %get-tuple-element.8.w_hbm, bf16[2752,512]{1,0:T(8,128)(2,1)} %wdn.1), custom_call_target="tpu_custom_call" | custom-call | tf_op jit(solution)/shard_map/mlp_part/pallas_call | solution.py:975
  410.0 2.3 copy.10
  (1 shorter events, 0.0 us)

commit v4 on v3

v4 whole, which is shorter than its diff:
```python
import functools

import jax
import jax.numpy as jnp
from jax import lax
from jax.experimental import pallas as pl
from jax.experimental.pallas import tpu as pltpu
from jax.sharding import PartitionSpec as P

HEAD_DIM = 128
EPS = 1e-5
THETA = 10000.0
MESH = pl.DeviceIdType.MESH
F32 = jnp.float32
BF16 = jnp.bfloat16
NX = 4
NJ = 4
NCH = 16
VMEM_LIMIT = 67_043_328


def rem(a, b):
    return lax.rem(a, jnp.int32(b))


def div(a, b):
    return lax.div(a, jnp.int32(b))


def al(v, m):
    return pl.multiple_of(v, m)


def remote(src, dst, ssem, rsem, dev):
    return pltpu.make_async_remote_copy(src_ref=src, dst_ref=dst, send_sem=ssem, recv_sem=rsem, device_id=dev, device_id_type=MESH)


ATTENTION_STEPS = (
    ("S", "b", 1, 1), ("WA", 0), ("XP", 2), ("XE", 3), ("S", "b", 0, 0), ("XP", 3), ("S", "b", 1, 0), ("XP", 0), ("WOP",),
    ("XE", 0), ("WP", 0), ("O", "b", 1), ("ST", 3), ("WA", 1), ("ST", 0), ("S", "b", 0, 1), ("XP", 1), ("O", "b", 0),
    ("XE", 1), ("N", 3), ("WP", 1), ("XE", 2), ("XE", 4), ("ST", 1), ("YH", 3), ("G", 3, 2), ("G", 1, 2), ("O", "a", 1),
    ("N", 1), ("F", "a", 0), ("F", "a", 1), ("ST", 2), ("G", 2, 2), ("S", "a", 1, 0), ("N", 0), ("G", 0, 0), ("YH", 1),
    ("N", 2), ("S", "a", 0, 1), ("S", "a", 1, 1), ("ST", 4), ("YH", 0), ("R", 3, 2), ("O", "a", 0), ("F", "b", 1), ("N", 4),
    ("G", 1, 0), ("G", 3, 0), ("G", 0, 3), ("R", 2, 2), ("G", 2, 0), ("R", 1, 2), ("R", 3, 0), ("YH", 2), ("G", 1, 1),
    ("R", 1, 0), ("R", 0, 3), ("A", 3, 0), ("YH", 4), ("R", 2, 0), ("G", 1, 3), ("G", 3, 1), ("G", 2, 1), ("A", 1, 0),
    ("A", 2, 0), ("R", 3, 1), ("G", 3, 3), ("A", 3, 1), ("G", 2, 3), ("P", 2, 0), ("R", 1, 1), ("P", 1, 0), ("R", 2, 1),
    ("R", 1, 3), ("A", 2, 1), ("R", 0, 0), ("A", 2, 2), ("A", 3, 2), ("P", 3, 0), ("R", 3, 3), ("A", 1, 1), ("R", 2, 3),
    ("P", 2, 1), ("DP", 1), ("X", 2, 0), ("A", 2, 3), ("X", 1, 0), ("A", 1, 2), ("A", 3, 3), ("P", 3, 2), ("A", 1, 3),
    ("P", 3, 1), ("X", 2, 1), ("X", 3, 0), ("P", 1, 2), ("P", 2, 2), ("P", 2, 3), ("P", 1, 1), ("M", 0), ("P", 3, 3),
    ("G", 0, 1), ("G", 0, 2), ("X", 2, 2), ("X", 3, 1), ("P", 1, 3), ("X", 1, 1), ("M", 1), ("S", "a", 0, 0), ("A", 0, 0),
    ("X", 3, 2), ("X", 1, 2), ("F", "b", 0), ("R", 0, 2), ("X", 2, 3), ("M", 2), ("X", 1, 3), ("R", 0, 1), ("A", 0, 1),
    ("A", 0, 2), ("X", 3, 3), ("M", 3), ("A", 0, 3), ("DP", 0), ("P", 0, 0), ("P", 0, 1), ("P", 0, 2), ("P", 0, 3),
    ("X", 0, 0), ("T", 0), ("X", 0, 1), ("X", 0, 2), ("T", 1), ("T", 2), ("X", 0, 3), ("T", 3),
)
MLP_STEPS = (
    ("XF", 0, 1), ("YR", 0), ("XH", 0, 1), ("XF", 0, 2), ("YRH", 0), ("N", 0, 1), ("XH", 0, 2), ("XF", 3, 0), ("XF", 0, 0),
    ("XF", 0, 3), ("N", 0, 2), ("XF", 1, 0), ("XH", 0, 3), ("XH", 0, 0), ("XH", 3, 0), ("XF", 0, 4), ("N", 0, 3), ("G", 0, 1),
    ("XF", 2, 0), ("N", 3, 0), ("XH", 1, 0), ("YH", 2), ("YH", 1), ("N", 0, 0), ("G", 1, 1), ("G", 3, 0), ("XH", 0, 4),
    ("G", 0, 0), ("N", 1, 0), ("G", 3, 1), ("P", 3, 0), ("N", 0, 4), ("G", 1, 0), ("G", 0, 2), ("YH", 3), ("XH", 2, 0),
    ("G", 3, 2), ("G", 2, 1), ("G", 1, 2), ("P", 1, 1), ("G", 0, 3), ("P", 1, 2), ("X", 1, 1), ("P", 3, 1), ("P", 0, 2),
    ("P", 2, 1), ("N", 2, 0), ("G", 2, 0), ("YH", 4), ("X", 3, 0), ("G", 3, 3), ("X", 2, 1), ("G", 1, 3), ("X", 3, 1),
    ("P", 2, 0), ("P", 3, 2), ("P", 1, 0), ("G", 2, 2), ("X", 2, 0), ("G", 2, 3), ("M", 1), ("X", 1, 0), ("P", 2, 2),
    ("X", 3, 2), ("M", 0), ("P", 2, 3), ("P", 1, 3), ("P", 3, 3), ("P", 0, 1), ("X", 0, 2), ("X", 2, 2), ("X", 1, 2),
    ("X", 2, 3), ("M", 2), ("X", 3, 3), ("X", 0, 1), ("P", 0, 3), ("X", 1, 3), ("P", 0, 0), ("M", 3), ("T", 2), ("X", 0, 3),
    ("T", 1), ("X", 0, 0), ("T", 0), ("T", 3),
)


class Place:
    def __init__(self):
        tx, ty = lax.axis_index("tx"), lax.axis_index("ty")
        self.x, self.c, self.y = div(tx, 2), rem(tx, 2), ty
        x, c, y = self.x, self.c, self.y
        self.xr, self.xl, self.xo = rem(x + 1, NX), rem(x + 3, NX), rem(x + 2, NX)
        self.yu, self.yd, self.yo = rem(y + 1, NX), rem(y + 3, NX), rem(y + 2, NX)
        self.right = {"tx": self.xr * 2 + c, "ty": y}
        self.left = {"tx": self.xl * 2 + c, "ty": y}
        self.up = {"tx": tx, "ty": self.yu}
        self.down = {"tx": tx, "ty": self.yd}
        self.partner = {"tx": x * 2 + 1 - c, "ty": y}
        self.xa, self.xb = x + 1 - 2 * rem(x, 2), rem(x + 3 + 2 * rem(x, 2), NX)
        self.pa, self.pb = {"tx": self.xa * 2 + c, "ty": y}, {"tx": self.xb * 2 + c, "ty": y}

    def barrier(self):
        sem = pltpu.get_barrier_semaphore()
        for dev in (self.right, self.left, self.up, self.down, self.partner):
            pl.semaphore_signal(sem, inc=1, device_id=dev, device_id_type=MESH)
        pl.semaphore_wait(sem, 5)


class Spread:
    def __init__(self, at, src, xg, units, sx, rx, sy, ry, syh, ryh):
        self.at, self.src, self.xg, self.units, self.kc = at, src, xg, units, src.shape[2]
        self.sx, self.rx, self.sy, self.ry, self.syh, self.ryh = sx, rx, sy, ry, syh, ryh
        pairs = [(r, u) for u, unit in enumerate(units) for r in ((0, 3, 1, 2) if unit[3] else (0,))]
        self.index = {pair: i for i, pair in enumerate(pairs)}
        self.seqs = (at.y, at.yu, at.yo, at.yd)

    def cols(self, x):
        return pl.ds(al(x * self.kc, 128), self.kc)

    def keep_own(self):
        for j in range(NJ):
            self.xg[self.at.y, j, :, self.cols(self.at.x)] = self.src[j]

    def xcopy(self, kind, r, u):
        at, s = self.at, self.seqs[r]
        j, lo, n, _ = self.units[u]
        i = self.index[r, u]
        if kind < 2:
            dst = self.xg.at[s, j, pl.ds(lo, n), self.cols(at.x)]
            src = self.src.at[j, pl.ds(lo, n)] if r == 0 else dst
        elif kind == 2:
            src = dst = self.xg.at[s, j, pl.ds(lo, n // 2), self.cols(at.xl)]
        else:
            src = dst = self.xg.at[s, j, pl.ds(lo + n // 2, n // 2), self.cols(at.xr)]
        return remote(src, dst, self.sx.at[kind, i], self.rx.at[kind, i], at.left if kind % 2 else at.right)

    def xwait(self, kind, r, u):
        at = self.at
        j, lo, n, _ = self.units[u]
        i = self.index[r, u]
        x = (at.xl, at.xr, at.xo, at.xo)[kind]
        rows = (pl.ds(lo, n), pl.ds(lo, n), pl.ds(lo, n // 2), pl.ds(lo + n // 2, n // 2))[kind]
        dst = self.xg.at[self.seqs[r], j, rows, self.cols(x)]
        remote(dst, dst, self.sx.at[kind, i], self.rx.at[kind, i], at.right).wait_recv()

    def yref(self, s, u, lo, n):
        j, _, _, first = self.units[u]
        rows = pl.ds(lo, n)
        return self.xg.at[s, j, rows, self.cols(self.at.x)] if first else self.xg.at[s, j, rows]

    def ycopy(self, d, u):
        j, lo, n, first = self.units[u]
        dst = self.yref(self.at.y, u, lo, n)
        src = self.src.at[j, pl.ds(lo, n)] if first else dst
        return remote(src, dst, self.sy.at[d, u], self.ry.at[d, u], self.at.down if d else self.at.up)

    def ywait(self, d, u):
        _, lo, n, _ = self.units[u]
        dst = self.yref(self.at.yu if d else self.at.yd, u, lo, n)
        remote(dst, dst, self.sy.at[d, u], self.ry.at[d, u], self.at.up).wait_recv()

    def yhalf(self, d, u):
        _, lo, n, _ = self.units[u]
        ref = self.yref(self.at.yu if d else self.at.yd, u, lo + d * (n // 2), n // 2)
        return remote(ref, ref, self.syh.at[d, u], self.ryh.at[d, u], self.at.down if d else self.at.up)

    def yhalf_wait(self, d, u):
        _, lo, n, _ = self.units[u]
        dst = self.yref(self.at.yo, u, lo + d * (n // 2), n // 2)
        remote(dst, dst, self.syh.at[d, u], self.ryh.at[d, u], self.at.up).wait_recv()

    def YR(self, u):
        for d in range(2):
            self.ycopy(d, u).start()

    def YH(self, u):
        for d in range(2):
            self.ywait(d, u)
            self.yhalf(d, u).start()

    YRH = YH

    def XF(self, r, u):
        if r == 2:
            for d in range(2):
                self.yhalf_wait(d, u)
        for kind in range(2):
            self.xcopy(kind, r, u).start()

    def XH(self, r, u):
        for kind in range(2):
            self.xwait(kind, r, u)
            self.xcopy(kind + 2, r, u).start()

    def N(self, r, u):
        j, lo, n, first = self.units[u]
        for kind in (2, 3):
            self.xwait(kind, r, u)
            self.xcopy(kind, r, u).wait_send()
        if r:
            for kind in range(2):
                self.xcopy(kind, r, u).wait_send()
        if r % 2:
            self.yhalf(0 if r == 3 else 1, u).wait_send()
        width, rows, s = self.xg.shape[-1], 8, self.seqs[r]

        def body(i, carry):
            at_rows = pl.ds(al(lo + i * rows, rows), rows)
            v = self.xg[s, j, at_rows, :].astype(F32)
            mean = jnp.sum(v, axis=-1, keepdims=True) / width
            var = jnp.sum(v * v, axis=-1, keepdims=True) / width - mean * mean
            self.xg[s, j, at_rows, :] = ((v - mean) * lax.rsqrt(var + EPS)).astype(BF16)
            return carry

        lax.fori_loop(0, n // rows, body, 0)
        if not first:
            self.YR(u)

    def chunk_wait(self, r, j):
        if r == 2:
            for u, unit in enumerate(self.units):
                if unit[0] == j and not unit[3]:
                    for d in range(2):
                        self.yhalf_wait(d, u)

    def drain(self):
        for u, unit in enumerate(self.units):
            for d in range(2):
                self.xcopy(d, 0, u).wait_send()
                self.ycopy(d, u).wait_send()
                if not unit[3]:
                    self.yhalf(d, u).wait_send()


class Reduce:
    def __init__(self, at, zb, ya, yb, yfd, yfu, ss, rs):
        self.at, self.zb, self.ya, self.yb, self.yfd, self.yfu, self.ss, self.rs = at, zb, ya, yb, yfd, yfu, ss, rs
        self.ch = zb.shape[2]
        self.h = self.ch // 2

    def copy(self, kind, j):
        at, h, ch = self.at, self.h, self.ch
        src, dst = (
            lambda: (self.zb.at[2, j, pl.ds(0, h)], self.ya.at[j]),
            lambda: (self.zb.at[2, j, pl.ds(h, ch - h)], self.yb.at[j]),
            lambda: (self.zb.at[1, j], self.yfd.at[j]),
            lambda: (self.zb.at[3, j], self.yfu.at[j]),
        )[kind]()
        return remote(src, dst, self.ss.at[kind, j], self.rs.at[kind, j], at.down if kind % 2 else at.up)

    def wait(self, kind, j):
        self.copy(kind, j).wait_recv()

    def halves(self, j):
        self.copy(0, j).start()
        self.copy(1, j).start()

    def middle(self, j):
        h = self.h
        self.wait(0, j)
        self.zb[1, j, 0:h] = (self.zb[1, j, 0:h].astype(F32) + self.ya[j].astype(F32)).astype(BF16)
        self.copy(2, j).start()
        self.wait(1, j)
        self.zb[3, j, h:] = (self.zb[3, j, h:].astype(F32) + self.yb[j].astype(F32)).astype(BF16)
        self.copy(3, j).start()

    def total(self, j):
        self.wait(2, j)
        self.wait(3, j)
        return self.zb[0, j].astype(F32) + self.yfd[j].astype(F32) + self.yfu[j].astype(F32)

    def drain(self):
        for j in range(NJ):
            for kind in range(4):
                self.copy(kind, j).wait_send()


def attention_kernel(
    units, x_ref, cos_ref, sin_ref, wq, wk, wv, wo, wg_t, wu_t,
    h_ref, w_all,
    xc, xg, st_own, st_in, wb, wob, part, precv, qb, kvo, kvp, og, zb, ya, yb, yfd, yfu, own, drel_a, drel_b,
    sxe, rxe, sst, rst, sy, ry, syh, ryh, sd, rd, swa, rwa, swo, rwo, swp, rwp, lw, so, ro, spr, rpr, skv, rkv, sog, rog, syr, ryr,
    lg, sds, rds, sdo, rdo, sdf, rdf, sdp, rdp,
):
    at = Place()
    x, c, y = at.x, at.c, at.y
    ch, kc, h = xc.shape[1], xc.shape[2], xc.shape[1] // 2
    kd = wq.shape[0]
    hc = qb.shape[2]
    fc, f_a = w_all.shape[1], drel_a.shape[1]
    width = 2 * xg.shape[3]
    kh = div(x, 2)
    ng = rem(div(x + 1, 2), 2)
    gather = Spread(at, xc, xg, units, None, None, sy, ry, syh, ryh)
    reduce = Reduce(at, zb, ya, yb, yfd, yfu, syr, ryr)
    weights = (wq, wk, wv)

    def half_cols(core):
        return pl.ds(al(core * kd, 128), kd)

    def x_rows(j, core):
        return pl.ds(al((2 * j + core) * ch, 8), ch)

    def x_pair(j):
        return remote(x_ref.at[x_rows(j, 1 - c)], xc.at[j, :, half_cols(c)], sd.at[j], rd.at[j], at.partner)

    def pair_cols(xx):
        return pl.ds(al(rem(xx, 2) * kc, 128), kc)

    def xe_copy(u, xx):
        j, lo, n, _ = units[u]
        rows = pl.ds(lo, n)
        return remote(xc.at[j, rows], xg.at[y, j, rows, pair_cols(xx)], sxe.at[u], rxe.at[u], at.pa)

    def st_copy(u):
        j, lo, n, _ = units[u]
        rows = pl.ds(lo, n)
        return remote(st_own.at[j, rows], st_in.at[j, rows], sst.at[u], rst.at[u], at.pb)

    def XP(j):
        x_pair(j).start()

    def XE(u):
        j, lo, n, _ = units[u]
        if lo == 0:
            dst = xc.at[j, :, half_cols(1 - c)]
            remote(dst, dst, sd.at[j], rd.at[j], at.partner).wait_recv()
        xe_copy(u, x).start()
        xg[y, j, lo : lo + n, pair_cols(x)] = xc[j, lo : lo + n]

    def ST(u):
        j, lo, n, _ = units[u]
        xe_copy(u, at.xa).wait_recv()
        lane = lax.broadcasted_iota(jnp.int32, (8, 128), 1)

        def body(i, carry):
            rows = pl.ds(al(lo + i * 8, 8), 8)
            v = xg[y, j, rows, :].astype(F32)
            total, square = jnp.sum(v, axis=-1, keepdims=True), jnp.sum(v * v, axis=-1, keepdims=True)
            st_own[j, rows, :] = jnp.where(lane < 64, total, square)
            return carry

        lax.fori_loop(0, n // 8, body, 0)
        st_copy(u).start()

    def N(u):
        j, lo, n, _ = units[u]
        st_copy(u).wait_recv()

        def body(i, carry):
            rows = pl.ds(al(lo + i * 8, 8), 8)
            moments = (st_own[j, rows, :] + st_in[j, rows, :]) / width
            mean = moments[:, 0:1]
            var = moments[:, 64:65] - mean * mean
            v = xg[y, j, rows, :].astype(F32)
            xg[y, j, rows, :] = ((v - mean) * lax.rsqrt(var + EPS)).astype(BF16)
            return carry

        lax.fori_loop(0, n // 8, body, 0)
        gather.YR(u)

    def w_rows(xx, core):
        return pl.ds(al(rem(xx, 2) * kc + core * kd, 128), kd)

    def w_part(group, half, i):
        return weights[i].at[:, pl.ds(al((2 * group + half) * hc, 128), hc)]

    def w_cols(half, i):
        return pl.ds(half * 3 * hc + i * hc, hc)

    def wa_copy(half, i, xx):
        return remote(w_part(1 - ng, half, i), wb.at[w_rows(xx, c), w_cols(half, i)], swa.at[half, i], rwa.at[half, i], at.pa)

    def wo_copy(half, i, core):
        return remote(w_part(ng, half, i), wb.at[w_rows(x, core), w_cols(half, i)], swo.at[half, i], rwo.at[half, i], at.partner)

    def w_local(half, i):
        return pltpu.make_async_copy(w_part(ng, half, i), wb.at[w_rows(x, c), w_cols(half, i)], lw.at[half, i])

    def wp_copy(half, core):
        ref = wb.at[w_rows(at.xa, core), pl.ds(half * 3 * hc, 3 * hc)]
        return remote(ref, ref, swp.at[half], rwp.at[half], at.partner)

    o_local = pltpu.make_async_copy(wo, wob.at[:, half_cols(c)], lw.at[2, 0])
    o_pair = remote(wo, wob.at[:, half_cols(c)], so.at[0], ro.at[0], at.partner)
    pieces = [(half, i) for half in range(2) for i in range(3)]

    def WOP():
        for half, i in pieces:
            wo_copy(half, i, c).start()
        o_pair.start()

    def WA(half):
        for i in range(3):
            wa_copy(half, i, x).start()

    def WP(half):
        for i in range(3):
            wa_copy(half, i, at.xa).wait_recv()
        wp_copy(half, c).start()

    def w_ready():
        for half, i in pieces:
            w_local(half, i).wait()
            wo_copy(half, i, 1 - c).wait_recv()
        for half in range(2):
            wp_copy(half, 1 - c).wait_recv()
        for m in range(2):
            d_in(m).wait()
            d_out(m).start()
            d_pair(m, 3, c).start()

    def o_ready():
        o_local.wait()
        dst = wob.at[:, half_cols(1 - c)]
        remote(dst, dst, so.at[0], ro.at[0], at.partner).wait_recv()

    mlp_weights = (wg_t, wu_t)
    parts = ((0, f_a), (f_a, fc - f_a))

    def d_src(m, xx, p):
        return mlp_weights[m].at[pl.ds(al(xx * fc + parts[p][0], 8), parts[p][1])]

    def d_dst(m, xx, p):
        return w_all.at[m, pl.ds(*parts[p]), pl.ds(al((2 * xx + c) * kd, 128), kd)]

    def s_copy(d, m, p, xx):
        to, dev = ((at.xa, at.pa), (at.xb, at.pb))[d]
        return remote(d_src(m, to, p), d_dst(m, xx, p), sds.at[d, m, p], rds.at[d, m, p], dev)

    def o_copy(d, m):
        return remote(d_src(m, at.xo, d), (drel_a, drel_b)[d].at[m], sdo.at[d, m], rdo.at[d, m], (at.pa, at.pb)[d])

    def f_copy(d, m, xx):
        return remote((drel_a, drel_b)[d].at[m], d_dst(m, xx, d), sdf.at[d, m], rdf.at[d, m], (at.pb, at.pa)[d])

    def d_in(m):
        return pltpu.make_async_copy(mlp_weights[m].at[pl.ds(al(x * fc, 8), fc)], own.at[m], lg.at[0, m])

    def d_all(m, xx, core):
        return w_all.at[m, :, pl.ds(al((2 * xx + core) * kd, 128), kd)]

    def d_out(m):
        return pltpu.make_async_copy(own.at[m], d_all(m, x, c), lg.at[1, m])

    def d_pair(m, k, core):
        dst = d_all(m, (at.xa, at.xb, at.xo, x)[k], core)
        return remote(own.at[m] if k == 3 else dst, dst, sdp.at[m, k], rdp.at[m, k], at.partner)

    def S(link, m, p):
        s_copy("ab".index(link), m, p, x).start()

    def O(link, m):
        o_copy("ab".index(link), m).start()

    def F(link, m):
        d = "ba".index(link)
        o_copy(d, m).wait_recv()
        f_copy(d, m, (at.xa, at.xb)[d]).start()

    def DP(m):
        for d in range(2):
            for p in range(2):
                s_copy(d, m, p, (at.xa, at.xb)[d]).wait_recv()
            f_copy(d, m, at.xo).wait_recv()
        for k in range(3):
            d_pair(m, k, c).start()

    def pr_copy(n):
        src = part.at[n, :, pl.ds(al((1 - kh) * 3 * hc, 128), 3 * hc)]
        return remote(src, precv.at[n], spr.at[n], rpr.at[n], at.pb)

    def G(r, j):
        gather.chunk_wait(r, j)
        s, n = gather.seqs[r], r * NJ + j

        def columns(i, carry):
            cols = pl.ds(al(i * 256, 128), 256)
            part[n, :, cols] = jnp.dot(xg[s, j], wb[:, cols], preferred_element_type=F32).astype(BF16)
            return carry

        lax.fori_loop(0, wb.shape[1] // 256, columns, 0)
        pr_copy(n).start()

    def kv_copy(r, j):
        s, n = gather.seqs[r], r * NJ + j
        return remote(kvo.at[s, j], kvp.at[s, j], skv.at[n], rkv.at[n], at.partner)

    def R(r, j):
        s, n = gather.seqs[r], r * NJ + j
        pr_copy(n).wait_recv()
        rows = pl.ds(al((2 * j + c) * ch, 8), ch)
        cos_t, sin_t = cos_ref[rows, :], sin_ref[rows, :]

        def total(col, size):
            mine = part[n, :, pl.ds(al(kh * 3 * hc + col, 128), size)]
            return (mine.astype(F32) + precv[n, :, col : col + size].astype(F32)).astype(BF16)

        def turned(col):
            v = total(col, HEAD_DIM).astype(F32)
            return (v * cos_t + pltpu.roll(v, HEAD_DIM // 2, axis=1) * sin_t).astype(BF16)

        for col in range(0, hc, HEAD_DIM):
            qb[n, :, col : col + HEAD_DIM] = turned(col)
            kvo[s, j, :, col : col + HEAD_DIM] = turned(hc + col)
        kvo[s, j, :, hc:] = total(2 * hc, hc)
        kv_copy(r, j).start()

    def o_cols(xx):
        return pl.ds(al((2 * rem(div(xx + 1, 2), 2) + div(xx, 2)) * hc, 128), hc)

    def og_copy(kind, n):
        if kind < 2:
            ref = og.at[n, :, o_cols(x)]
        elif kind == 2:
            ref = og.at[n, pl.ds(0, h), o_cols(at.xa)]
        else:
            ref = og.at[n, pl.ds(h, ch - h), o_cols(at.xb)]
        return remote(ref, ref, sog.at[kind, n], rog.at[kind, n], at.pa if kind in (0, 3) else at.pb)

    def og_wait(kind, n):
        xx = (at.xa, at.xb, at.xo, at.xo)[kind]
        rows = (pl.ds(0, ch), pl.ds(0, ch), pl.ds(0, h), pl.ds(h, ch - h))[kind]
        dst = og.at[n, rows, o_cols(xx)]
        remote(dst, dst, sog.at[kind, n], rog.at[kind, n], at.pa).wait_recv()

    def A(r, j):
        s, n = gather.seqs[r], r * NJ + j
        kv_copy(r, j).wait_recv()
        keys = (j + 1) * ch
        iq = lax.broadcasted_iota(jnp.int32, (ch, keys), 0) + j * ch
        ik = lax.broadcasted_iota(jnp.int32, (ch, keys), 1)
        own_ok = iq >= ik
        par_ok = ik < (j + c) * ch
        contract = (((1,), (1,)), ((), ()))
        first = (2 * ng + kh) * hc
        for lo in range(0, hc, HEAD_DIM):
            q = qb[n, :, lo : lo + HEAD_DIM]
            k_own = kvo[s, 0 : j + 1, :, lo : lo + HEAD_DIM].reshape(keys, HEAD_DIM)
            k_par = kvp[s, 0 : j + 1, :, lo : lo + HEAD_DIM].reshape(keys, HEAD_DIM)
            s_own = lax.dot_general(q, k_own, contract, preferred_element_type=F32) * HEAD_DIM**-0.5
            s_par = lax.dot_general(q, k_par, contract, preferred_element_type=F32) * HEAD_DIM**-0.5
            s_own = jnp.where(own_ok, s_own, -1e30)
            s_par = jnp.where(par_ok, s_par, -1e30)
            top = jnp.maximum(jnp.max(s_own, axis=1, keepdims=True), jnp.max(s_par, axis=1, keepdims=True))
            e_own, e_par = jnp.exp(s_own - top), jnp.exp(s_par - top)
            inv = 1.0 / (jnp.sum(e_own, axis=1, keepdims=True) + jnp.sum(e_par, axis=1, keepdims=True))
            v_own = kvo[s, 0 : j + 1, :, hc + lo : hc + lo + HEAD_DIM].reshape(keys, HEAD_DIM)
            v_par = kvp[s, 0 : j + 1, :, hc + lo : hc + lo + HEAD_DIM].reshape(keys, HEAD_DIM)
            out = jnp.dot((e_own * inv).astype(BF16), v_own, preferred_element_type=F32)
            out += jnp.dot((e_par * inv).astype(BF16), v_par, preferred_element_type=F32)
            og[n, :, pl.ds(al(first + lo, 128), HEAD_DIM)] = out.astype(BF16)
        og_copy(0, n).start()
        og_copy(1, n).start()

    def P(r, j):
        n = r * NJ + j
        for kind in range(2):
            og_wait(kind, n)
            og_copy(kind + 2, n).start()

    def X(r, j):
        n = r * NJ + j
        og_wait(2, n)
        og_wait(3, n)

        def columns(i, carry):
            cols = pl.ds(al(i * 256, 128), 256)
            zb[r, j, :, cols] = jnp.dot(og[n], wob[:, cols], preferred_element_type=F32).astype(BF16)
            return carry

        lax.fori_loop(0, kc // 256, columns, 0)
        if r == 2:
            reduce.halves(j)

    def T(j):
        attn = reduce.total(j).astype(BF16)
        h_ref[j] = (xc[j].astype(F32) + attn.astype(F32)).astype(BF16)

    for half, i in pieces:
        w_local(half, i).start()
    o_local.start()
    for m in range(2):
        d_in(m).start()
    for j in range(NJ):
        xc[j, :, half_cols(c)] = x_ref[x_rows(j, c), :]
    at.barrier()
    ops = {
        "XP": XP, "WOP": WOP, "XE": XE, "ST": ST, "N": N, "YH": gather.YH, "WA": WA, "WP": WP, "S": S, "O": O, "F": F, "DP": DP,
        "G": G, "R": R, "A": A, "P": P, "X": X, "M": reduce.middle, "T": T,
    }
    waits = {"G": w_ready, "X": o_ready}
    for step in ATTENTION_STEPS:
        if step[0] in waits:
            waits.pop(step[0])()
        ops[step[0]](*step[1:])

    for m in range(2):
        for k in range(4):
            d_pair(m, k, 1 - c).wait_recv()
            d_pair(m, k, c).wait_send()
        d_out(m).wait()
        for d in range(2):
            for p in range(2):
                s_copy(d, m, p, x).wait_send()
            o_copy(d, m).wait_send()
            f_copy(d, m, x).wait_send()
    for j in range(NJ):
        x_pair(j).wait_send()
    for u in range(len(units)):
        xe_copy(u, x).wait_send()
        st_copy(u).wait_send()
        for d in range(2):
            gather.ycopy(d, u).wait_send()
            gather.yhalf(d, u).wait_send()
    reduce.drain()
    o_pair.wait_send()
    for half, i in pieces:
        wa_copy(half, i, x).wait_send()
        wo_copy(half, i, c).wait_send()
    for half in range(2):
        wp_copy(half, c).wait_send()

    def chunk_sent(n, carry):
        pr_copy(n).wait_send()
        remote(kvo.at[0, 0], kvp.at[0, 0], skv.at[n], rkv.at[n], at.partner).wait_send()
        for kind in range(4):
            og_copy(kind, n).wait_send()
        return carry

    lax.fori_loop(0, NCH, chunk_sent, 0)


def mlp_kernel(
    units, h_ref, w_hbm, wdn, y_ref,
    xg, wt, wd, ag, acc, zb, ya, yb, yfd, yfu, yst,
    sx, rx, sy, ry, syh, ryh, sa, ra, syr, ryr, sd, rd, lw, lwd, swd, rwd,
):
    at = Place()
    x, c, y = at.x, at.c, at.y
    ch, kc, h = h_ref.shape[1], h_ref.shape[2], h_ref.shape[1] // 2
    width = xg.shape[-1]
    kd = kc // 2
    fc, tiles = w_hbm.shape[1], wt.shape[0]
    fp = tiles * 128
    gather = Spread(at, h_ref, xg, units, sx, rx, sy, ry, syh, ryh)
    reduce = Reduce(at, zb, ya, yb, yfd, yfu, syr, ryr)

    def w_in(m, i):
        n = min(128, fc - i * 128)
        return pltpu.make_async_copy(w_hbm.at[m, pl.ds(i * 128, n)], wt.at[i, pl.ds(m * 128, n)], lw.at[m, i])

    def d_own(q):
        return pltpu.make_async_copy(wdn.at[pl.ds(q * fc, fc)], wd.at[pl.ds(q * fp, fc), pl.ds(al(c * kd, 128), kd)], lwd.at[q])

    def d_pair(q):
        dst = wd.at[pl.ds(q * fp, fc), pl.ds(al(c * kd, 128), kd)]
        return remote(wdn.at[pl.ds(q * fc, fc)], dst, swd.at[q], rwd.at[q], at.partner)

    def d_pair_wait(q):
        dst = wd.at[pl.ds(q * fp, fc), pl.ds(al((1 - c) * kd, 128), kd)]
        remote(dst, dst, swd.at[q], rwd.at[q], at.partner).wait_recv()

    for m in range(2):
        for i in range(tiles):
            w_in(m, i).start()
    for q in range(NX):
        d_own(q).start()
    rest = fc - (tiles - 1) * 128
    if rest < 128:
        for m in range(2):
            wt[tiles - 1, m * 128 + rest : (m + 1) * 128, :] = jnp.zeros((128 - rest, width), BF16)
        for q in range(NX):
            wd[q * fp + fc : (q + 1) * fp, :] = jnp.zeros((fp - fc, kc), BF16)
    at.barrier()
    for q in range(NX):
        d_pair(q).start()

    def a_cols(xx):
        return pl.ds(al(xx * fp, 128), fp)

    def a_copy(kind, n):
        if kind < 2:
            ref = ag.at[n, :, a_cols(x)]
        elif kind == 2:
            ref = ag.at[n, pl.ds(0, h), a_cols(at.xl)]
        else:
            ref = ag.at[n, pl.ds(h, ch - h), a_cols(at.xr)]
        return remote(ref, ref, sa.at[kind, n], ra.at[kind, n], at.left if kind % 2 else at.right)

    def a_wait(kind, n):
        xx = (at.xl, at.xr, at.xo, at.xo)[kind]
        rows = (pl.ds(0, ch), pl.ds(0, ch), pl.ds(0, h), pl.ds(h, ch - h))[kind]
        dst = ag.at[n, rows, a_cols(xx)]
        remote(dst, dst, sa.at[kind, n], ra.at[kind, n], at.right).wait_recv()

    def G(r, j):
        gather.chunk_wait(r, j)
        s, n = gather.seqs[r], r * NJ + j

        def columns(i, carry):
            acc[...] = jnp.zeros_like(acc)

            def depth(k, carry):
                cols = pl.ds(al(k * (width // 2), 128), width // 2)
                acc[...] += lax.dot_general(xg[s, j, :, cols], wt[i, :, cols], (((1,), (1,)), ((), ())), preferred_element_type=F32)
                return carry

            lax.fori_loop(0, 2, depth, 0)
            out = acc[...]
            g, u = out[:, :128].astype(BF16).astype(F32), out[:, 128:].astype(BF16).astype(F32)
            ag[n, :, pl.ds(al(x * fp + i * 128, 128), 128)] = (g / (1.0 + jnp.exp(-g)) * u).astype(BF16)
            return carry

        lax.fori_loop(0, tiles, columns, 0)
        for kind in range(2):
            a_copy(kind, n).start()

    def P(r, j):
        n = r * NJ + j
        for kind in range(2):
            a_wait(kind, n)
            a_copy(kind + 2, n).start()

    def X(r, j):
        n = r * NJ + j
        for kind in (2, 3):
            a_wait(kind, n)

        def columns(i, carry):
            cols = pl.ds(al(i * 256, 128), 256)
            acc[...] = jnp.zeros_like(acc)

            def depth(k, carry):
                part = pl.ds(al(k * 2 * fp, 128), 2 * fp)
                acc[...] += jnp.dot(ag[n, :, part], wd[part, cols], preferred_element_type=F32)
                return carry

            lax.fori_loop(0, 2, depth, 0)
            zb[r, j, :, cols] = acc[...].astype(BF16)
            return carry

        lax.fori_loop(0, kc // 256, columns, 0)
        if r == 2:
            reduce.halves(j)

    def y_rows(j, core):
        return pl.ds(al((2 * j + core) * ch, 8), ch)

    def y_copy(j):
        return remote(yst.at[1 - c, j], y_ref.at[y_rows(j, c)], sd.at[j], rd.at[j], at.partner)

    def y_wait(j):
        dst = y_ref.at[y_rows(j, 1 - c)]
        remote(dst, dst, sd.at[j], rd.at[j], at.partner).wait_recv()

    def T(j):
        mlp = reduce.total(j).astype(BF16)
        out = (h_ref[j].astype(F32) + mlp.astype(F32)).astype(BF16)
        yst[0, j] = out[:, :kd]
        yst[1, j] = out[:, kd:]
        y_copy(j).start()
        y_ref[y_rows(j, c), :] = yst[c, j]

    ops = {"G": G, "P": P, "X": X, "M": reduce.middle, "T": T}
    for name in ("YR", "YRH", "YH", "XF", "XH", "N"):
        ops[name] = getattr(gather, name)
    waits = {
        "N": gather.keep_own,
        "G": lambda: [w_in(m, i).wait() for m in range(2) for i in range(tiles)],
        "X": lambda: [(d_own(q).wait(), d_pair_wait(q)) for q in range(NX)],
    }
    for step in MLP_STEPS:
        if step[0] in waits:
            waits.pop(step[0])()
        ops[step[0]](*step[1:])

    gather.drain()
    reduce.drain()
    for q in range(NX):
        d_pair(q).wait_send()

    def chunk_sent(n, carry):
        for kind in range(4):
            a_copy(kind, n).wait_send()
        return carry

    lax.fori_loop(0, NCH, chunk_sent, 0)
    for j in range(NJ):
        y_copy(j).wait_send()
        y_wait(j)


def vmem(*shape, dtype=BF16):
    return pltpu.VMEM(shape, dtype)


def sems(*shape):
    return pltpu.SemaphoreType.DMA(shape)


def solution(mesh):
    assert mesh.shape["tx"] == 2 * NX and mesh.shape["ty"] == NX
    act_spec = P(("dp", "ty"), None, "tx")
    col_spec = P("tx", "ty")
    row_spec = P("ty", "tx")
    any_spec = pl.BlockSpec(memory_space=pl.ANY)
    vmem_spec = pl.BlockSpec(memory_space=pltpu.VMEM)

    def layer(x_blk, w_q, w_k, w_v, w_o, w_gate, w_up, w_down):
        _, seq, kd = x_blk.shape
        kc, width = 2 * kd, 2 * NX * kd
        ch = seq // (2 * NJ)
        h = ch // 2
        row_heads = w_q.shape[1]
        hc = row_heads // NX
        fc = w_down.shape[0] // NX
        assert hc % HEAD_DIM == 0
        tiles = (fc + 127) // 128
        f_a = (fc // 2 + 15) // 16 * 16

        half = HEAD_DIM // 2
        inv_freq = THETA ** (-2.0 * jnp.arange(half, dtype=F32) / HEAD_DIM)
        angles = jnp.arange(seq, dtype=F32)[:, None] * inv_freq[None, :]
        cos_t, sin_t = jnp.cos(angles), jnp.sin(angles)
        cos_t = jnp.concatenate([cos_t, cos_t], axis=1)
        sin_t = jnp.concatenate([-sin_t, sin_t], axis=1)

        reduce_scratch = [vmem(NX, NJ, ch, kc), vmem(NJ, h, kc), vmem(NJ, ch - h, kc), vmem(NJ, ch, kc), vmem(NJ, ch, kc)]
        units = ((0, 0, h, 0), (0, h, h, 0)) + tuple((j, 0, ch, 0) for j in range(1, NJ))
        n_u = len(units)
        h_blk, w_all = pl.pallas_call(
            functools.partial(attention_kernel, units),
            out_shape=(jax.ShapeDtypeStruct((NJ, ch, kc), BF16), jax.ShapeDtypeStruct((2, fc, width), BF16)),
            in_specs=[vmem_spec] * 3 + [any_spec] * 6,
            out_specs=(vmem_spec, any_spec),
            scratch_shapes=[
                vmem(NJ, ch, kc), vmem(NX, NJ, ch, 2 * kc), vmem(NJ, ch, 128, dtype=F32), vmem(NJ, ch, 128, dtype=F32),
                vmem(2 * kc, 6 * hc), vmem(row_heads, kc), vmem(NCH, ch, 6 * hc), vmem(NCH, ch, 3 * hc), vmem(NCH, ch, hc),
                vmem(NX, NJ, ch, 2 * hc), vmem(NX, NJ, ch, 2 * hc), vmem(NCH, ch, row_heads), *reduce_scratch,
                vmem(2, fc, kd), vmem(2, f_a, kd), vmem(2, fc - f_a, kd),
                sems(n_u), sems(n_u), sems(n_u), sems(n_u), sems(2, n_u), sems(2, n_u), sems(2, n_u), sems(2, n_u),
                sems(NJ), sems(NJ), sems(2, 3), sems(2, 3), sems(2, 3), sems(2, 3), sems(2), sems(2), sems(3, 3), sems(1), sems(1),
                sems(NCH), sems(NCH), sems(NCH), sems(NCH), sems(4, NCH), sems(4, NCH), sems(4, NJ), sems(4, NJ),
                sems(2, 2), sems(2, 2, 2), sems(2, 2, 2), sems(2, 2), sems(2, 2), sems(2, 2), sems(2, 2), sems(2, 4), sems(2, 4),
            ],
            compiler_params=pltpu.CompilerParams(collective_id=0, has_side_effects=True, vmem_limit_bytes=VMEM_LIMIT),
            name="attention_part",
        )(x_blk[0], cos_t, sin_t, w_q, w_k, w_v, w_o, w_gate.T, w_up.T)

        units = ((0, 0, h, 1), (0, h, h, 0)) + tuple((j, 0, ch, 0) for j in range(1, NJ))
        n_x = n_u + 3
        y_blk = pl.pallas_call(
            functools.partial(mlp_kernel, units),
            out_shape=jax.ShapeDtypeStruct((seq, kd), BF16),
            in_specs=[vmem_spec, any_spec, any_spec],
            out_specs=vmem_spec,
            scratch_shapes=[
                vmem(NX, NJ, ch, width), vmem(tiles, 256, width), vmem(NX * tiles * 128, kc), vmem(NCH, ch, NX * tiles * 128),
                vmem(ch, 256, dtype=F32),
                *reduce_scratch, vmem(2, NJ, ch, kd),
                sems(4, n_x), sems(4, n_x), sems(2, n_u), sems(2, n_u), sems(2, n_u), sems(2, n_u),
                sems(4, NCH), sems(4, NCH), sems(4, NJ), sems(4, NJ), sems(NJ), sems(NJ),
                sems(2, tiles), sems(NX), sems(NX), sems(NX),
            ],
            compiler_params=pltpu.CompilerParams(collective_id=1, has_side_effects=True, vmem_limit_bytes=VMEM_LIMIT),
            name="mlp_part",
        )(h_blk, w_all, w_down)
        return y_blk[None]

    return jax.shard_map(
        layer,
        mesh=mesh,
        in_specs=(act_spec, col_spec, col_spec, col_spec, row_spec, col_spec, col_spec, row_spec),
        out_specs=act_spec,
        check_vma=False,
    )
```

time: 412 us -> 395 us (0.959)
  Pallas kernels: 407 us -> 389 us
    pallas_call x1, Pallas kernels: 212 us -> 188 us  [layer(): pl.pallas_call(functools.partial(attention_kernel, units), out_shape=(jax...]
    pallas_call x1, Pallas kernels: 194 us -> 201 us  [layer(): pl.pallas_call(functools.partial(mlp_kernel, units), out_shape=jax.ShapeD...]
where the time goes in v4:
time: 395 us; the launch traced here: 394 us
  Pallas kernels  389 us (98%)
    pallas_call x1, Pallas kernels, layer(): pl.pallas_call(functools.partial(mlp_kernel, units), out_shape=jax.ShapeD...  201 us
    pallas_call x1, Pallas kernels, layer(): pl.pallas_call(functools.partial(attention_kernel, units), out_shape=(jax...  188 us

profile of v4, /device:TPU:97, one launch (start us, length us, event | category | flops | bytes accessed | tf_op | source)
XLA Modules:
  0.0 394.5 jit_solution(11132010473268527310)
XLA Ops:
  0.0 2.0 fusion.2
  2.0 1.3 pad_maximum_fusion
  3.3 188.3 %attention_part.1 = (bf16[4,128,1024]{2,1,0:T(8,128)(2,1)}, bf16[2,688,4096]{2,1,0:T(8,128)(2,1)}) custom-call(bf16[1024,512]{1,0:T(8,128)(2,1)} %bitcast.7, f32[1024,128]{1,0:T(8,128)} %get-tuple-element.12.cos_ref, f32[1024,128]{1,0:T(8,128)} %get-tuple-element.13.sin_ref, bf16[512,1024]{1,0:T(8,128)(2,1)} %wq.1, bf16[512,1024]{1,0:T(8,128)(2,1)} %wk.1, ...), custom_call_target="tpu_custom_call" | custom-call | tf_op jit(solution)/shard_map/attention_part/pallas_call | solution.py:814
  191.7 200.6 %mlp_part.1 = bf16[1024,512]{1,0:T(8,128)(2,1)} custom-call(bf16[4,128,1024]{2,1,0:T(8,128)(2,1)} %get-tuple-element.7.h_ref, bf16[2,688,4096]{2,1,0:T(8,128)(2,1)} %get-tuple-element.8.w_hbm, bf16[2752,512]{1,0:T(8,128)(2,1)} %wdn.1), custom_call_target="tpu_custom_call" | custom-call | tf_op jit(solution)/shard_map/mlp_part/pallas_call | solution.py:835
  392.2 2.3 copy.10
  (1 shorter events, 0.0 us)

commit v5 on v4

--- a/solution.py
+++ b/solution.py
@@ -53,16 +53,16 @@
     ("X", 0, 0), ("T", 0), ("X", 0, 1), ("X", 0, 2), ("T", 1), ("T", 2), ("X", 0, 3), ("T", 3),
 )
 MLP_STEPS = (
-    ("XF", 0, 1), ("YR", 0), ("XH", 0, 1), ("XF", 0, 2), ("YRH", 0), ("N", 0, 1), ("XH", 0, 2), ("XF", 3, 0), ("XF", 0, 0),
-    ("XF", 0, 3), ("N", 0, 2), ("XF", 1, 0), ("XH", 0, 3), ("XH", 0, 0), ("XH", 3, 0), ("XF", 0, 4), ("N", 0, 3), ("G", 0, 1),
-    ("XF", 2, 0), ("N", 3, 0), ("XH", 1, 0), ("YH", 2), ("YH", 1), ("N", 0, 0), ("G", 1, 1), ("G", 3, 0), ("XH", 0, 4),
-    ("G", 0, 0), ("N", 1, 0), ("G", 3, 1), ("P", 3, 0), ("N", 0, 4), ("G", 1, 0), ("G", 0, 2), ("YH", 3), ("XH", 2, 0),
-    ("G", 3, 2), ("G", 2, 1), ("G", 1, 2), ("P", 1, 1), ("G", 0, 3), ("P", 1, 2), ("X", 1, 1), ("P", 3, 1), ("P", 0, 2),
-    ("P", 2, 1), ("N", 2, 0), ("G", 2, 0), ("YH", 4), ("X", 3, 0), ("G", 3, 3), ("X", 2, 1), ("G", 1, 3), ("X", 3, 1),
-    ("P", 2, 0), ("P", 3, 2), ("P", 1, 0), ("G", 2, 2), ("X", 2, 0), ("G", 2, 3), ("M", 1), ("X", 1, 0), ("P", 2, 2),
-    ("X", 3, 2), ("M", 0), ("P", 2, 3), ("P", 1, 3), ("P", 3, 3), ("P", 0, 1), ("X", 0, 2), ("X", 2, 2), ("X", 1, 2),
-    ("X", 2, 3), ("M", 2), ("X", 3, 3), ("X", 0, 1), ("P", 0, 3), ("X", 1, 3), ("P", 0, 0), ("M", 3), ("T", 2), ("X", 0, 3),
-    ("T", 1), ("X", 0, 0), ("T", 0), ("T", 3),
+    ("XF", 0, 1), ("XF", 0, 2), ("YR", 0), ("XH", 0, 1), ("YRH", 0), ("XH", 0, 2), ("XF", 3, 0), ("XF", 0, 3), ("N", 0, 1),
+    ("XF", 2, 0), ("N", 0, 2), ("YH", 1), ("XH", 0, 3), ("XF", 0, 4), ("WT", 0), ("XH", 2, 0), ("XF", 1, 0), ("WT", 1),
+    ("XH", 3, 0), ("WT", 2), ("N", 0, 3), ("YH", 2), ("XF", 0, 0), ("N", 3, 0), ("XH", 1, 0), ("WT", 3), ("XH", 0, 4),
+    ("N", 2, 0), ("G", 3, 1), ("N", 1, 0), ("G", 3, 0), ("XH", 0, 0), ("G", 2, 0), ("G", 1, 0), ("YH", 3), ("P", 3, 0),
+    ("G", 1, 1), ("P", 3, 1), ("G", 1, 2), ("G", 2, 1), ("G", 0, 2), ("N", 0, 4), ("P", 1, 2), ("P", 2, 1), ("P", 1, 0),
+    ("G", 2, 2), ("P", 1, 1), ("G", 3, 2), ("G", 0, 1), ("P", 2, 0), ("P", 0, 2), ("X", 3, 1), ("X", 3, 0), ("P", 2, 2),
+    ("X", 1, 0), ("X", 2, 1), ("YH", 4), ("G", 1, 3), ("X", 1, 1), ("G", 3, 3), ("N", 0, 0), ("X", 2, 0), ("P", 3, 2),
+    ("M", 1), ("X", 2, 2), ("G", 2, 3), ("M", 0), ("P", 1, 3), ("P", 3, 3), ("X", 3, 2), ("X", 1, 2), ("M", 2), ("P", 2, 3),
+    ("G", 0, 0), ("G", 0, 3), ("X", 2, 3), ("P", 0, 1), ("P", 0, 0), ("X", 1, 3), ("X", 3, 3), ("M", 3), ("P", 0, 3),
+    ("X", 0, 2), ("T", 2), ("X", 0, 1), ("T", 1), ("X", 0, 0), ("T", 0), ("X", 0, 3), ("T", 3),
 )
 
 
@@ -615,7 +615,7 @@
 
 def mlp_kernel(
     units, h_ref, w_hbm, wdn, y_ref,
-    xg, wt, wd, ag, acc, zb, ya, yb, yfd, yfu, yst,
+    xg, wt, raw, wd, ag, acc, zb, ya, yb, yfd, yfu, yst,
     sx, rx, sy, ry, syh, ryh, sa, ra, syr, ryr, sd, rd, lw, lwd, swd, rwd,
 ):
     at = Place()
@@ -623,14 +623,32 @@
     ch, kc, h = h_ref.shape[1], h_ref.shape[2], h_ref.shape[1] // 2
     width = xg.shape[-1]
     kd = kc // 2
-    fc, tiles = w_hbm.shape[1], wt.shape[0]
+    fc, tiles = w_hbm.shape[1], wt.shape[1] // 256
     fp = tiles * 128
+    blocks, slots = 2 * tiles, raw.shape[0]
     gather = Spread(at, h_ref, xg, units, sx, rx, sy, ry, syh, ryh)
     reduce = Reduce(at, zb, ya, yb, yfd, yfu, syr, ryr)
 
-    def w_in(m, i):
+    def w_in(q):
+        i, m = q // 2, q % 2
         n = min(128, fc - i * 128)
-        return pltpu.make_async_copy(w_hbm.at[m, pl.ds(i * 128, n)], wt.at[i, pl.ds(m * 128, n)], lw.at[m, i])
+        return pltpu.make_async_copy(w_hbm.at[m, pl.ds(i * 128, n)], raw.at[q % slots, pl.ds(0, n)], lw.at[q])
+
+    def WT(g):
+        for q in range(g * blocks // 4, (g + 1) * blocks // 4):
+            i, m, slot = q // 2, q % 2, q % slots
+            w_in(q).wait()
+            if fc < (i + 1) * 128:
+                raw[slot, fc - i * 128 :, :] = jnp.zeros(((i + 1) * 128 - fc, width), BF16)
+
+            def turn(k, carry, slot=slot, q=q):
+                part = pl.ds(al(k * (width // 4), 128), width // 4)
+                wt[part, q * 128 : (q + 1) * 128] = raw[slot, :, part].T
+                return carry
+
+            lax.fori_loop(0, 4, turn, 0)
+            if q + slots < blocks:
+                w_in(q + slots).start()
 
     def d_own(q):
         return pltpu.make_async_copy(wdn.at[pl.ds(q * fc, fc)], wd.at[pl.ds(q * fp, fc), pl.ds(al(c * kd, 128), kd)], lwd.at[q])
@@ -643,16 +661,11 @@
         dst = wd.at[pl.ds(q * fp, fc), pl.ds(al((1 - c) * kd, 128), kd)]
         remote(dst, dst, swd.at[q], rwd.at[q], at.partner).wait_recv()
 
-    for m in range(2):
-        for i in range(tiles):
-            w_in(m, i).start()
+    for q in range(slots):
+        w_in(q).start()
     for q in range(NX):
         d_own(q).start()
-    rest = fc - (tiles - 1) * 128
-    if rest < 128:
-        for m in range(2):
-            wt[tiles - 1, m * 128 + rest : (m + 1) * 128, :] = jnp.zeros((128 - rest, width), BF16)
-        for q in range(NX):
+        if fc < fp:
             wd[q * fp + fc : (q + 1) * fp, :] = jnp.zeros((fp - fc, kc), BF16)
     at.barrier()
     for q in range(NX):
@@ -682,10 +695,11 @@
 
         def columns(i, carry):
             acc[...] = jnp.zeros_like(acc)
+            cols = pl.ds(al(i * 256, 128), 256)
 
             def depth(k, carry):
-                cols = pl.ds(al(k * (width // 2), 128), width // 2)
-                acc[...] += lax.dot_general(xg[s, j, :, cols], wt[i, :, cols], (((1,), (1,)), ((), ())), preferred_element_type=F32)
+                part = pl.ds(al(k * (width // 2), 128), width // 2)
+                acc[...] += jnp.dot(xg[s, j, :, part], wt[part, cols], preferred_element_type=F32)
                 return carry
 
             lax.fori_loop(0, 2, depth, 0)
@@ -744,12 +758,11 @@
         y_copy(j).start()
         y_ref[y_rows(j, c), :] = yst[c, j]
 
-    ops = {"G": G, "P": P, "X": X, "M": reduce.middle, "T": T}
+    ops = {"G": G, "P": P, "X": X, "M": reduce.middle, "T": T, "WT": WT}
     for name in ("YR", "YRH", "YH", "XF", "XH", "N"):
         ops[name] = getattr(gather, name)
     waits = {
         "N": gather.keep_own,
-        "G": lambda: [w_in(m, i).wait() for m in range(2) for i in range(tiles)],
         "X": lambda: [(d_own(q).wait(), d_pair_wait(q)) for q in range(NX)],
     }
     for step in MLP_STEPS:
@@ -830,7 +843,8 @@
             name="attention_part",
         )(x_blk[0], cos_t, sin_t, w_q, w_k, w_v, w_o, w_gate.T, w_up.T)
 
-        units = ((0, 0, h, 1), (0, h, h, 0)) + tuple((j, 0, ch, 0) for j in range(1, NJ))
+        first = ch * 3 // 4
+        units = ((0, 0, first, 1), (0, first, ch - first, 0)) + tuple((j, 0, ch, 0) for j in range(1, NJ))
         n_x = n_u + 3
         y_blk = pl.pallas_call(
             functools.partial(mlp_kernel, units),
@@ -838,12 +852,12 @@
             in_specs=[vmem_spec, any_spec, any_spec],
             out_specs=vmem_spec,
             scratch_shapes=[
-                vmem(NX, NJ, ch, width), vmem(tiles, 256, width), vmem(NX * tiles * 128, kc), vmem(NCH, ch, NX * tiles * 128),
+                vmem(NX, NJ, ch, width), vmem(width, tiles * 256), vmem(3, 128, width), vmem(NX * tiles * 128, kc), vmem(NCH, ch, NX * tiles * 128),
                 vmem(ch, 256, dtype=F32),
                 *reduce_scratch, vmem(2, NJ, ch, kd),
                 sems(4, n_x), sems(4, n_x), sems(2, n_u), sems(2, n_u), sems(2, n_u), sems(2, n_u),
                 sems(4, NCH), sems(4, NCH), sems(4, NJ), sems(4, NJ), sems(NJ), sems(NJ),
-                sems(2, tiles), sems(NX), sems(NX), sems(NX),
+                sems(2 * tiles), sems(NX), sems(NX), sems(NX),
             ],
             compiler_params=pltpu.CompilerParams(collective_id=1, has_side_effects=True, vmem_limit_bytes=VMEM_LIMIT),
             name="mlp_part",

time: 395 us -> 377 us (0.954)
  Pallas kernels: 389 us -> 371 us
    pallas_call x1, Pallas kernels: 201 us -> 182 us  [layer(): pl.pallas_call(functools.partial(mlp_kernel, units), out_shape=jax.ShapeD...]
where the time goes in v5:
time: 377 us; the launch traced here: 376 us
  Pallas kernels  371 us (98%)
    pallas_call x1, Pallas kernels, layer(): pl.pallas_call(functools.partial(attention_kernel, units), out_shape=(jax...  188 us
    pallas_call x1, Pallas kernels, layer(): pl.pallas_call(functools.partial(mlp_kernel, units), out_shape=jax.ShapeD...  182 us

profile of v5, /device:TPU:97, one launch (start us, length us, event | category | flops | bytes accessed | tf_op | source)
XLA Modules:
  0.0 376.4 jit_solution(1658468315687737197)
XLA Ops:
  0.0 2.0 fusion.2
  2.0 1.3 pad_maximum_fusion
  3.3 188.3 %attention_part.1 = (bf16[4,128,1024]{2,1,0:T(8,128)(2,1)}, bf16[2,688,4096]{2,1,0:T(8,128)(2,1)}) custom-call(bf16[1024,512]{1,0:T(8,128)(2,1)} %bitcast.7, f32[1024,128]{1,0:T(8,128)} %get-tuple-element.12.cos_ref, f32[1024,128]{1,0:T(8,128)} %get-tuple-element.13.sin_ref, bf16[512,1024]{1,0:T(8,128)(2,1)} %wq.1, bf16[512,1024]{1,0:T(8,128)(2,1)} %wk.1, ...), custom_call_target="tpu_custom_call" | custom-call | tf_op jit(solution)/shard_map/attention_part/pallas_call | solution.py:827
  191.7 182.5 %mlp_part.1 = bf16[1024,512]{1,0:T(8,128)(2,1)} custom-call(bf16[4,128,1024]{2,1,0:T(8,128)(2,1)} %get-tuple-element.7.h_ref, bf16[2,688,4096]{2,1,0:T(8,128)(2,1)} %get-tuple-element.8.w_hbm, bf16[2752,512]{1,0:T(8,128)(2,1)} %wdn.1), custom_call_target="tpu_custom_call" | custom-call | tf_op jit(solution)/shard_map/mlp_part/pallas_call | solution.py:849
  374.1 2.3 copy.10
  (1 shorter events, 0.0 us)

commit v6 on v5

--- a/solution.py
+++ b/solution.py
@@ -2,6 +2,7 @@
 
 import jax
 import jax.numpy as jnp
+import numpy as np
 from jax import lax
 from jax.experimental import pallas as pl
 from jax.experimental.pallas import tpu as pltpu
@@ -36,33 +37,34 @@
 
 
 ATTENTION_STEPS = (
-    ("S", "b", 1, 1), ("WA", 0), ("XP", 2), ("XE", 3), ("S", "b", 0, 0), ("XP", 3), ("S", "b", 1, 0), ("XP", 0), ("WOP",),
-    ("XE", 0), ("WP", 0), ("O", "b", 1), ("ST", 3), ("WA", 1), ("ST", 0), ("S", "b", 0, 1), ("XP", 1), ("O", "b", 0),
-    ("XE", 1), ("N", 3), ("WP", 1), ("XE", 2), ("XE", 4), ("ST", 1), ("YH", 3), ("G", 3, 2), ("G", 1, 2), ("O", "a", 1),
-    ("N", 1), ("F", "a", 0), ("F", "a", 1), ("ST", 2), ("G", 2, 2), ("S", "a", 1, 0), ("N", 0), ("G", 0, 0), ("YH", 1),
-    ("N", 2), ("S", "a", 0, 1), ("S", "a", 1, 1), ("ST", 4), ("YH", 0), ("R", 3, 2), ("O", "a", 0), ("F", "b", 1), ("N", 4),
-    ("G", 1, 0), ("G", 3, 0), ("G", 0, 3), ("R", 2, 2), ("G", 2, 0), ("R", 1, 2), ("R", 3, 0), ("YH", 2), ("G", 1, 1),
-    ("R", 1, 0), ("R", 0, 3), ("A", 3, 0), ("YH", 4), ("R", 2, 0), ("G", 1, 3), ("G", 3, 1), ("G", 2, 1), ("A", 1, 0),
-    ("A", 2, 0), ("R", 3, 1), ("G", 3, 3), ("A", 3, 1), ("G", 2, 3), ("P", 2, 0), ("R", 1, 1), ("P", 1, 0), ("R", 2, 1),
-    ("R", 1, 3), ("A", 2, 1), ("R", 0, 0), ("A", 2, 2), ("A", 3, 2), ("P", 3, 0), ("R", 3, 3), ("A", 1, 1), ("R", 2, 3),
-    ("P", 2, 1), ("DP", 1), ("X", 2, 0), ("A", 2, 3), ("X", 1, 0), ("A", 1, 2), ("A", 3, 3), ("P", 3, 2), ("A", 1, 3),
-    ("P", 3, 1), ("X", 2, 1), ("X", 3, 0), ("P", 1, 2), ("P", 2, 2), ("P", 2, 3), ("P", 1, 1), ("M", 0), ("P", 3, 3),
-    ("G", 0, 1), ("G", 0, 2), ("X", 2, 2), ("X", 3, 1), ("P", 1, 3), ("X", 1, 1), ("M", 1), ("S", "a", 0, 0), ("A", 0, 0),
-    ("X", 3, 2), ("X", 1, 2), ("F", "b", 0), ("R", 0, 2), ("X", 2, 3), ("M", 2), ("X", 1, 3), ("R", 0, 1), ("A", 0, 1),
-    ("A", 0, 2), ("X", 3, 3), ("M", 3), ("A", 0, 3), ("DP", 0), ("P", 0, 0), ("P", 0, 1), ("P", 0, 2), ("P", 0, 3),
+    ("XP", 2), ("O", "b", 0), ("S", "b", 1, 1), ("XE", 3), ("WA", 0), ("XP", 3), ("WA", 1), ("WOP",), ("XP", 0), ("XE", 0),
+    ("ST", 3), ("S", "b", 1, 0), ("N", 3), ("S", "b", 0, 0), ("XP", 1), ("S", "b", 0, 1), ("XE", 1), ("XE", 2), ("O", "b", 1),
+    ("WP", 0), ("WP", 1), ("YH", 3), ("ST", 0), ("G", 1, 2), ("O", "a", 1), ("XE", 4), ("N", 0), ("ST", 1), ("G", 3, 2),
+    ("F", "a", 0), ("G", 2, 2), ("ST", 2), ("N", 1), ("S", "a", 1, 0), ("G", 0, 0), ("YH", 0), ("F", "b", 1), ("YH", 1),
+    ("R", 1, 2), ("F", "a", 1), ("G", 1, 0), ("N", 2), ("ST", 4), ("G", 2, 0), ("G", 3, 0), ("YH", 2), ("O", "a", 0),
+    ("R", 2, 2), ("N", 4), ("G", 0, 3), ("G", 3, 1), ("R", 1, 0), ("R", 2, 0), ("G", 1, 1), ("R", 3, 0), ("G", 2, 1),
+    ("S", "a", 0, 1), ("A", 1, 0), ("YH", 4), ("S", "a", 1, 1), ("G", 1, 3), ("R", 3, 1), ("R", 2, 1), ("R", 0, 0),
+    ("A", 3, 0), ("R", 1, 1), ("R", 3, 2), ("A", 2, 0), ("A", 2, 1), ("P", 1, 0), ("G", 2, 3), ("A", 1, 1), ("A", 3, 1),
+    ("P", 2, 0), ("A", 2, 2), ("P", 2, 1), ("G", 3, 3), ("DP", 1), ("R", 2, 3), ("R", 1, 3), ("A", 3, 2), ("P", 3, 1),
+    ("X", 1, 0), ("P", 3, 0), ("X", 2, 0), ("P", 2, 2), ("A", 2, 3), ("A", 1, 2), ("X", 2, 1), ("G", 0, 2), ("P", 1, 1),
+    ("R", 3, 3), ("P", 3, 2), ("X", 2, 2), ("X", 3, 0), ("M", 0), ("P", 2, 3), ("A", 3, 3), ("X", 3, 1), ("P", 1, 2),
+    ("A", 1, 3), ("G", 0, 1), ("X", 1, 1), ("M", 1), ("S", "a", 0, 0), ("X", 1, 2), ("X", 2, 3), ("R", 0, 2), ("F", "b", 0),
+    ("X", 3, 2), ("R", 0, 3), ("P", 3, 3), ("P", 1, 3), ("R", 0, 1), ("A", 0, 0), ("A", 0, 1), ("M", 2), ("A", 0, 2),
+    ("A", 0, 3), ("X", 3, 3), ("X", 1, 3), ("M", 3), ("DP", 0), ("P", 0, 0), ("P", 0, 1), ("P", 0, 2), ("P", 0, 3),
     ("X", 0, 0), ("T", 0), ("X", 0, 1), ("X", 0, 2), ("T", 1), ("T", 2), ("X", 0, 3), ("T", 3),
 )
 MLP_STEPS = (
-    ("XF", 0, 1), ("XF", 0, 2), ("YR", 0), ("XH", 0, 1), ("YRH", 0), ("XH", 0, 2), ("XF", 3, 0), ("XF", 0, 3), ("N", 0, 1),
-    ("XF", 2, 0), ("N", 0, 2), ("YH", 1), ("XH", 0, 3), ("XF", 0, 4), ("WT", 0), ("XH", 2, 0), ("XF", 1, 0), ("WT", 1),
-    ("XH", 3, 0), ("WT", 2), ("N", 0, 3), ("YH", 2), ("XF", 0, 0), ("N", 3, 0), ("XH", 1, 0), ("WT", 3), ("XH", 0, 4),
-    ("N", 2, 0), ("G", 3, 1), ("N", 1, 0), ("G", 3, 0), ("XH", 0, 0), ("G", 2, 0), ("G", 1, 0), ("YH", 3), ("P", 3, 0),
-    ("G", 1, 1), ("P", 3, 1), ("G", 1, 2), ("G", 2, 1), ("G", 0, 2), ("N", 0, 4), ("P", 1, 2), ("P", 2, 1), ("P", 1, 0),
-    ("G", 2, 2), ("P", 1, 1), ("G", 3, 2), ("G", 0, 1), ("P", 2, 0), ("P", 0, 2), ("X", 3, 1), ("X", 3, 0), ("P", 2, 2),
-    ("X", 1, 0), ("X", 2, 1), ("YH", 4), ("G", 1, 3), ("X", 1, 1), ("G", 3, 3), ("N", 0, 0), ("X", 2, 0), ("P", 3, 2),
-    ("M", 1), ("X", 2, 2), ("G", 2, 3), ("M", 0), ("P", 1, 3), ("P", 3, 3), ("X", 3, 2), ("X", 1, 2), ("M", 2), ("P", 2, 3),
-    ("G", 0, 0), ("G", 0, 3), ("X", 2, 3), ("P", 0, 1), ("P", 0, 0), ("X", 1, 3), ("X", 3, 3), ("M", 3), ("P", 0, 3),
-    ("X", 0, 2), ("T", 2), ("X", 0, 1), ("T", 1), ("X", 0, 0), ("T", 0), ("X", 0, 3), ("T", 3),
+    ("YR", 0), ("XF", 0, 1), ("XF", 0, 3), ("XH", 0, 1), ("XF", 0, 2), ("WT", 0), ("YRH", 0), ("XH", 0, 3), ("WT", 1),
+    ("XF", 0, 0), ("N", 0, 1), ("XH", 0, 2), ("XF", 0, 4), ("XF", 0, 5), ("WT", 2), ("N", 0, 3), ("N", 0, 2), ("XF", 2, 0),
+    ("XH", 0, 0), ("XH", 0, 4), ("YH", 1), ("YH", 3), ("XH", 2, 0), ("XF", 3, 0), ("XF", 1, 0), ("YH", 2), ("WT", 3),
+    ("XH", 0, 5), ("N", 0, 4), ("G", 0, 1), ("G", 3, 1), ("N", 0, 5), ("XH", 3, 0), ("N", 0, 0), ("G", 1, 1), ("G", 2, 1),
+    ("P", 3, 1), ("XH", 1, 0), ("P", 1, 1), ("P", 2, 1), ("G", 0, 3), ("N", 2, 0), ("G", 2, 0), ("G", 0, 0), ("N", 1, 0),
+    ("N", 3, 0), ("YH", 4), ("G", 1, 2), ("G", 1, 0), ("X", 3, 1), ("G", 3, 2), ("X", 1, 1), ("G", 3, 0), ("P", 0, 1),
+    ("YH", 5), ("P", 2, 0), ("G", 1, 3), ("X", 2, 1), ("G", 3, 3), ("P", 3, 0), ("X", 2, 0), ("G", 2, 2), ("P", 1, 0),
+    ("X", 3, 0), ("P", 1, 2), ("P", 2, 2), ("G", 2, 3), ("M", 1), ("X", 1, 0), ("P", 3, 2), ("X", 2, 2), ("X", 0, 1),
+    ("P", 2, 3), ("P", 1, 3), ("M", 0), ("G", 0, 2), ("P", 3, 3), ("X", 1, 2), ("X", 2, 3), ("X", 3, 2), ("M", 2), ("P", 0, 3),
+    ("X", 1, 3), ("T", 1), ("P", 0, 2), ("P", 0, 0), ("X", 3, 3), ("M", 3), ("X", 0, 3), ("X", 0, 0), ("X", 0, 2), ("T", 2),
+    ("T", 0), ("T", 3),
 )
 
 
@@ -258,15 +260,15 @@
 
 
 def attention_kernel(
-    units, x_ref, cos_ref, sin_ref, wq, wk, wv, wo, wg_t, wu_t,
+    units, x_ref, turn_ref, base_ref, wq, wk, wv, wo, wg_t, wu_t,
     h_ref, w_all,
-    xc, xg, st_own, st_in, wb, wob, part, precv, qb, kvo, kvp, og, zb, ya, yb, yfd, yfu, own, drel_a, drel_b,
+    xc, xg, cos_all, sin_all, st_own, st_in, wb, wob, part, precv, qb, kvo, kvp, og, zb, ya, yb, yfd, yfu, own, drel_a, drel_b,
     sxe, rxe, sst, rst, sy, ry, syh, ryh, sd, rd, swa, rwa, swo, rwo, swp, rwp, lw, so, ro, spr, rpr, skv, rkv, sog, rog, syr, ryr,
     lg, sds, rds, sdo, rdo, sdf, rdf, sdp, rdp,
 ):
     at = Place()
     x, c, y = at.x, at.c, at.y
-    ch, kc, h = xc.shape[1], xc.shape[2], xc.shape[1] // 2
+    ch, kc = xc.shape[1], xc.shape[2]
     kd = wq.shape[0]
     hc = qb.shape[2]
     fc, f_a = w_all.shape[1], drel_a.shape[1]
@@ -296,7 +298,7 @@
 
     def st_copy(u):
         j, lo, n, _ = units[u]
-        rows = pl.ds(lo, n)
+        rows = pl.ds(lo // 4, n // 4)
         return remote(st_own.at[j, rows], st_in.at[j, rows], sst.at[u], rst.at[u], at.pb)
 
     def XP(j):
@@ -316,13 +318,15 @@
         lane = lax.broadcasted_iota(jnp.int32, (8, 128), 1)
 
         def body(i, carry):
-            rows = pl.ds(al(lo + i * 8, 8), 8)
-            v = xg[y, j, rows, :].astype(F32)
-            total, square = jnp.sum(v, axis=-1, keepdims=True), jnp.sum(v * v, axis=-1, keepdims=True)
-            st_own[j, rows, :] = jnp.where(lane < 64, total, square)
+            packed = jnp.zeros((8, 128), F32)
+            for g in range(4):
+                v = xg[y, j, pl.ds(al(lo + g * (n // 4) + i * 8, 8), 8), :].astype(F32)
+                total, square = jnp.sum(v, axis=-1, keepdims=True), jnp.sum(v * v, axis=-1, keepdims=True)
+                packed = jnp.where(lane // 32 == g, jnp.where(lane % 32 < 16, total, square), packed)
+            st_own[j, pl.ds(al(lo // 4 + i * 8, 8), 8), :] = packed
             return carry
 
-        lax.fori_loop(0, n // 8, body, 0)
+        lax.fori_loop(0, n // 32, body, 0)
         st_copy(u).start()
 
     def N(u):
@@ -330,15 +334,17 @@
         st_copy(u).wait_recv()
 
         def body(i, carry):
-            rows = pl.ds(al(lo + i * 8, 8), 8)
-            moments = (st_own[j, rows, :] + st_in[j, rows, :]) / width
-            mean = moments[:, 0:1]
-            var = moments[:, 64:65] - mean * mean
-            v = xg[y, j, rows, :].astype(F32)
-            xg[y, j, rows, :] = ((v - mean) * lax.rsqrt(var + EPS)).astype(BF16)
+            at_rows = pl.ds(al(lo // 4 + i * 8, 8), 8)
+            moments = (st_own[j, at_rows, :] + st_in[j, at_rows, :]) / width
+            for g in range(4):
+                rows = pl.ds(al(lo + g * (n // 4) + i * 8, 8), 8)
+                mean = moments[:, 32 * g : 32 * g + 1]
+                var = moments[:, 32 * g + 16 : 32 * g + 17] - mean * mean
+                v = xg[y, j, rows, :].astype(F32)
+                xg[y, j, rows, :] = ((v - mean) * lax.rsqrt(var + EPS)).astype(BF16)
             return carry
 
-        lax.fori_loop(0, n // 8, body, 0)
+        lax.fori_loop(0, n // 32, body, 0)
         gather.YR(u)
 
     def w_rows(xx, core):
@@ -471,8 +477,7 @@
     def R(r, j):
         s, n = gather.seqs[r], r * NJ + j
         pr_copy(n).wait_recv()
-        rows = pl.ds(al((2 * j + c) * ch, 8), ch)
-        cos_t, sin_t = cos_ref[rows, :], sin_ref[rows, :]
+        cos_t, sin_t = cos_all[j], sin_all[j]
 
         def total(col, size):
             mine = part[n, :, pl.ds(al(kh * 3 * hc + col, 128), size)]
@@ -491,18 +496,20 @@
     def o_cols(xx):
         return pl.ds(al((2 * rem(div(xx + 1, 2), 2) + div(xx, 2)) * hc, 128), hc)
 
+    cut = ch // 8
+
     def og_copy(kind, n):
         if kind < 2:
             ref = og.at[n, :, o_cols(x)]
         elif kind == 2:
-            ref = og.at[n, pl.ds(0, h), o_cols(at.xa)]
+            ref = og.at[n, pl.ds(0, cut), o_cols(at.xa)]
         else:
-            ref = og.at[n, pl.ds(h, ch - h), o_cols(at.xb)]
+            ref = og.at[n, pl.ds(cut, ch - cut), o_cols(at.xb)]
         return remote(ref, ref, sog.at[kind, n], rog.at[kind, n], at.pa if kind in (0, 3) else at.pb)
 
     def og_wait(kind, n):
         xx = (at.xa, at.xb, at.xo, at.xo)[kind]
-        rows = (pl.ds(0, ch), pl.ds(0, ch), pl.ds(0, h), pl.ds(h, ch - h))[kind]
+        rows = (pl.ds(0, ch), pl.ds(0, ch), pl.ds(0, cut), pl.ds(cut, ch - cut))[kind]
         dst = og.at[n, rows, o_cols(xx)]
         remote(dst, dst, sog.at[kind, n], rog.at[kind, n], at.pa).wait_recv()
 
@@ -516,10 +523,13 @@
         par_ok = ik < (j + c) * ch
         contract = (((1,), (1,)), ((), ()))
         first = (2 * ng + kh) * hc
-        for lo in range(0, hc, HEAD_DIM):
-            q = qb[n, :, lo : lo + HEAD_DIM]
-            k_own = kvo[s, 0 : j + 1, :, lo : lo + HEAD_DIM].reshape(keys, HEAD_DIM)
-            k_par = kvp[s, 0 : j + 1, :, lo : lo + HEAD_DIM].reshape(keys, HEAD_DIM)
+
+        def head(i, carry):
+            cols = pl.ds(al(i * HEAD_DIM, 128), HEAD_DIM)
+            v_cols = pl.ds(al(hc + i * HEAD_DIM, 128), HEAD_DIM)
+            q = qb[n, :, cols]
+            k_own = kvo[s, 0 : j + 1, :, cols].reshape(keys, HEAD_DIM)
+            k_par = kvp[s, 0 : j + 1, :, cols].reshape(keys, HEAD_DIM)
             s_own = lax.dot_general(q, k_own, contract, preferred_element_type=F32) * HEAD_DIM**-0.5
             s_par = lax.dot_general(q, k_par, contract, preferred_element_type=F32) * HEAD_DIM**-0.5
             s_own = jnp.where(own_ok, s_own, -1e30)
@@ -527,11 +537,14 @@
             top = jnp.maximum(jnp.max(s_own, axis=1, keepdims=True), jnp.max(s_par, axis=1, keepdims=True))
             e_own, e_par = jnp.exp(s_own - top), jnp.exp(s_par - top)
             inv = 1.0 / (jnp.sum(e_own, axis=1, keepdims=True) + jnp.sum(e_par, axis=1, keepdims=True))
-            v_own = kvo[s, 0 : j + 1, :, hc + lo : hc + lo + HEAD_DIM].reshape(keys, HEAD_DIM)
-            v_par = kvp[s, 0 : j + 1, :, hc + lo : hc + lo + HEAD_DIM].reshape(keys, HEAD_DIM)
+            v_own = kvo[s, 0 : j + 1, :, v_cols].reshape(keys, HEAD_DIM)
+            v_par = kvp[s, 0 : j + 1, :, v_cols].reshape(keys, HEAD_DIM)
             out = jnp.dot((e_own * inv).astype(BF16), v_own, preferred_element_type=F32)
             out += jnp.dot((e_par * inv).astype(BF16), v_par, preferred_element_type=F32)
-            og[n, :, pl.ds(al(first + lo, 128), HEAD_DIM)] = out.astype(BF16)
+            og[n, :, pl.ds(al(first + i * HEAD_DIM, 128), HEAD_DIM)] = out.astype(BF16)
+            return carry
+
+        lax.fori_loop(0, hc // HEAD_DIM, head, 0)
         og_copy(0, n).start()
         og_copy(1, n).start()
 
@@ -567,11 +580,20 @@
     for j in range(NJ):
         xc[j, :, half_cols(c)] = x_ref[x_rows(j, c), :]
     at.barrier()
+
+    def angles():
+        lane = lax.broadcasted_iota(jnp.int32, (ch, HEAD_DIM), 1)
+        for j in range(NJ):
+            base_cos, base_sin = base_ref[0, pl.ds(2 * j + c, 1), :], base_ref[1, pl.ds(2 * j + c, 1), :]
+            cos_all[j] = base_cos * turn_ref[0] - base_sin * turn_ref[1]
+            sine = base_sin * turn_ref[0] + base_cos * turn_ref[1]
+            sin_all[j] = jnp.where(lane < HEAD_DIM // 2, -sine, sine)
+
     ops = {
         "XP": XP, "WOP": WOP, "XE": XE, "ST": ST, "N": N, "YH": gather.YH, "WA": WA, "WP": WP, "S": S, "O": O, "F": F, "DP": DP,
         "G": G, "R": R, "A": A, "P": P, "X": X, "M": reduce.middle, "T": T,
     }
-    waits = {"G": w_ready, "X": o_ready}
+    waits = {"G": w_ready, "X": o_ready, "WP": angles}
     for step in ATTENTION_STEPS:
         if step[0] in waits:
             waits.pop(step[0])()
@@ -615,7 +637,7 @@
 
 def mlp_kernel(
     units, h_ref, w_hbm, wdn, y_ref,
-    xg, wt, raw, wd, ag, acc, zb, ya, yb, yfd, yfu, yst,
+    xg, wt, raw, wd, wr, ag, ar, act, acc, zb, ya, yb, yfd, yfu, yst,
     sx, rx, sy, ry, syh, ryh, sa, ra, syr, ryr, sd, rd, lw, lwd, swd, rwd,
 ):
     at = Place()
@@ -624,7 +646,8 @@
     width = xg.shape[-1]
     kd = kc // 2
     fc, tiles = w_hbm.shape[1], wt.shape[1] // 256
-    fp = tiles * 128
+    fm = (tiles - 1) * 128
+    fr = fc - fm
     blocks, slots = 2 * tiles, raw.shape[0]
     gather = Spread(at, h_ref, xg, units, sx, rx, sy, ry, syh, ryh)
     reduce = Reduce(at, zb, ya, yb, yfd, yfu, syr, ryr)
@@ -650,44 +673,48 @@
             if q + slots < blocks:
                 w_in(q + slots).start()
 
-    def d_own(q):
-        return pltpu.make_async_copy(wdn.at[pl.ds(q * fc, fc)], wd.at[pl.ds(q * fp, fc), pl.ds(al(c * kd, 128), kd)], lwd.at[q])
-
-    def d_pair(q):
-        dst = wd.at[pl.ds(q * fp, fc), pl.ds(al(c * kd, 128), kd)]
-        return remote(wdn.at[pl.ds(q * fc, fc)], dst, swd.at[q], rwd.at[q], at.partner)
-
-    def d_pair_wait(q):
-        dst = wd.at[pl.ds(q * fp, fc), pl.ds(al((1 - c) * kd, 128), kd)]
-        remote(dst, dst, swd.at[q], rwd.at[q], at.partner).wait_recv()
-
+    def d_refs(q, core):
+        cols = pl.ds(al(core * kd, 128), kd)
+        main, rest = wdn.at[pl.ds(q * fc, fm)], wdn.at[pl.ds(q * fc + fm, fr)]
+        return (main, wd.at[pl.ds(q * fm, fm), cols]), (rest, wr.at[pl.ds(q * 128, fr), cols])
+
+    def d_own(q, k):
+        src, dst = d_refs(q, c)[k]
+        return pltpu.make_async_copy(src, dst, lwd.at[q, k])
+
+    def d_pair(q, k, core):
+        src, dst = d_refs(q, core)[k]
+        return remote(src, dst, swd.at[q, k], rwd.at[q, k], at.partner)
+
+    quarters = [(q, k) for q in range(NX) for k in range(2)]
     for q in range(slots):
         w_in(q).start()
+    for q, k in quarters:
+        d_own(q, k).start()
     for q in range(NX):
-        d_own(q).start()
-        if fc < fp:
-            wd[q * fp + fc : (q + 1) * fp, :] = jnp.zeros((fp - fc, kc), BF16)
+        wr[q * 128 + fr : (q + 1) * 128, :] = jnp.zeros((128 - fr, kc), BF16)
     at.barrier()
-    for q in range(NX):
-        d_pair(q).start()
-
-    def a_cols(xx):
-        return pl.ds(al(xx * fp, 128), fp)
-
-    def a_copy(kind, n):
+    for q, k in quarters:
+        d_pair(q, k, c).start()
+
+    def a_refs(kind, n, xx):
+        main, rest = pl.ds(al(xx * fm, 128), fm), pl.ds(al(xx * 128, 128), 128)
         if kind < 2:
-            ref = ag.at[n, :, a_cols(x)]
-        elif kind == 2:
-            ref = ag.at[n, pl.ds(0, h), a_cols(at.xl)]
-        else:
-            ref = ag.at[n, pl.ds(h, ch - h), a_cols(at.xr)]
-        return remote(ref, ref, sa.at[kind, n], ra.at[kind, n], at.left if kind % 2 else at.right)
+            return ag.at[n, :, main], ar.at[n, :, rest]
+        lo = (kind - 2) * h
+        return ag.at[n, pl.ds(lo, h), main], ar.at[n, pl.ds(lo // 2, h // 2), rest]
+
+    def a_copies(kind, n):
+        refs = a_refs(kind, n, (x, x, at.xl, at.xr)[kind])
+        return [remote(v, v, sa.at[kind, n, k], ra.at[kind, n, k], at.left if kind % 2 else at.right) for k, v in enumerate(refs)]
 
     def a_wait(kind, n):
-        xx = (at.xl, at.xr, at.xo, at.xo)[kind]
-        rows = (pl.ds(0, ch), pl.ds(0, ch), pl.ds(0, h), pl.ds(h, ch - h))[kind]
-        dst = ag.at[n, rows, a_cols(xx)]
-        remote(dst, dst, sa.at[kind, n], ra.at[kind, n], at.right).wait_recv()
+        for k, v in enumerate(a_refs(kind, n, (at.xl, at.xr, at.xo, at.xo)[kind])):
+            remote(v, v, sa.at[kind, n, k], ra.at[kind, n, k], at.right).wait_recv()
+
+    def a_start(kind, n):
+        for copy in a_copies(kind, n):
+            copy.start()
 
     def G(r, j):
         gather.chunk_wait(r, j)
@@ -705,30 +732,37 @@
             lax.fori_loop(0, 2, depth, 0)
             out = acc[...]
             g, u = out[:, :128].astype(BF16).astype(F32), out[:, 128:].astype(BF16).astype(F32)
-            ag[n, :, pl.ds(al(x * fp + i * 128, 128), 128)] = (g / (1.0 + jnp.exp(-g)) * u).astype(BF16)
+            act[:, pl.ds(al(i * 128, 128), 128)] = (g / (1.0 + jnp.exp(-g)) * u).astype(BF16)
             return carry
 
         lax.fori_loop(0, tiles, columns, 0)
+        ag[n, :, pl.ds(al(x * fm, 128), fm)] = act[:, :fm]
+        below = pltpu.roll(act[h:, fm:].astype(F32), 64, axis=1)
+        ar[n, :, pl.ds(al(x * 128, 128), 128)] = (act[:h, fm:].astype(F32) + below).astype(BF16)
         for kind in range(2):
-            a_copy(kind, n).start()
+            a_start(kind, n)
 
     def P(r, j):
         n = r * NJ + j
         for kind in range(2):
             a_wait(kind, n)
-            a_copy(kind + 2, n).start()
+            a_start(kind + 2, n)
 
     def X(r, j):
         n = r * NJ + j
         for kind in (2, 3):
             a_wait(kind, n)
+        for q in range(NX):
+            cols = pl.ds(q * 128, 128)
+            act[0:h, cols] = ar[n, :, cols]
+            act[h:, cols] = pltpu.roll(ar[n, :, cols].astype(F32), 64, axis=1).astype(BF16)
 
         def columns(i, carry):
             cols = pl.ds(al(i * 256, 128), 256)
-            acc[...] = jnp.zeros_like(acc)
+            acc[...] = jnp.dot(act[:, : NX * 128], wr[:, cols], preferred_element_type=F32)
 
             def depth(k, carry):
-                part = pl.ds(al(k * 2 * fp, 128), 2 * fp)
+                part = pl.ds(al(k * 2 * fm, 128), 2 * fm)
                 acc[...] += jnp.dot(ag[n, :, part], wd[part, cols], preferred_element_type=F32)
                 return carry
 
@@ -763,7 +797,7 @@
         ops[name] = getattr(gather, name)
     waits = {
         "N": gather.keep_own,
-        "X": lambda: [(d_own(q).wait(), d_pair_wait(q)) for q in range(NX)],
+        "X": lambda: [(d_own(q, k).wait(), d_pair(q, k, 1 - c).wait_recv()) for q, k in quarters],
     }
     for step in MLP_STEPS:
         if step[0] in waits:
@@ -772,12 +806,13 @@
 
     gather.drain()
     reduce.drain()
-    for q in range(NX):
-        d_pair(q).wait_send()
+    for q, k in quarters:
+        d_pair(q, k, c).wait_send()
 
     def chunk_sent(n, carry):
         for kind in range(4):
-            a_copy(kind, n).wait_send()
+            for copy in a_copies(kind, n):
+                copy.wait_send()
         return carry
 
     lax.fori_loop(0, NCH, chunk_sent, 0)
@@ -814,12 +849,12 @@
         tiles = (fc + 127) // 128
         f_a = (fc // 2 + 15) // 16 * 16
 
-        half = HEAD_DIM // 2
-        inv_freq = THETA ** (-2.0 * jnp.arange(half, dtype=F32) / HEAD_DIM)
-        angles = jnp.arange(seq, dtype=F32)[:, None] * inv_freq[None, :]
-        cos_t, sin_t = jnp.cos(angles), jnp.sin(angles)
-        cos_t = jnp.concatenate([cos_t, cos_t], axis=1)
-        sin_t = jnp.concatenate([-sin_t, sin_t], axis=1)
+        inv_freq = THETA ** (-2.0 * np.arange(HEAD_DIM // 2) / HEAD_DIM)
+        inv_freq = np.concatenate([inv_freq, inv_freq])
+        turn = np.arange(ch)[:, None] * inv_freq
+        base = np.arange(2 * NJ)[:, None] * ch * inv_freq
+        turn = jnp.asarray(np.stack([np.cos(turn), np.sin(turn)]), F32)
+        base = jnp.asarray(np.stack([np.cos(base), np.sin(base)]), F32)
 
         reduce_scratch = [vmem(NX, NJ, ch, kc), vmem(NJ, h, kc), vmem(NJ, ch - h, kc), vmem(NJ, ch, kc), vmem(NJ, ch, kc)]
         units = ((0, 0, h, 0), (0, h, h, 0)) + tuple((j, 0, ch, 0) for j in range(1, NJ))
@@ -830,7 +865,8 @@
             in_specs=[vmem_spec] * 3 + [any_spec] * 6,
             out_specs=(vmem_spec, any_spec),
             scratch_shapes=[
-                vmem(NJ, ch, kc), vmem(NX, NJ, ch, 2 * kc), vmem(NJ, ch, 128, dtype=F32), vmem(NJ, ch, 128, dtype=F32),
+                vmem(NJ, ch, kc), vmem(NX, NJ, ch, 2 * kc), vmem(NJ, ch, HEAD_DIM, dtype=F32), vmem(NJ, ch, HEAD_DIM, dtype=F32),
+                vmem(NJ, ch // 4, 128, dtype=F32), vmem(NJ, ch // 4, 128, dtype=F32),
                 vmem(2 * kc, 6 * hc), vmem(row_heads, kc), vmem(NCH, ch, 6 * hc), vmem(NCH, ch, 3 * hc), vmem(NCH, ch, hc),
                 vmem(NX, NJ, ch, 2 * hc), vmem(NX, NJ, ch, 2 * hc), vmem(NCH, ch, row_heads), *reduce_scratch,
                 vmem(2, fc, kd), vmem(2, f_a, kd), vmem(2, fc - f_a, kd),
@@ -841,23 +877,25 @@
             ],
             compiler_params=pltpu.CompilerParams(collective_id=0, has_side_effects=True, vmem_limit_bytes=VMEM_LIMIT),
             name="attention_part",
-        )(x_blk[0], cos_t, sin_t, w_q, w_k, w_v, w_o, w_gate.T, w_up.T)
+        )(x_blk[0], turn, base, w_q, w_k, w_v, w_o, w_gate.T, w_up.T)
 
         first = ch * 3 // 4
-        units = ((0, 0, first, 1), (0, first, ch - first, 0)) + tuple((j, 0, ch, 0) for j in range(1, NJ))
-        n_x = n_u + 3
+        units = ((0, 0, first, 1), (0, first, ch - first, 0), (1, 0, h, 0), (1, h, h, 0)) + tuple((j, 0, ch, 0) for j in range(2, NJ))
+        n_u, n_x = len(units), len(units) + 3
         y_blk = pl.pallas_call(
             functools.partial(mlp_kernel, units),
             out_shape=jax.ShapeDtypeStruct((seq, kd), BF16),
             in_specs=[vmem_spec, any_spec, any_spec],
             out_specs=vmem_spec,
             scratch_shapes=[
-                vmem(NX, NJ, ch, width), vmem(width, tiles * 256), vmem(3, 128, width), vmem(NX * tiles * 128, kc), vmem(NCH, ch, NX * tiles * 128),
+                vmem(NX, NJ, ch, width), vmem(width, tiles * 256), vmem(3, 128, width),
+                vmem(NX * (tiles - 1) * 128, kc), vmem(NX * 128, kc), vmem(NCH, ch, NX * (tiles - 1) * 128), vmem(NCH, h, NX * 128),
+                vmem(ch, tiles * 128),
                 vmem(ch, 256, dtype=F32),
                 *reduce_scratch, vmem(2, NJ, ch, kd),
                 sems(4, n_x), sems(4, n_x), sems(2, n_u), sems(2, n_u), sems(2, n_u), sems(2, n_u),
-                sems(4, NCH), sems(4, NCH), sems(4, NJ), sems(4, NJ), sems(NJ), sems(NJ),
-                sems(2 * tiles), sems(NX), sems(NX), sems(NX),
+                sems(4, NCH, 2), sems(4, NCH, 2), sems(4, NJ), sems(4, NJ), sems(NJ), sems(NJ),
+                sems(2 * tiles), sems(NX, 2), sems(NX, 2), sems(NX, 2),
             ],
             compiler_params=pltpu.CompilerParams(collective_id=1, has_side_effects=True, vmem_limit_bytes=VMEM_LIMIT),
             name="mlp_part",

time: 377 us -> 371 us (0.984)
    pallas_call x1, Pallas kernels: 188 us -> 177 us  [layer(): pl.pallas_call(functools.partial(attention_kernel, units), out_shape=(jax...]
    pallas_call x1, Pallas kernels: 182 us -> 191 us  [layer(): pl.pallas_call(functools.partial(mlp_kernel, units), out_shape=jax.ShapeD...]
where the time goes in v6:
time: 371 us; the launch traced here: 370 us
  Pallas kernels  368 us (99%)
    pallas_call x1, Pallas kernels, layer(): pl.pallas_call(functools.partial(mlp_kernel, units), out_shape=jax.ShapeD...  191 us
    pallas_call x1, Pallas kernels, layer(): pl.pallas_call(functools.partial(attention_kernel, units), out_shape=(jax...  177 us

profile of v6, /device:TPU:97, one launch (start us, length us, event | category | flops | bytes accessed | tf_op | source)
XLA Modules:
  0.0 370.5 jit_solution(315668450550525177)
XLA Ops:
  0.0 176.7 %attention_part.1 = (bf16[4,128,1024]{2,1,0:T(8,128)(2,1)}, bf16[2,688,4096]{2,1,0:T(8,128)(2,1)}) custom-call(bf16[1024,512]{1,0:T(8,128)(2,1)} %bitcast.7, f32[2,128,128]{2,1,0:T(8,128)} %constant.4.clone.turn_ref, f32[2,8,128]{2,1,0:T(8,128)} %constant.5.clone.base_ref, bf16[512,1024]{1,0:T(8,128)(2,1)} %wq.1, bf16[512,1024]{1,0:T(8,128)(2,1)} %wk.1, ...), custom_call_target="tpu_custom_call" | custom-call | tf_op jit(solution)/shard_map/attention_part/pallas_call | solution.py:862
  176.7 191.5 %mlp_part.1 = bf16[1024,512]{1,0:T(8,128)(2,1)} custom-call(bf16[4,128,1024]{2,1,0:T(8,128)(2,1)} %get-tuple-element.7.h_ref, bf16[2,688,4096]{2,1,0:T(8,128)(2,1)} %get-tuple-element.8.w_hbm, bf16[2752,512]{1,0:T(8,128)(2,1)} %wdn.1), custom_call_target="tpu_custom_call" | custom-call | tf_op jit(solution)/shard_map/mlp_part/pallas_call | solution.py:885
  368.2 2.3 copy.12

commit v7 on v6

--- a/solution.py
+++ b/solution.py
@@ -18,6 +18,7 @@
 NJ = 4
 NCH = 16
 VMEM_LIMIT = 67_043_328
+GROUPS = (((0, 0), (0, 1)), ((0, 2), (0, 3)), *(((3, j), (1, j)) for j in range(NJ)), *(((2, j),) for j in range(NJ)))
 
 
 def rem(a, b):
@@ -37,34 +38,26 @@
 
 
 ATTENTION_STEPS = (
-    ("XP", 2), ("O", "b", 0), ("S", "b", 1, 1), ("XE", 3), ("WA", 0), ("XP", 3), ("WA", 1), ("WOP",), ("XP", 0), ("XE", 0),
-    ("ST", 3), ("S", "b", 1, 0), ("N", 3), ("S", "b", 0, 0), ("XP", 1), ("S", "b", 0, 1), ("XE", 1), ("XE", 2), ("O", "b", 1),
-    ("WP", 0), ("WP", 1), ("YH", 3), ("ST", 0), ("G", 1, 2), ("O", "a", 1), ("XE", 4), ("N", 0), ("ST", 1), ("G", 3, 2),
-    ("F", "a", 0), ("G", 2, 2), ("ST", 2), ("N", 1), ("S", "a", 1, 0), ("G", 0, 0), ("YH", 0), ("F", "b", 1), ("YH", 1),
-    ("R", 1, 2), ("F", "a", 1), ("G", 1, 0), ("N", 2), ("ST", 4), ("G", 2, 0), ("G", 3, 0), ("YH", 2), ("O", "a", 0),
-    ("R", 2, 2), ("N", 4), ("G", 0, 3), ("G", 3, 1), ("R", 1, 0), ("R", 2, 0), ("G", 1, 1), ("R", 3, 0), ("G", 2, 1),
-    ("S", "a", 0, 1), ("A", 1, 0), ("YH", 4), ("S", "a", 1, 1), ("G", 1, 3), ("R", 3, 1), ("R", 2, 1), ("R", 0, 0),
-    ("A", 3, 0), ("R", 1, 1), ("R", 3, 2), ("A", 2, 0), ("A", 2, 1), ("P", 1, 0), ("G", 2, 3), ("A", 1, 1), ("A", 3, 1),
-    ("P", 2, 0), ("A", 2, 2), ("P", 2, 1), ("G", 3, 3), ("DP", 1), ("R", 2, 3), ("R", 1, 3), ("A", 3, 2), ("P", 3, 1),
-    ("X", 1, 0), ("P", 3, 0), ("X", 2, 0), ("P", 2, 2), ("A", 2, 3), ("A", 1, 2), ("X", 2, 1), ("G", 0, 2), ("P", 1, 1),
-    ("R", 3, 3), ("P", 3, 2), ("X", 2, 2), ("X", 3, 0), ("M", 0), ("P", 2, 3), ("A", 3, 3), ("X", 3, 1), ("P", 1, 2),
-    ("A", 1, 3), ("G", 0, 1), ("X", 1, 1), ("M", 1), ("S", "a", 0, 0), ("X", 1, 2), ("X", 2, 3), ("R", 0, 2), ("F", "b", 0),
-    ("X", 3, 2), ("R", 0, 3), ("P", 3, 3), ("P", 1, 3), ("R", 0, 1), ("A", 0, 0), ("A", 0, 1), ("M", 2), ("A", 0, 2),
-    ("A", 0, 3), ("X", 3, 3), ("X", 1, 3), ("M", 3), ("DP", 0), ("P", 0, 0), ("P", 0, 1), ("P", 0, 2), ("P", 0, 3),
-    ("X", 0, 0), ("T", 0), ("X", 0, 1), ("X", 0, 2), ("T", 1), ("T", 2), ("X", 0, 3), ("T", 3),
+    ("XP", 2), ("XP", 0), ("S", "b", 0, 0), ("XE", 3), ("XP", 1), ("WA", 0), ("S", "b", 0, 1), ("ST", 3), ("O", "b", 1),
+    ("N", 3), ("O", "b", 0), ("XP", 3), ("WA", 1), ("XE", 0), ("WOP",), ("S", "b", 1, 0), ("WP", 0), ("XE", 1), ("XE", 2),
+    ("YH", 3), ("S", "b", 1, 1), ("WP", 1), ("O", "a", 1), ("S", "a", 1, 0), ("ST", 0), ("G", 8), ("ST", 1), ("N", 0),
+    ("G", 4), ("N", 1), ("YH", 0), ("ST", 2), ("XE", 4), ("F", "a", 0), ("F", "b", 1), ("O", "a", 0), ("YH", 1), ("F", "a", 1),
+    ("N", 2), ("G", 2), ("ST", 4), ("G", 6), ("YH", 2), ("G", 3), ("S", "a", 1, 1), ("N", 4), ("G", 7), ("R", 6), ("R", 2),
+    ("G", 1), ("R", 3), ("R", 7), ("YH", 4), ("R", 8), ("A", 2), ("A", 6), ("A", 7), ("A", 8), ("R", 4), ("G", 9),
+    ("S", "a", 0, 1), ("P", 2), ("R", 1), ("G", 5), ("P", 8), ("P", 6), ("DP", 1), ("P", 7), ("A", 3), ("A", 4), ("R", 9),
+    ("A", 9), ("G", 0), ("X", 8), ("R", 5), ("X", 6), ("P", 3), ("X", 7), ("A", 5), ("P", 9), ("P", 4), ("X", 2),
+    ("S", "a", 0, 0), ("M", 0), ("F", "b", 0), ("X", 3), ("M", 1), ("P", 5), ("R", 0), ("X", 9), ("X", 4), ("M", 2), ("A", 0),
+    ("A", 1), ("X", 5), ("M", 3), ("DP", 0), ("P", 0), ("P", 1), ("X", 0), ("T", 1), ("T", 0), ("X", 1), ("T", 2), ("T", 3),
 )
 MLP_STEPS = (
-    ("YR", 0), ("XF", 0, 1), ("XF", 0, 3), ("XH", 0, 1), ("XF", 0, 2), ("WT", 0), ("YRH", 0), ("XH", 0, 3), ("WT", 1),
-    ("XF", 0, 0), ("N", 0, 1), ("XH", 0, 2), ("XF", 0, 4), ("XF", 0, 5), ("WT", 2), ("N", 0, 3), ("N", 0, 2), ("XF", 2, 0),
-    ("XH", 0, 0), ("XH", 0, 4), ("YH", 1), ("YH", 3), ("XH", 2, 0), ("XF", 3, 0), ("XF", 1, 0), ("YH", 2), ("WT", 3),
-    ("XH", 0, 5), ("N", 0, 4), ("G", 0, 1), ("G", 3, 1), ("N", 0, 5), ("XH", 3, 0), ("N", 0, 0), ("G", 1, 1), ("G", 2, 1),
-    ("P", 3, 1), ("XH", 1, 0), ("P", 1, 1), ("P", 2, 1), ("G", 0, 3), ("N", 2, 0), ("G", 2, 0), ("G", 0, 0), ("N", 1, 0),
-    ("N", 3, 0), ("YH", 4), ("G", 1, 2), ("G", 1, 0), ("X", 3, 1), ("G", 3, 2), ("X", 1, 1), ("G", 3, 0), ("P", 0, 1),
-    ("YH", 5), ("P", 2, 0), ("G", 1, 3), ("X", 2, 1), ("G", 3, 3), ("P", 3, 0), ("X", 2, 0), ("G", 2, 2), ("P", 1, 0),
-    ("X", 3, 0), ("P", 1, 2), ("P", 2, 2), ("G", 2, 3), ("M", 1), ("X", 1, 0), ("P", 3, 2), ("X", 2, 2), ("X", 0, 1),
-    ("P", 2, 3), ("P", 1, 3), ("M", 0), ("G", 0, 2), ("P", 3, 3), ("X", 1, 2), ("X", 2, 3), ("X", 3, 2), ("M", 2), ("P", 0, 3),
-    ("X", 1, 3), ("T", 1), ("P", 0, 2), ("P", 0, 0), ("X", 3, 3), ("M", 3), ("X", 0, 3), ("X", 0, 0), ("X", 0, 2), ("T", 2),
-    ("T", 0), ("T", 3),
+    ("YR", 0), ("XF", 0, 1), ("XF", 0, 3), ("WT", 0), ("XH", 0, 1), ("XF", 0, 2), ("YRH", 0), ("XH", 0, 3), ("XF", 0, 5),
+    ("N", 0, 1), ("N", 0, 3), ("XH", 0, 2), ("XF", 0, 4), ("N", 0, 2), ("XF", 2, 0), ("XF", 3, 0), ("XF", 0, 0), ("XH", 3, 0),
+    ("XH", 2, 0), ("XH", 0, 4), ("WT", 1), ("YH", 1), ("XF", 1, 0), ("WT", 2), ("WT", 3), ("XH", 0, 5), ("YH", 3), ("YH", 2),
+    ("G", 3), ("N", 3, 0), ("N", 0, 4), ("XH", 0, 0), ("N", 0, 5), ("G", 7), ("N", 2, 0), ("G", 6), ("N", 0, 0), ("XH", 1, 0),
+    ("P", 3), ("G", 0), ("G", 1), ("P", 7), ("N", 1, 0), ("X", 3), ("G", 2), ("P", 6), ("YH", 4), ("G", 4), ("YH", 5),
+    ("X", 7), ("G", 5), ("X", 6), ("G", 8), ("P", 2), ("P", 8), ("G", 9), ("M", 1), ("P", 4), ("X", 8), ("X", 2), ("P", 9),
+    ("M", 0), ("P", 5), ("P", 0), ("P", 1), ("X", 9), ("X", 4), ("M", 2), ("X", 5), ("M", 3), ("X", 0), ("T", 0), ("X", 1),
+    ("T", 1), ("T", 2), ("T", 3),
 )
 
 
@@ -91,7 +84,8 @@
 
 
 class Spread:
-    def __init__(self, at, src, xg, units, sx, rx, sy, ry, syh, ryh):
+    def __init__(self, at, src, xg, units, sums, sx, rx, sy, ry, syh, ryh):
+        self.sums = sums
         self.at, self.src, self.xg, self.units, self.kc = at, src, xg, units, src.shape[2]
         self.sx, self.rx, self.sy, self.ry, self.syh, self.ryh = sx, rx, sy, ry, syh, ryh
         pairs = [(r, u) for u, unit in enumerate(units) for r in ((0, 3, 1, 2) if unit[3] else (0,))]
@@ -186,17 +180,14 @@
                 self.xcopy(kind, r, u).wait_send()
         if r % 2:
             self.yhalf(0 if r == 3 else 1, u).wait_send()
-        width, rows, s = self.xg.shape[-1], 8, self.seqs[r]
-
-        def body(i, carry):
-            at_rows = pl.ds(al(lo + i * rows, rows), rows)
-            v = self.xg[s, j, at_rows, :].astype(F32)
-            mean = jnp.sum(v, axis=-1, keepdims=True) / width
-            var = jnp.sum(v * v, axis=-1, keepdims=True) / width - mean * mean
-            self.xg[s, j, at_rows, :] = ((v - mean) * lax.rsqrt(var + EPS)).astype(BF16)
-            return carry
-
-        lax.fori_loop(0, n // rows, body, 0)
+        width, ref = self.xg.shape[-1], self.xg.at[self.seqs[r], j]
+        s1, s2 = self.sums
+        lane_sums(ref, lo, n, s1, s2)
+        mean = jnp.sum(s1[0:n, :], axis=-1, keepdims=True) / width
+        var = jnp.sum(s2[0:n, :], axis=-1, keepdims=True) / width - mean * mean
+        s1[0:n, :] = jnp.broadcast_to(mean, (n, 128))
+        s2[0:n, :] = jnp.broadcast_to(lax.rsqrt(var + EPS), (n, 128))
+        scale_rows(ref, lo, n, s1, s2)
         if not first:
             self.YR(u)
 
@@ -214,6 +205,61 @@
                 self.ycopy(d, u).wait_send()
                 if not unit[3]:
                     self.yhalf(d, u).wait_send()
+
+
+def rows_of(refs):
+    return refs[0][...] if len(refs) == 1 else jnp.concatenate([ref[...] for ref in refs], axis=0)
+
+
+def product(refs, weight, depth, n_cols, done, wide=True):
+    step = 512 if wide and len(refs) == 1 and n_cols % 512 == 0 else 256
+
+    def columns(i, carry):
+        out = jnp.dot(rows_of(refs), weight[0:depth, pl.ds(al(i * step, 128), step)], preferred_element_type=F32)
+        done(i * step, step, out)
+        return carry
+
+    lax.fori_loop(0, n_cols // step, columns, 0)
+
+
+def lane_sums(ref, lo, n, s1, s2):
+    width, rows, wide = ref.shape[-1], 32, 512
+
+    def some_rows(i, carry):
+        def some_columns(k, sums):
+            a, b = sums
+            v = ref[pl.ds(al(lo + i * rows, 8), rows), pl.ds(al(k * wide, 128), wide)].astype(F32)
+            for c in range(0, wide, 128):
+                part = v[:, c : c + 128]
+                a, b = a + part, b + part * part
+            return a, b
+
+        zero = jnp.zeros((rows, 128), F32)
+        a, b = lax.fori_loop(0, width // wide, some_columns, (zero, zero))
+        s1[pl.ds(al(i * rows, 8), rows), :] = a
+        s2[pl.ds(al(i * rows, 8), rows), :] = b
+        return carry
+
+    lax.fori_loop(0, n // rows, some_rows, 0)
+
+
+def scale_rows(ref, lo, n, means, scales):
+    width, rows, wide = ref.shape[-1], 32, 512
+
+    def some_rows(i, carry):
+        mean, scale = (t[pl.ds(al(i * rows, 8), rows), :] for t in (means, scales))
+
+        def some_columns(k, carry):
+            at_rows = pl.ds(al(lo + i * rows, 8), rows)
+            for c in range(0, wide, 128):
+                cols = pl.ds(al(k * wide + c, 128), 128)
+                ref[at_rows, cols] = ((ref[at_rows, cols].astype(F32) - mean) * scale).astype(BF16)
+            return carry
+
+        lax.fori_loop(0, width // wide, some_columns, 0)
+        return carry
+
+    lax.fori_loop(0, n // rows, some_rows, 0)
 
 
 class Reduce:
@@ -262,7 +308,7 @@
 def attention_kernel(
     units, x_ref, turn_ref, base_ref, wq, wk, wv, wo, wg_t, wu_t,
     h_ref, w_all,
-    xc, xg, cos_all, sin_all, st_own, st_in, wb, wob, part, precv, qb, kvo, kvp, og, zb, ya, yb, yfd, yfu, own, drel_a, drel_b,
+    xc, xg, cos_all, sin_all, st_own, st_in, s1, s2, wb, wob, part, precv, qb, kvo, kvp, og, zb, ya, yb, yfd, yfu, own, drel_a, drel_b,
     sxe, rxe, sst, rst, sy, ry, syh, ryh, sd, rd, swa, rwa, swo, rwo, swp, rwp, lw, so, ro, spr, rpr, skv, rkv, sog, rog, syr, ryr,
     lg, sds, rds, sdo, rdo, sdf, rdf, sdp, rdp,
 ):
@@ -275,7 +321,7 @@
     width = 2 * xg.shape[3]
     kh = div(x, 2)
     ng = rem(div(x + 1, 2), 2)
-    gather = Spread(at, xc, xg, units, None, None, sy, ry, syh, ryh)
+    gather = Spread(at, xc, xg, units, (s1, s2), None, None, sy, ry, syh, ryh)
     reduce = Reduce(at, zb, ya, yb, yfd, yfu, syr, ryr)
     weights = (wq, wk, wv)
 
@@ -315,36 +361,30 @@
     def ST(u):
         j, lo, n, _ = units[u]
         xe_copy(u, at.xa).wait_recv()
-        lane = lax.broadcasted_iota(jnp.int32, (8, 128), 1)
-
-        def body(i, carry):
-            packed = jnp.zeros((8, 128), F32)
-            for g in range(4):
-                v = xg[y, j, pl.ds(al(lo + g * (n // 4) + i * 8, 8), 8), :].astype(F32)
-                total, square = jnp.sum(v, axis=-1, keepdims=True), jnp.sum(v * v, axis=-1, keepdims=True)
-                packed = jnp.where(lane // 32 == g, jnp.where(lane % 32 < 16, total, square), packed)
-            st_own[j, pl.ds(al(lo // 4 + i * 8, 8), 8), :] = packed
-            return carry
-
-        lax.fori_loop(0, n // 32, body, 0)
+        quarter = n // 4
+        lane = lax.broadcasted_iota(jnp.int32, (quarter, 128), 1)
+        lane_sums(xg.at[y, j], lo, n, s1, s2)
+        packed = jnp.zeros((quarter, 128), F32)
+        for g in range(4):
+            rows = pl.ds(g * quarter, quarter)
+            total, square = (jnp.sum(t[rows, :], axis=-1, keepdims=True) for t in (s1, s2))
+            packed = jnp.where(lane // 32 == g, jnp.where(lane % 32 < 16, total, square), packed)
+        st_own[j, lo // 4 : lo // 4 + quarter, :] = packed
         st_copy(u).start()
 
     def N(u):
         j, lo, n, _ = units[u]
         st_copy(u).wait_recv()
-
-        def body(i, carry):
-            at_rows = pl.ds(al(lo // 4 + i * 8, 8), 8)
-            moments = (st_own[j, at_rows, :] + st_in[j, at_rows, :]) / width
-            for g in range(4):
-                rows = pl.ds(al(lo + g * (n // 4) + i * 8, 8), 8)
-                mean = moments[:, 32 * g : 32 * g + 1]
-                var = moments[:, 32 * g + 16 : 32 * g + 17] - mean * mean
-                v = xg[y, j, rows, :].astype(F32)
-                xg[y, j, rows, :] = ((v - mean) * lax.rsqrt(var + EPS)).astype(BF16)
-            return carry
-
-        lax.fori_loop(0, n // 32, body, 0)
+        quarter = n // 4
+        at_rows = slice(lo // 4, lo // 4 + quarter)
+        moments = (st_own[j, at_rows, :] + st_in[j, at_rows, :]) / width
+        for g in range(4):
+            mean = moments[:, 32 * g : 32 * g + 1]
+            var = moments[:, 32 * g + 16 : 32 * g + 17] - mean * mean
+            rows = pl.ds(g * quarter, quarter)
+            s1[rows, :] = jnp.broadcast_to(mean, (quarter, 128))
+            s2[rows, :] = jnp.broadcast_to(lax.rsqrt(var + EPS), (quarter, 128))
+        scale_rows(xg.at[y, j], lo, n, s1, s2)
         gather.YR(u)
 
     def w_rows(xx, core):
@@ -458,23 +498,23 @@
         src = part.at[n, :, pl.ds(al((1 - kh) * 3 * hc, 128), 3 * hc)]
         return remote(src, precv.at[n], spr.at[n], rpr.at[n], at.pb)
 
-    def G(r, j):
-        gather.chunk_wait(r, j)
-        s, n = gather.seqs[r], r * NJ + j
-
-        def columns(i, carry):
-            cols = pl.ds(al(i * 256, 128), 256)
-            part[n, :, cols] = jnp.dot(xg[s, j], wb[:, cols], preferred_element_type=F32).astype(BF16)
-            return carry
-
-        lax.fori_loop(0, wb.shape[1] // 256, columns, 0)
-        pr_copy(n).start()
+    def G(g):
+        for r, j in GROUPS[g]:
+            gather.chunk_wait(r, j)
+
+        def done(col, size, out):
+            for i, (r, j) in enumerate(GROUPS[g]):
+                part[r * NJ + j, :, pl.ds(al(col, 128), size)] = out[i * ch : (i + 1) * ch].astype(BF16)
+
+        product([xg.at[gather.seqs[r], j] for r, j in GROUPS[g]], wb, wb.shape[0], wb.shape[1], done)
+        for r, j in GROUPS[g]:
+            pr_copy(r * NJ + j).start()
 
     def kv_copy(r, j):
         s, n = gather.seqs[r], r * NJ + j
         return remote(kvo.at[s, j], kvp.at[s, j], skv.at[n], rkv.at[n], at.partner)
 
-    def R(r, j):
+    def rotate(r, j):
         s, n = gather.seqs[r], r * NJ + j
         pr_copy(n).wait_recv()
         cos_t, sin_t = cos_all[j], sin_all[j]
@@ -492,6 +532,10 @@
             kvo[s, j, :, col : col + HEAD_DIM] = turned(hc + col)
         kvo[s, j, :, hc:] = total(2 * hc, hc)
         kv_copy(r, j).start()
+
+    def R(g):
+        for r, j in GROUPS[g]:
+            rotate(r, j)
 
     def o_cols(xx):
         return pl.ds(al((2 * rem(div(xx + 1, 2), 2) + div(xx, 2)) * hc, 128), hc)
@@ -513,60 +557,65 @@
         dst = og.at[n, rows, o_cols(xx)]
         remote(dst, dst, sog.at[kind, n], rog.at[kind, n], at.pa).wait_recv()
 
-    def A(r, j):
+    def attend(r, j, i):
         s, n = gather.seqs[r], r * NJ + j
-        kv_copy(r, j).wait_recv()
         keys = (j + 1) * ch
         iq = lax.broadcasted_iota(jnp.int32, (ch, keys), 0) + j * ch
         ik = lax.broadcasted_iota(jnp.int32, (ch, keys), 1)
         own_ok = iq >= ik
         par_ok = ik < (j + c) * ch
         contract = (((1,), (1,)), ((), ()))
-        first = (2 * ng + kh) * hc
+        cols = pl.ds(al(i * HEAD_DIM, 128), HEAD_DIM)
+        v_cols = pl.ds(al(hc + i * HEAD_DIM, 128), HEAD_DIM)
+        q = qb[n, :, cols]
+        k_own = kvo[s, 0 : j + 1, :, cols].reshape(keys, HEAD_DIM)
+        k_par = kvp[s, 0 : j + 1, :, cols].reshape(keys, HEAD_DIM)
+        s_own = lax.dot_general(q, k_own, contract, preferred_element_type=F32) * HEAD_DIM**-0.5
+        s_par = lax.dot_general(q, k_par, contract, preferred_element_type=F32) * HEAD_DIM**-0.5
+        s_own = jnp.where(own_ok, s_own, -1e30)
+        s_par = jnp.where(par_ok, s_par, -1e30)
+        top = jnp.maximum(jnp.max(s_own, axis=1, keepdims=True), jnp.max(s_par, axis=1, keepdims=True))
+        e_own, e_par = jnp.exp(s_own - top), jnp.exp(s_par - top)
+        inv = 1.0 / (jnp.sum(e_own, axis=1, keepdims=True) + jnp.sum(e_par, axis=1, keepdims=True))
+        v_own = kvo[s, 0 : j + 1, :, v_cols].reshape(keys, HEAD_DIM)
+        v_par = kvp[s, 0 : j + 1, :, v_cols].reshape(keys, HEAD_DIM)
+        out = jnp.dot((e_own * inv).astype(BF16), v_own, preferred_element_type=F32)
+        out += jnp.dot((e_par * inv).astype(BF16), v_par, preferred_element_type=F32)
+        og[n, :, pl.ds(al((2 * ng + kh) * hc + i * HEAD_DIM, 128), HEAD_DIM)] = out.astype(BF16)
+
+    def A(g):
+        for r, j in GROUPS[g]:
+            kv_copy(r, j).wait_recv()
 
         def head(i, carry):
-            cols = pl.ds(al(i * HEAD_DIM, 128), HEAD_DIM)
-            v_cols = pl.ds(al(hc + i * HEAD_DIM, 128), HEAD_DIM)
-            q = qb[n, :, cols]
-            k_own = kvo[s, 0 : j + 1, :, cols].reshape(keys, HEAD_DIM)
-            k_par = kvp[s, 0 : j + 1, :, cols].reshape(keys, HEAD_DIM)
-            s_own = lax.dot_general(q, k_own, contract, preferred_element_type=F32) * HEAD_DIM**-0.5
-            s_par = lax.dot_general(q, k_par, contract, preferred_element_type=F32) * HEAD_DIM**-0.5
-            s_own = jnp.where(own_ok, s_own, -1e30)
-            s_par = jnp.where(par_ok, s_par, -1e30)
-            top = jnp.maximum(jnp.max(s_own, axis=1, keepdims=True), jnp.max(s_par, axis=1, keepdims=True))
-            e_own, e_par = jnp.exp(s_own - top), jnp.exp(s_par - top)
-            inv = 1.0 / (jnp.sum(e_own, axis=1, keepdims=True) + jnp.sum(e_par, axis=1, keepdims=True))
-            v_own = kvo[s, 0 : j + 1, :, v_cols].reshape(keys, HEAD_DIM)
-            v_par = kvp[s, 0 : j + 1, :, v_cols].reshape(keys, HEAD_DIM)
-            out = jnp.dot((e_own * inv).astype(BF16), v_own, preferred_element_type=F32)
-            out += jnp.dot((e_par * inv).astype(BF16), v_par, preferred_element_type=F32)
-            og[n, :, pl.ds(al(first + i * HEAD_DIM, 128), HEAD_DIM)] = out.astype(BF16)
+            for r, j in GROUPS[g]:
+                attend(r, j, i)
             return carry
 
         lax.fori_loop(0, hc // HEAD_DIM, head, 0)
-        og_copy(0, n).start()
-        og_copy(1, n).start()
-
-    def P(r, j):
-        n = r * NJ + j
-        for kind in range(2):
-            og_wait(kind, n)
-            og_copy(kind + 2, n).start()
-
-    def X(r, j):
-        n = r * NJ + j
-        og_wait(2, n)
-        og_wait(3, n)
-
-        def columns(i, carry):
-            cols = pl.ds(al(i * 256, 128), 256)
-            zb[r, j, :, cols] = jnp.dot(og[n], wob[:, cols], preferred_element_type=F32).astype(BF16)
-            return carry
-
-        lax.fori_loop(0, kc // 256, columns, 0)
-        if r == 2:
-            reduce.halves(j)
+        for r, j in GROUPS[g]:
+            og_copy(0, r * NJ + j).start()
+            og_copy(1, r * NJ + j).start()
+
+    def P(g):
+        for r, j in GROUPS[g]:
+            for kind in range(2):
+                og_wait(kind, r * NJ + j)
+                og_copy(kind + 2, r * NJ + j).start()
+
+    def X(g):
+        for r, j in GROUPS[g]:
+            og_wait(2, r * NJ + j)
+            og_wait(3, r * NJ + j)
+
+        def done(col, size, out):
+            for i, (r, j) in enumerate(GROUPS[g]):
+                zb[r, j, :, pl.ds(al(col, 128), size)] = out[i * ch : (i + 1) * ch].astype(BF16)
+
+        product([og.at[r * NJ + j] for r, j in GROUPS[g]], wob, wob.shape[0], kc, done)
+        for r, j in GROUPS[g]:
+            if r == 2:
+                reduce.halves(j)
 
     def T(j):
         attn = reduce.total(j).astype(BF16)
@@ -637,7 +686,7 @@
 
 def mlp_kernel(
     units, h_ref, w_hbm, wdn, y_ref,
-    xg, wt, raw, wd, wr, ag, ar, act, acc, zb, ya, yb, yfd, yfu, yst,
+    xg, wt, raw, wd, ag, ar, act, s1, s2, zb, ya, yb, yfd, yfu, yst,
     sx, rx, sy, ry, syh, ryh, sa, ra, syr, ryr, sd, rd, lw, lwd, swd, rwd,
 ):
     at = Place()
@@ -649,7 +698,7 @@
     fm = (tiles - 1) * 128
     fr = fc - fm
     blocks, slots = 2 * tiles, raw.shape[0]
-    gather = Spread(at, h_ref, xg, units, sx, rx, sy, ry, syh, ryh)
+    gather = Spread(at, h_ref, xg, units, (s1, s2), sx, rx, sy, ry, syh, ryh)
     reduce = Reduce(at, zb, ya, yb, yfd, yfu, syr, ryr)
 
     def w_in(q):
@@ -676,7 +725,7 @@
     def d_refs(q, core):
         cols = pl.ds(al(core * kd, 128), kd)
         main, rest = wdn.at[pl.ds(q * fc, fm)], wdn.at[pl.ds(q * fc + fm, fr)]
-        return (main, wd.at[pl.ds(q * fm, fm), cols]), (rest, wr.at[pl.ds(q * 128, fr), cols])
+        return (main, wd.at[pl.ds(q * fm, fm), cols]), (rest, wd.at[pl.ds(NX * fm + q * 128, fr), cols])
 
     def d_own(q, k):
         src, dst = d_refs(q, c)[k]
@@ -692,7 +741,7 @@
     for q, k in quarters:
         d_own(q, k).start()
     for q in range(NX):
-        wr[q * 128 + fr : (q + 1) * 128, :] = jnp.zeros((128 - fr, kc), BF16)
+        wd[NX * fm + q * 128 + fr : NX * fm + (q + 1) * 128, :] = jnp.zeros((128 - fr, kc), BF16)
     at.barrier()
     for q, k in quarters:
         d_pair(q, k, c).start()
@@ -716,63 +765,50 @@
         for copy in a_copies(kind, n):
             copy.start()
 
-    def G(r, j):
-        gather.chunk_wait(r, j)
-        s, n = gather.seqs[r], r * NJ + j
-
-        def columns(i, carry):
-            acc[...] = jnp.zeros_like(acc)
-            cols = pl.ds(al(i * 256, 128), 256)
-
-            def depth(k, carry):
-                part = pl.ds(al(k * (width // 2), 128), width // 2)
-                acc[...] += jnp.dot(xg[s, j, :, part], wt[part, cols], preferred_element_type=F32)
-                return carry
-
-            lax.fori_loop(0, 2, depth, 0)
-            out = acc[...]
-            g, u = out[:, :128].astype(BF16).astype(F32), out[:, 128:].astype(BF16).astype(F32)
-            act[:, pl.ds(al(i * 128, 128), 128)] = (g / (1.0 + jnp.exp(-g)) * u).astype(BF16)
-            return carry
-
-        lax.fori_loop(0, tiles, columns, 0)
-        ag[n, :, pl.ds(al(x * fm, 128), fm)] = act[:, :fm]
-        below = pltpu.roll(act[h:, fm:].astype(F32), 64, axis=1)
-        ar[n, :, pl.ds(al(x * 128, 128), 128)] = (act[:h, fm:].astype(F32) + below).astype(BF16)
-        for kind in range(2):
-            a_start(kind, n)
-
-    def P(r, j):
-        n = r * NJ + j
-        for kind in range(2):
-            a_wait(kind, n)
-            a_start(kind + 2, n)
-
-    def X(r, j):
-        n = r * NJ + j
-        for kind in (2, 3):
-            a_wait(kind, n)
-        for q in range(NX):
-            cols = pl.ds(q * 128, 128)
-            act[0:h, cols] = ar[n, :, cols]
-            act[h:, cols] = pltpu.roll(ar[n, :, cols].astype(F32), 64, axis=1).astype(BF16)
-
-        def columns(i, carry):
-            cols = pl.ds(al(i * 256, 128), 256)
-            acc[...] = jnp.dot(act[:, : NX * 128], wr[:, cols], preferred_element_type=F32)
-
-            def depth(k, carry):
-                part = pl.ds(al(k * 2 * fm, 128), 2 * fm)
-                acc[...] += jnp.dot(ag[n, :, part], wd[part, cols], preferred_element_type=F32)
-                return carry
-
-            lax.fori_loop(0, 2, depth, 0)
-            zb[r, j, :, cols] = acc[...].astype(BF16)
-            return carry
-
-        lax.fori_loop(0, kc // 256, columns, 0)
-        if r == 2:
-            reduce.halves(j)
+    def G(g):
+        for r, j in GROUPS[g]:
+            gather.chunk_wait(r, j)
+
+        def done(col, size, out):
+            for k in range(0, size, 256):
+                gate, up = out[:, k : k + 128].astype(BF16).astype(F32), out[:, k + 128 : k + 256].astype(BF16).astype(F32)
+                value = (gate / (1.0 + jnp.exp(-gate)) * up).astype(BF16)
+                act[0 : value.shape[0], pl.ds(al(div(col + k, 2), 128), 128)] = value
+
+        product([xg.at[gather.seqs[r], j] for r, j in GROUPS[g]], wt, width, wt.shape[1], done)
+        for i, (r, j) in enumerate(GROUPS[g]):
+            n, lo = r * NJ + j, i * ch
+            ag[n, :, pl.ds(al(x * fm, 128), fm)] = act[lo : lo + ch, :fm]
+            below = pltpu.roll(act[lo + h : lo + ch, fm:].astype(F32), 64, axis=1)
+            ar[n, :, pl.ds(al(x * 128, 128), 128)] = (act[lo : lo + h, fm:].astype(F32) + below).astype(BF16)
+            for kind in range(2):
+                a_start(kind, n)
+
+    def P(g):
+        for r, j in GROUPS[g]:
+            for kind in range(2):
+                a_wait(kind, r * NJ + j)
+                a_start(kind + 2, r * NJ + j)
+
+    def X(g):
+        for r, j in GROUPS[g]:
+            n = r * NJ + j
+            for kind in (2, 3):
+                a_wait(kind, n)
+            for q in range(NX):
+                cols = pl.ds(NX * fm + q * 128, 128)
+                rest = ar[n, :, q * 128 : (q + 1) * 128]
+                ag[n, 0:h, cols] = rest
+                ag[n, h:, cols] = pltpu.roll(rest.astype(F32), 64, axis=1).astype(BF16)
+
+        def done(col, size, out):
+            for i, (r, j) in enumerate(GROUPS[g]):
+                zb[r, j, :, pl.ds(al(col, 128), size)] = out[i * ch : (i + 1) * ch].astype(BF16)
+
+        product([ag.at[r * NJ + j] for r, j in GROUPS[g]], wd, wd.shape[0], kc, done, wide=False)
+        for r, j in GROUPS[g]:
+            if r == 2:
+                reduce.halves(j)
 
     def y_rows(j, core):
         return pl.ds(al((2 * j + core) * ch, 8), ch)
@@ -866,7 +902,7 @@
             out_specs=(vmem_spec, any_spec),
             scratch_shapes=[
                 vmem(NJ, ch, kc), vmem(NX, NJ, ch, 2 * kc), vmem(NJ, ch, HEAD_DIM, dtype=F32), vmem(NJ, ch, HEAD_DIM, dtype=F32),
-                vmem(NJ, ch // 4, 128, dtype=F32), vmem(NJ, ch // 4, 128, dtype=F32),
+                vmem(NJ, ch // 4, 128, dtype=F32), vmem(NJ, ch // 4, 128, dtype=F32), vmem(ch, 128, dtype=F32), vmem(ch, 128, dtype=F32),
                 vmem(2 * kc, 6 * hc), vmem(row_heads, kc), vmem(NCH, ch, 6 * hc), vmem(NCH, ch, 3 * hc), vmem(NCH, ch, hc),
                 vmem(NX, NJ, ch, 2 * hc), vmem(NX, NJ, ch, 2 * hc), vmem(NCH, ch, row_heads), *reduce_scratch,
                 vmem(2, fc, kd), vmem(2, f_a, kd), vmem(2, fc - f_a, kd),
@@ -879,7 +915,7 @@
             name="attention_part",
         )(x_blk[0], turn, base, w_q, w_k, w_v, w_o, w_gate.T, w_up.T)
 
-        first = ch * 3 // 4
+        first = ch * 3 // 4 // 32 * 32
         units = ((0, 0, first, 1), (0, first, ch - first, 0), (1, 0, h, 0), (1, h, h, 0)) + tuple((j, 0, ch, 0) for j in range(2, NJ))
         n_u, n_x = len(units), len(units) + 3
         y_blk = pl.pallas_call(
@@ -889,9 +925,8 @@
             out_specs=vmem_spec,
             scratch_shapes=[
                 vmem(NX, NJ, ch, width), vmem(width, tiles * 256), vmem(3, 128, width),
-                vmem(NX * (tiles - 1) * 128, kc), vmem(NX * 128, kc), vmem(NCH, ch, NX * (tiles - 1) * 128), vmem(NCH, h, NX * 128),
-                vmem(ch, tiles * 128),
-                vmem(ch, 256, dtype=F32),
+                vmem(NX * tiles * 128, kc), vmem(NCH, ch, NX * tiles * 128), vmem(NCH, h, NX * 128), vmem(2 * ch, tiles * 128),
+                vmem(ch, 128, dtype=F32), vmem(ch, 128, dtype=F32),
                 *reduce_scratch, vmem(2, NJ, ch, kd),
                 sems(4, n_x), sems(4, n_x), sems(2, n_u), sems(2, n_u), sems(2, n_u), sems(2, n_u),
                 sems(4, NCH, 2), sems(4, NCH, 2), sems(4, NJ), sems(4, NJ), sems(NJ), sems(NJ),

time: 371 us -> 344 us (0.927)
  Pallas kernels: 368 us -> 342 us
    pallas_call x1, Pallas kernels: 191 us -> 165 us  [layer(): pl.pallas_call(functools.partial(mlp_kernel, units), out_shape=jax.ShapeD...]
where the time goes in v7:
time: 344 us
  Pallas kernels  342 us (99%)
    pallas_call x1, Pallas kernels, layer(): pl.pallas_call(functools.partial(attention_kernel, units), out_shape=(jax...  177 us
    pallas_call x1, Pallas kernels, layer(): pl.pallas_call(functools.partial(mlp_kernel, units), out_shape=jax.ShapeD...  165 us

profile of v7, /device:TPU:97, one launch (start us, length us, event | category | flops | bytes accessed | tf_op | source)
XLA Modules:
  0.0 344.1 jit_solution(18106306442531885493)
XLA Ops:
  0.0 176.6 %attention_part.1 = (bf16[4,128,1024]{2,1,0:T(8,128)(2,1)}, bf16[2,688,4096]{2,1,0:T(8,128)(2,1)}) custom-call(bf16[1024,512]{1,0:T(8,128)(2,1)} %bitcast.7, f32[2,128,128]{2,1,0:T(8,128)} %constant.4.clone.turn_ref, f32[2,8,128]{2,1,0:T(8,128)} %constant.5.clone.base_ref, bf16[512,1024]{1,0:T(8,128)(2,1)} %wq.1, bf16[512,1024]{1,0:T(8,128)(2,1)} %wk.1, ...), custom_call_target="tpu_custom_call" | custom-call | tf_op jit(solution)/shard_map/attention_part/pallas_call | solution.py:898
  176.6 165.2 %mlp_part.1 = bf16[1024,512]{1,0:T(8,128)(2,1)} custom-call(bf16[4,128,1024]{2,1,0:T(8,128)(2,1)} %get-tuple-element.7.h_ref, bf16[2,688,4096]{2,1,0:T(8,128)(2,1)} %get-tuple-element.8.w_hbm, bf16[2752,512]{1,0:T(8,128)(2,1)} %wdn.1), custom_call_target="tpu_custom_call" | custom-call | tf_op jit(solution)/shard_map/mlp_part/pallas_call | solution.py:921
  341.8 2.3 copy.12

commit v8 on v7

--- a/solution.py
+++ b/solution.py
@@ -18,7 +18,7 @@
 NJ = 4
 NCH = 16
 VMEM_LIMIT = 67_043_328
-GROUPS = (((0, 0), (0, 1)), ((0, 2), (0, 3)), *(((3, j), (1, j)) for j in range(NJ)), *(((2, j),) for j in range(NJ)))
+GROUPS = (*(((0, j),) for j in range(NJ)), *(((3, j), (1, j)) for j in range(NJ)), *(((2, j),) for j in range(NJ)))
 
 
 def rem(a, b):
@@ -38,26 +38,27 @@
 
 
 ATTENTION_STEPS = (
-    ("XP", 2), ("XP", 0), ("S", "b", 0, 0), ("XE", 3), ("XP", 1), ("WA", 0), ("S", "b", 0, 1), ("ST", 3), ("O", "b", 1),
-    ("N", 3), ("O", "b", 0), ("XP", 3), ("WA", 1), ("XE", 0), ("WOP",), ("S", "b", 1, 0), ("WP", 0), ("XE", 1), ("XE", 2),
-    ("YH", 3), ("S", "b", 1, 1), ("WP", 1), ("O", "a", 1), ("S", "a", 1, 0), ("ST", 0), ("G", 8), ("ST", 1), ("N", 0),
-    ("G", 4), ("N", 1), ("YH", 0), ("ST", 2), ("XE", 4), ("F", "a", 0), ("F", "b", 1), ("O", "a", 0), ("YH", 1), ("F", "a", 1),
-    ("N", 2), ("G", 2), ("ST", 4), ("G", 6), ("YH", 2), ("G", 3), ("S", "a", 1, 1), ("N", 4), ("G", 7), ("R", 6), ("R", 2),
-    ("G", 1), ("R", 3), ("R", 7), ("YH", 4), ("R", 8), ("A", 2), ("A", 6), ("A", 7), ("A", 8), ("R", 4), ("G", 9),
-    ("S", "a", 0, 1), ("P", 2), ("R", 1), ("G", 5), ("P", 8), ("P", 6), ("DP", 1), ("P", 7), ("A", 3), ("A", 4), ("R", 9),
-    ("A", 9), ("G", 0), ("X", 8), ("R", 5), ("X", 6), ("P", 3), ("X", 7), ("A", 5), ("P", 9), ("P", 4), ("X", 2),
-    ("S", "a", 0, 0), ("M", 0), ("F", "b", 0), ("X", 3), ("M", 1), ("P", 5), ("R", 0), ("X", 9), ("X", 4), ("M", 2), ("A", 0),
-    ("A", 1), ("X", 5), ("M", 3), ("DP", 0), ("P", 0), ("P", 1), ("X", 0), ("T", 1), ("T", 0), ("X", 1), ("T", 2), ("T", 3),
+    ("WA", 0), ("S", "b", 0, 0), ("XP", 0), ("O", "b", 1), ("XE", 0), ("O", "b", 0), ("XE", 1), ("WA", 1), ("XP", 2),
+    ("ST", 0), ("ST", 1), ("XP", 1), ("S", "b", 1, 0), ("XP", 3), ("XE", 2), ("S", "b", 0, 1), ("S", "b", 1, 1), ("N", 0),
+    ("XE", 3), ("N", 1), ("WOP",), ("WP", 1), ("O", "a", 0), ("WP", 0), ("YH", 0), ("YH", 1), ("ST", 2), ("G", 0), ("N", 2),
+    ("G", 8), ("ST", 3), ("F", "a", 1), ("G", 4), ("R", 0), ("R", 8), ("A", 8), ("A", 0), ("YH", 2), ("G", 1), ("XE", 4),
+    ("N", 3), ("R", 4), ("A", 4), ("P", 8), ("P", 0), ("G", 9), ("G", 2), ("P", 4), ("ST", 4), ("O", "a", 1), ("X", 8),
+    ("G", 5), ("YH", 3), ("R", 9), ("X", 0), ("A", 9), ("X", 4), ("M", 0), ("S", "a", 0, 1), ("N", 4), ("G", 10), ("P", 9),
+    ("T", 0), ("HF", 0), ("R", 1), ("R", 5), ("A", 5), ("X", 9), ("R", 10), ("HH", 0), ("A", 1), ("YH", 4), ("G", 6),
+    ("F", "a", 0), ("P", 5), ("HN", 0), ("A", 10), ("G", 11), ("S", "a", 0, 0), ("R", 2), ("G", 7), ("R", 6), ("P", 10),
+    ("A", 6), ("X", 5), ("R", 11), ("S", "a", 1, 0), ("M", 1), ("G", 3), ("A", 11), ("R", 7), ("A", 2), ("X", 10), ("A", 7),
+    ("HY", 0), ("R", 3), ("P", 11), ("P", 6), ("F", "b", 0), ("P", 7), ("F", "b", 1), ("X", 11), ("S", "a", 1, 1), ("X", 6),
+    ("M", 2), ("A", 3), ("DP", 0), ("P", 1), ("X", 7), ("P", 2), ("M", 3), ("DP", 1), ("P", 3), ("HO", 0), ("X", 1), ("X", 2),
+    ("T", 1), ("T", 2), ("X", 3), ("T", 3),
 )
 MLP_STEPS = (
-    ("YR", 0), ("XF", 0, 1), ("XF", 0, 3), ("WT", 0), ("XH", 0, 1), ("XF", 0, 2), ("YRH", 0), ("XH", 0, 3), ("XF", 0, 5),
-    ("N", 0, 1), ("N", 0, 3), ("XH", 0, 2), ("XF", 0, 4), ("N", 0, 2), ("XF", 2, 0), ("XF", 3, 0), ("XF", 0, 0), ("XH", 3, 0),
-    ("XH", 2, 0), ("XH", 0, 4), ("WT", 1), ("YH", 1), ("XF", 1, 0), ("WT", 2), ("WT", 3), ("XH", 0, 5), ("YH", 3), ("YH", 2),
-    ("G", 3), ("N", 3, 0), ("N", 0, 4), ("XH", 0, 0), ("N", 0, 5), ("G", 7), ("N", 2, 0), ("G", 6), ("N", 0, 0), ("XH", 1, 0),
-    ("P", 3), ("G", 0), ("G", 1), ("P", 7), ("N", 1, 0), ("X", 3), ("G", 2), ("P", 6), ("YH", 4), ("G", 4), ("YH", 5),
-    ("X", 7), ("G", 5), ("X", 6), ("G", 8), ("P", 2), ("P", 8), ("G", 9), ("M", 1), ("P", 4), ("X", 8), ("X", 2), ("P", 9),
-    ("M", 0), ("P", 5), ("P", 0), ("P", 1), ("X", 9), ("X", 4), ("M", 2), ("X", 5), ("M", 3), ("X", 0), ("T", 0), ("X", 1),
-    ("T", 1), ("T", 2), ("T", 3),
+    ("XF", 0, 1), ("YR", 0), ("WT", 0), ("XF", 0, 0), ("XH", 0, 1), ("XF", 0, 3), ("YRH", 0), ("XF", 2, 0), ("N", 0, 1),
+    ("WT", 1), ("WT", 2), ("XH", 0, 3), ("XF", 0, 2), ("WT", 3), ("XF", 1, 0), ("XF", 3, 0), ("N", 0, 3), ("G", 8), ("YH", 1),
+    ("XH", 2, 0), ("G", 4), ("P", 8), ("XH", 3, 0), ("XH", 0, 0), ("XH", 0, 2), ("G", 3), ("XH", 1, 0), ("YH", 3), ("G", 7),
+    ("N", 2, 0), ("N", 0, 0), ("G", 9), ("N", 0, 2), ("P", 7), ("G", 11), ("P", 4), ("P", 9), ("N", 1, 0), ("N", 3, 0),
+    ("G", 5), ("X", 8), ("G", 1), ("X", 4), ("YH", 2), ("P", 11), ("G", 6), ("X", 9), ("X", 7), ("X", 11), ("P", 5), ("M", 0),
+    ("G", 10), ("G", 0), ("M", 3), ("X", 5), ("P", 10), ("P", 3), ("M", 1), ("P", 6), ("G", 2), ("P", 1), ("X", 10), ("X", 3),
+    ("P", 0), ("X", 6), ("M", 2), ("T", 3), ("P", 2), ("X", 1), ("T", 1), ("X", 0), ("T", 0), ("X", 2), ("T", 2),
 )
 
 
@@ -96,7 +97,7 @@
         return pl.ds(al(x * self.kc, 128), self.kc)
 
     def keep_own(self):
-        for j in range(NJ):
+        for j in {unit[0]: 0 for unit in self.units}:
             self.xg[self.at.y, j, :, self.cols(self.at.x)] = self.src[j]
 
     def xcopy(self, kind, r, u):
@@ -211,8 +212,8 @@
     return refs[0][...] if len(refs) == 1 else jnp.concatenate([ref[...] for ref in refs], axis=0)
 
 
-def product(refs, weight, depth, n_cols, done, wide=True):
-    step = 512 if wide and len(refs) == 1 and n_cols % 512 == 0 else 256
+def product(refs, weight, depth, n_cols, done):
+    step = 256
 
     def columns(i, carry):
         out = jnp.dot(rows_of(refs), weight[0:depth, pl.ds(al(i * step, 128), step)], preferred_element_type=F32)
@@ -307,10 +308,10 @@
 
 def attention_kernel(
     units, x_ref, turn_ref, base_ref, wq, wk, wv, wo, wg_t, wu_t,
-    h_ref, w_all,
-    xc, xg, cos_all, sin_all, st_own, st_in, s1, s2, wb, wob, part, precv, qb, kvo, kvp, og, zb, ya, yb, yfd, yfu, own, drel_a, drel_b,
+    h_ref, w_all, hg_all,
+    xc, xg, hg, cos_all, sin_all, st_own, st_in, s1, s2, wb, wob, part, precv, qb, kvo, kvp, og, zb, ya, yb, yfd, yfu, own, drel_a, drel_b,
     sxe, rxe, sst, rst, sy, ry, syh, ryh, sd, rd, swa, rwa, swo, rwo, swp, rwp, lw, so, ro, spr, rpr, skv, rkv, sog, rog, syr, ryr,
-    lg, sds, rds, sdo, rdo, sdf, rdf, sdp, rdp,
+    lg, sds, rds, sdo, rdo, sdf, rdf, sdp, rdp, shx, rhx, shy, rhy, shz, rhz, lh,
 ):
     at = Place()
     x, c, y = at.x, at.c, at.y
@@ -323,6 +324,7 @@
     ng = rem(div(x + 1, 2), 2)
     gather = Spread(at, xc, xg, units, (s1, s2), None, None, sy, ry, syh, ryh)
     reduce = Reduce(at, zb, ya, yb, yfd, yfu, syr, ryr)
+    ahead = Spread(at, h_ref, hg, ((0, 0, ch, 0),), (s1, s2), shx, rhx, shy, rhy, shz, rhz)
     weights = (wq, wk, wv)
 
     def half_cols(core):
@@ -621,6 +623,23 @@
         attn = reduce.total(j).astype(BF16)
         h_ref[j] = (xc[j].astype(F32) + attn.astype(F32)).astype(BF16)
 
+    def h_out(r):
+        return pltpu.make_async_copy(hg.at[ahead.seqs[r], 0], hg_all.at[ahead.seqs[r]], lh.at[r])
+
+    def HF(u):
+        ahead.keep_own()
+        ahead.XF(0, u)
+
+    def HY(u):
+        ahead.YH(u)
+        for r in (0, 1, 3):
+            h_out(r).start()
+
+    def HO(u):
+        for d in range(2):
+            ahead.yhalf_wait(d, u)
+        h_out(2).start()
+
     for half, i in pieces:
         w_local(half, i).start()
     o_local.start()
@@ -641,6 +660,7 @@
     ops = {
         "XP": XP, "WOP": WOP, "XE": XE, "ST": ST, "N": N, "YH": gather.YH, "WA": WA, "WP": WP, "S": S, "O": O, "F": F, "DP": DP,
         "G": G, "R": R, "A": A, "P": P, "X": X, "M": reduce.middle, "T": T,
+        "HF": HF, "HH": lambda u: ahead.XH(0, u), "HN": lambda u: ahead.N(0, u), "HY": HY, "HO": HO,
     }
     waits = {"G": w_ready, "X": o_ready, "WP": angles}
     for step in ATTENTION_STEPS:
@@ -667,6 +687,9 @@
             gather.ycopy(d, u).wait_send()
             gather.yhalf(d, u).wait_send()
     reduce.drain()
+    ahead.drain()
+    for r in range(NX):
+        h_out(r).wait()
     o_pair.wait_send()
     for half, i in pieces:
         wa_copy(half, i, x).wait_send()
@@ -685,9 +708,9 @@
 
 
 def mlp_kernel(
-    units, h_ref, w_hbm, wdn, y_ref,
+    units, h_ref, w_hbm, wdn, hg_hbm, y_ref,
     xg, wt, raw, wd, ag, ar, act, s1, s2, zb, ya, yb, yfd, yfu, yst,
-    sx, rx, sy, ry, syh, ryh, sa, ra, syr, ryr, sd, rd, lw, lwd, swd, rwd,
+    sx, rx, sy, ry, syh, ryh, sa, ra, syr, ryr, sd, rd, lw, lwd, swd, rwd, lh,
 ):
     at = Place()
     x, c, y = at.x, at.c, at.y
@@ -738,6 +761,11 @@
     quarters = [(q, k) for q in range(NX) for k in range(2)]
     for q in range(slots):
         w_in(q).start()
+    def h_in(s):
+        return pltpu.make_async_copy(hg_hbm.at[s], xg.at[s, 0], lh.at[s])
+
+    for s in range(NX):
+        h_in(s).start()
     for q, k in quarters:
         d_own(q, k).start()
     for q in range(NX):
@@ -805,7 +833,7 @@
             for i, (r, j) in enumerate(GROUPS[g]):
                 zb[r, j, :, pl.ds(al(col, 128), size)] = out[i * ch : (i + 1) * ch].astype(BF16)
 
-        product([ag.at[r * NJ + j] for r, j in GROUPS[g]], wd, wd.shape[0], kc, done, wide=False)
+        product([ag.at[r * NJ + j] for r, j in GROUPS[g]], wd, wd.shape[0], kc, done)
         for r, j in GROUPS[g]:
             if r == 2:
                 reduce.halves(j)
@@ -833,6 +861,7 @@
         ops[name] = getattr(gather, name)
     waits = {
         "N": gather.keep_own,
+        "G": lambda: [h_in(s).wait() for s in range(NX)],
         "X": lambda: [(d_own(q, k).wait(), d_pair(q, k, 1 - c).wait_recv()) for q, k in quarters],
     }
     for step in MLP_STEPS:
@@ -895,13 +924,17 @@
         reduce_scratch = [vmem(NX, NJ, ch, kc), vmem(NJ, h, kc), vmem(NJ, ch - h, kc), vmem(NJ, ch, kc), vmem(NJ, ch, kc)]
         units = ((0, 0, h, 0), (0, h, h, 0)) + tuple((j, 0, ch, 0) for j in range(1, NJ))
         n_u = len(units)
-        h_blk, w_all = pl.pallas_call(
+        h_blk, w_all, hg_all = pl.pallas_call(
             functools.partial(attention_kernel, units),
-            out_shape=(jax.ShapeDtypeStruct((NJ, ch, kc), BF16), jax.ShapeDtypeStruct((2, fc, width), BF16)),
+            out_shape=(
+                jax.ShapeDtypeStruct((NJ, ch, kc), BF16),
+                jax.ShapeDtypeStruct((2, fc, width), BF16),
+                jax.ShapeDtypeStruct((NX, ch, width), BF16),
+            ),
             in_specs=[vmem_spec] * 3 + [any_spec] * 6,
-            out_specs=(vmem_spec, any_spec),
+            out_specs=(vmem_spec, any_spec, any_spec),
             scratch_shapes=[
-                vmem(NJ, ch, kc), vmem(NX, NJ, ch, 2 * kc), vmem(NJ, ch, HEAD_DIM, dtype=F32), vmem(NJ, ch, HEAD_DIM, dtype=F32),
+                vmem(NJ, ch, kc), vmem(NX, NJ, ch, 2 * kc), vmem(NX, 1, ch, width), vmem(NJ, ch, HEAD_DIM, dtype=F32), vmem(NJ, ch, HEAD_DIM, dtype=F32),
                 vmem(NJ, ch // 4, 128, dtype=F32), vmem(NJ, ch // 4, 128, dtype=F32), vmem(ch, 128, dtype=F32), vmem(ch, 128, dtype=F32),
                 vmem(2 * kc, 6 * hc), vmem(row_heads, kc), vmem(NCH, ch, 6 * hc), vmem(NCH, ch, 3 * hc), vmem(NCH, ch, hc),
                 vmem(NX, NJ, ch, 2 * hc), vmem(NX, NJ, ch, 2 * hc), vmem(NCH, ch, row_heads), *reduce_scratch,
@@ -910,18 +943,18 @@
                 sems(NJ), sems(NJ), sems(2, 3), sems(2, 3), sems(2, 3), sems(2, 3), sems(2), sems(2), sems(3, 3), sems(1), sems(1),
                 sems(NCH), sems(NCH), sems(NCH), sems(NCH), sems(4, NCH), sems(4, NCH), sems(4, NJ), sems(4, NJ),
                 sems(2, 2), sems(2, 2, 2), sems(2, 2, 2), sems(2, 2), sems(2, 2), sems(2, 2), sems(2, 2), sems(2, 4), sems(2, 4),
+                sems(4, 1), sems(4, 1), sems(2, 1), sems(2, 1), sems(2, 1), sems(2, 1), sems(NX),
             ],
             compiler_params=pltpu.CompilerParams(collective_id=0, has_side_effects=True, vmem_limit_bytes=VMEM_LIMIT),
             name="attention_part",
         )(x_blk[0], turn, base, w_q, w_k, w_v, w_o, w_gate.T, w_up.T)
 
-        first = ch * 3 // 4 // 32 * 32
-        units = ((0, 0, first, 1), (0, first, ch - first, 0), (1, 0, h, 0), (1, h, h, 0)) + tuple((j, 0, ch, 0) for j in range(2, NJ))
+        units = ((1, 0, h, 1), (1, h, h, 0)) + tuple((j, 0, ch, 0) for j in range(2, NJ))
         n_u, n_x = len(units), len(units) + 3
         y_blk = pl.pallas_call(
             functools.partial(mlp_kernel, units),
             out_shape=jax.ShapeDtypeStruct((seq, kd), BF16),
-            in_specs=[vmem_spec, any_spec, any_spec],
+            in_specs=[vmem_spec, any_spec, any_spec, any_spec],
             out_specs=vmem_spec,
             scratch_shapes=[
                 vmem(NX, NJ, ch, width), vmem(width, tiles * 256), vmem(3, 128, width),
@@ -930,11 +963,11 @@
                 *reduce_scratch, vmem(2, NJ, ch, kd),
                 sems(4, n_x), sems(4, n_x), sems(2, n_u), sems(2, n_u), sems(2, n_u), sems(2, n_u),
                 sems(4, NCH, 2), sems(4, NCH, 2), sems(4, NJ), sems(4, NJ), sems(NJ), sems(NJ),
-                sems(2 * tiles), sems(NX, 2), sems(NX, 2), sems(NX, 2),
+                sems(2 * tiles), sems(NX, 2), sems(NX, 2), sems(NX, 2), sems(NX),
             ],
             compiler_params=pltpu.CompilerParams(collective_id=1, has_side_effects=True, vmem_limit_bytes=VMEM_LIMIT),
             name="mlp_part",
-        )(h_blk, w_all, w_down)
+        )(h_blk, w_all, w_down, hg_all)
         return y_blk[None]
 
     return jax.shard_map(

time: 344 us -> 334 us (0.971)
  Pallas kernels: 342 us -> 332 us
    pallas_call x1, Pallas kernels: 165 us -> 147 us  [layer(): pl.pallas_call(functools.partial(mlp_kernel, units), out_shape=jax.ShapeD...]
    pallas_call x1, Pallas kernels: 177 us -> 185 us  [layer(): pl.pallas_call(functools.partial(attention_kernel, units), out_shape=(jax...]
where the time goes in v8:
time: 334 us
  Pallas kernels  332 us (99%)
    pallas_call x1, Pallas kernels, layer(): pl.pallas_call(functools.partial(attention_kernel, units), out_shape=(jax...  185 us
    pallas_call x1, Pallas kernels, layer(): pl.pallas_call(functools.partial(mlp_kernel, units), out_shape=jax.ShapeD...  147 us

profile of v8, /device:TPU:97, one launch (start us, length us, event | category | flops | bytes accessed | tf_op | source)
XLA Modules:
  0.0 333.9 jit_solution(4667295820135332300)
XLA Ops:
  0.0 184.8 %attention_part.1 = (bf16[4,128,1024]{2,1,0:T(8,128)(2,1)}, bf16[2,688,4096]{2,1,0:T(8,128)(2,1)}, bf16[4,128,4096]{2,1,0:T(8,128)(2,1)}) custom-call(bf16[1024,512]{1,0:T(8,128)(2,1)} %bitcast.7, f32[2,128,128]{2,1,0:T(8,128)} %constant.4.clone.turn_ref, f32[2,8,128]{2,1,0:T(8,128)} %constant.5.clone.base_ref, bf16[512,1024]{1,0:T(8,128)(2,1)} %wq.1, ...), custom_call_target="tpu_custom_call" | custom-call | tf_op jit(solution)/shard_map/attention_part/pallas_call | solution.py:927
  184.8 146.9 %mlp_part.1 = bf16[1024,512]{1,0:T(8,128)(2,1)} custom-call(bf16[4,128,1024]{2,1,0:T(8,128)(2,1)} %get-tuple-element.8.h_ref, bf16[2,688,4096]{2,1,0:T(8,128)(2,1)} %get-tuple-element.9.w_hbm, bf16[2752,512]{1,0:T(8,128)(2,1)} %wdn.1, bf16[4,128,4096]{2,1,0:T(8,128)(2,1)} %get-tuple-element.10.hg_hbm), custom_call_target="tpu_custom_call" | custom-call | tf_op jit(solution)/shard_map/mlp_part/pallas_call | solution.py:954
  331.7 2.3 copy.12

commit v9 on v8

--- a/solution.py
+++ b/solution.py
@@ -38,18 +38,18 @@
 
 
 ATTENTION_STEPS = (
-    ("WA", 0), ("S", "b", 0, 0), ("XP", 0), ("O", "b", 1), ("XE", 0), ("O", "b", 0), ("XE", 1), ("WA", 1), ("XP", 2),
-    ("ST", 0), ("ST", 1), ("XP", 1), ("S", "b", 1, 0), ("XP", 3), ("XE", 2), ("S", "b", 0, 1), ("S", "b", 1, 1), ("N", 0),
-    ("XE", 3), ("N", 1), ("WOP",), ("WP", 1), ("O", "a", 0), ("WP", 0), ("YH", 0), ("YH", 1), ("ST", 2), ("G", 0), ("N", 2),
-    ("G", 8), ("ST", 3), ("F", "a", 1), ("G", 4), ("R", 0), ("R", 8), ("A", 8), ("A", 0), ("YH", 2), ("G", 1), ("XE", 4),
-    ("N", 3), ("R", 4), ("A", 4), ("P", 8), ("P", 0), ("G", 9), ("G", 2), ("P", 4), ("ST", 4), ("O", "a", 1), ("X", 8),
-    ("G", 5), ("YH", 3), ("R", 9), ("X", 0), ("A", 9), ("X", 4), ("M", 0), ("S", "a", 0, 1), ("N", 4), ("G", 10), ("P", 9),
-    ("T", 0), ("HF", 0), ("R", 1), ("R", 5), ("A", 5), ("X", 9), ("R", 10), ("HH", 0), ("A", 1), ("YH", 4), ("G", 6),
-    ("F", "a", 0), ("P", 5), ("HN", 0), ("A", 10), ("G", 11), ("S", "a", 0, 0), ("R", 2), ("G", 7), ("R", 6), ("P", 10),
-    ("A", 6), ("X", 5), ("R", 11), ("S", "a", 1, 0), ("M", 1), ("G", 3), ("A", 11), ("R", 7), ("A", 2), ("X", 10), ("A", 7),
-    ("HY", 0), ("R", 3), ("P", 11), ("P", 6), ("F", "b", 0), ("P", 7), ("F", "b", 1), ("X", 11), ("S", "a", 1, 1), ("X", 6),
-    ("M", 2), ("A", 3), ("DP", 0), ("P", 1), ("X", 7), ("P", 2), ("M", 3), ("DP", 1), ("P", 3), ("HO", 0), ("X", 1), ("X", 2),
-    ("T", 1), ("T", 2), ("X", 3), ("T", 3),
+    ("S", "b", 0, 0), ("WA", 0), ("XP", 3), ("XP", 0), ("WOP",), ("XE", 1), ("XE", 0), ("O", "b", 0), ("XP", 1), ("XE", 2),
+    ("XP", 2), ("WA", 1), ("S", "b", 1, 0), ("ST", 1), ("S", "b", 0, 1), ("ST", 0), ("XE", 3), ("O", "b", 1), ("N", 1),
+    ("WP", 0), ("ST", 2), ("N", 0), ("S", "b", 1, 1), ("YH", 1), ("YH", 0), ("G", 0), ("N", 2), ("S", "a", 1, 0), ("WP", 1),
+    ("G", 8), ("G", 4), ("Q", 8), ("ST", 3), ("Q", 0), ("R", 8), ("A", 8), ("O", "a", 1), ("R", 0), ("YH", 2), ("G", 5),
+    ("N", 3), ("R", 4), ("P", 8), ("A", 4), ("G", 9), ("XE", 4), ("A", 0), ("R", 5), ("X", 8), ("P", 4), ("A", 5), ("YH", 3),
+    ("G", 1), ("R", 9), ("P", 0), ("ST", 4), ("A", 9), ("F", "a", 1), ("X", 4), ("M", 0), ("G", 2), ("G", 10), ("N", 4),
+    ("P", 5), ("X", 0), ("P", 9), ("T", 0), ("R", 2), ("HF", 0), ("G", 3), ("X", 9), ("O", "a", 0), ("X", 5), ("YH", 4),
+    ("HH", 0), ("G", 6), ("M", 1), ("S", "a", 1, 1), ("R", 10), ("A", 10), ("F", "a", 0), ("HN", 0), ("G", 11), ("G", 7),
+    ("P", 10), ("R", 6), ("R", 11), ("A", 6), ("A", 11), ("S", "a", 0, 0), ("R", 7), ("F", "b", 1), ("X", 10), ("A", 7),
+    ("P", 6), ("HY", 0), ("R", 1), ("P", 11), ("R", 3), ("A", 1), ("A", 2), ("P", 7), ("S", "a", 0, 1), ("X", 6),
+    ("F", "b", 0), ("DP", 1), ("X", 11), ("A", 3), ("M", 2), ("HO", 0), ("X", 7), ("P", 1), ("P", 2), ("M", 3), ("DP", 0),
+    ("P", 3), ("X", 1), ("T", 1), ("X", 2), ("T", 2), ("X", 3), ("T", 3),
 )
 MLP_STEPS = (
     ("XF", 0, 1), ("YR", 0), ("WT", 0), ("XF", 0, 0), ("XH", 0, 1), ("XF", 0, 3), ("YRH", 0), ("XF", 2, 0), ("N", 0, 1),
@@ -77,10 +77,11 @@
         self.xa, self.xb = x + 1 - 2 * rem(x, 2), rem(x + 3 + 2 * rem(x, 2), NX)
         self.pa, self.pb = {"tx": self.xa * 2 + c, "ty": y}, {"tx": self.xb * 2 + c, "ty": y}
 
-    def barrier(self):
+    def barrier(self, between):
         sem = pltpu.get_barrier_semaphore()
         for dev in (self.right, self.left, self.up, self.down, self.partner):
             pl.semaphore_signal(sem, inc=1, device_id=dev, device_id_type=MESH)
+        between()
         pl.semaphore_wait(sem, 5)
 
 
@@ -307,11 +308,11 @@
 
 
 def attention_kernel(
-    units, x_ref, turn_ref, base_ref, wq, wk, wv, wo, wg_t, wu_t,
-    h_ref, w_all, hg_all,
-    xc, xg, hg, cos_all, sin_all, st_own, st_in, s1, s2, wb, wob, part, precv, qb, kvo, kvp, og, zb, ya, yb, yfd, yfu, own, drel_a, drel_b,
+    units, x_hbm, turn_ref, base_ref, wq, wk, wv, wo, wg_t, wu_t,
+    h_hbm, w_all, hg_all,
+    x_ref, h_ref, xc, xg, hg, cos_all, sin_all, st_own, st_in, s1, s2, wb, wob, part, precv, qb, kvo, kvp, og, zb, ya, yb, yfd, yfu, own, drel_a, drel_b,
     sxe, rxe, sst, rst, sy, ry, syh, ryh, sd, rd, swa, rwa, swo, rwo, swp, rwp, lw, so, ro, spr, rpr, skv, rkv, sog, rog, syr, ryr,
-    lg, sds, rds, sdo, rdo, sdf, rdf, sdp, rdp, shx, rhx, shy, rhy, shz, rhz, lh,
+    lg, sds, rds, sdo, rdo, sdf, rdf, sdp, rdp, shx, rhx, shy, rhy, shz, rhz, lh, lx,
 ):
     at = Place()
     x, c, y = at.x, at.c, at.y
@@ -352,9 +353,12 @@
     def XP(j):
         x_pair(j).start()
 
+    arrived = []
+
     def XE(u):
         j, lo, n, _ = units[u]
-        if lo == 0:
+        if j not in arrived:
+            arrived.append(j)
             dst = xc.at[j, :, half_cols(1 - c)]
             remote(dst, dst, sd.at[j], rd.at[j], at.partner).wait_recv()
         xe_copy(u, x).start()
@@ -393,7 +397,8 @@
         return pl.ds(al(rem(xx, 2) * kc + core * kd, 128), kd)
 
     def w_part(group, half, i):
-        return weights[i].at[:, pl.ds(al((2 * group + half) * hc, 128), hc)]
+        side = kh if half else 1 - kh
+        return weights[i].at[:, pl.ds(al((2 * group + side) * hc, 128), hc)]
 
     def w_cols(half, i):
         return pl.ds(half * 3 * hc + i * hc, hc)
@@ -429,12 +434,20 @@
             wa_copy(half, i, at.xa).wait_recv()
         wp_copy(half, c).start()
 
-    def w_ready():
-        for half, i in pieces:
+    w_halves = [0, 1]
+
+    def w_ready(half):
+        if half not in w_halves:
+            return
+        w_halves.remove(half)
+        for i in range(3):
             w_local(half, i).wait()
             wo_copy(half, i, 1 - c).wait_recv()
-        for half in range(2):
-            wp_copy(half, 1 - c).wait_recv()
+        wp_copy(half, 1 - c).wait_recv()
+        if half:
+            own_out()
+
+    def own_out():
         for m in range(2):
             d_in(m).wait()
             d_out(m).start()
@@ -497,20 +510,33 @@
             d_pair(m, k, c).start()
 
     def pr_copy(n):
-        src = part.at[n, :, pl.ds(al((1 - kh) * 3 * hc, 128), 3 * hc)]
-        return remote(src, precv.at[n], spr.at[n], rpr.at[n], at.pb)
+        return remote(part.at[n, :, pl.ds(0, 3 * hc)], precv.at[n], spr.at[n], rpr.at[n], at.pb)
+
+    def project(g, first, size):
+        def done(col, step, out):
+            for i, (r, j) in enumerate(GROUPS[g]):
+                part[r * NJ + j, :, pl.ds(al(first + col, 128), step)] = out[i * ch : (i + 1) * ch].astype(BF16)
+
+        refs = [xg.at[gather.seqs[r], j] for r, j in GROUPS[g]]
+        product(refs, wb.at[:, pl.ds(first, size)], wb.shape[0], size, done)
+
+    split = {step[1] for step in ATTENTION_STEPS if step[0] == "Q"}
 
     def G(g):
+        w_ready(0)
         for r, j in GROUPS[g]:
             gather.chunk_wait(r, j)
-
-        def done(col, size, out):
-            for i, (r, j) in enumerate(GROUPS[g]):
-                part[r * NJ + j, :, pl.ds(al(col, 128), size)] = out[i * ch : (i + 1) * ch].astype(BF16)
-
-        product([xg.at[gather.seqs[r], j] for r, j in GROUPS[g]], wb, wb.shape[0], wb.shape[1], done)
+        if g in split:
+            project(g, 0, 3 * hc)
+        else:
+            w_ready(1)
+            project(g, 0, 6 * hc)
         for r, j in GROUPS[g]:
             pr_copy(r * NJ + j).start()
+
+    def Q(g):
+        w_ready(1)
+        project(g, 3 * hc, 3 * hc)
 
     def kv_copy(r, j):
         s, n = gather.seqs[r], r * NJ + j
@@ -522,7 +548,7 @@
         cos_t, sin_t = cos_all[j], sin_all[j]
 
         def total(col, size):
-            mine = part[n, :, pl.ds(al(kh * 3 * hc + col, 128), size)]
+            mine = part[n, :, 3 * hc + col : 3 * hc + col + size]
             return (mine.astype(F32) + precv[n, :, col : col + size].astype(F32)).astype(BF16)
 
         def turned(col):
@@ -622,6 +648,10 @@
     def T(j):
         attn = reduce.total(j).astype(BF16)
         h_ref[j] = (xc[j].astype(F32) + attn.astype(F32)).astype(BF16)
+        chunk_out(j).start()
+
+    def chunk_out(j):
+        return pltpu.make_async_copy(h_ref.at[j], h_hbm.at[j], lx.at[1 + j])
 
     def h_out(r):
         return pltpu.make_async_copy(hg.at[ahead.seqs[r], 0], hg_all.at[ahead.seqs[r]], lh.at[r])
@@ -640,14 +670,19 @@
             ahead.yhalf_wait(d, u)
         h_out(2).start()
 
-    for half, i in pieces:
-        w_local(half, i).start()
-    o_local.start()
-    for m in range(2):
-        d_in(m).start()
-    for j in range(NJ):
-        xc[j, :, half_cols(c)] = x_ref[x_rows(j, c), :]
-    at.barrier()
+    def own_rows():
+        for half, i in pieces:
+            w_local(half, i).start()
+        o_local.start()
+        for m in range(2):
+            d_in(m).start()
+        x_in.wait()
+        for j in range(NJ):
+            xc[j, :, half_cols(c)] = x_ref[x_rows(j, c), :]
+
+    x_in = pltpu.make_async_copy(x_hbm, x_ref, lx.at[0])
+    x_in.start()
+    at.barrier(own_rows)
 
     def angles():
         lane = lax.broadcasted_iota(jnp.int32, (ch, HEAD_DIM), 1)
@@ -659,10 +694,10 @@
 
     ops = {
         "XP": XP, "WOP": WOP, "XE": XE, "ST": ST, "N": N, "YH": gather.YH, "WA": WA, "WP": WP, "S": S, "O": O, "F": F, "DP": DP,
-        "G": G, "R": R, "A": A, "P": P, "X": X, "M": reduce.middle, "T": T,
+        "G": G, "Q": Q, "R": R, "A": A, "P": P, "X": X, "M": reduce.middle, "T": T,
         "HF": HF, "HH": lambda u: ahead.XH(0, u), "HN": lambda u: ahead.N(0, u), "HY": HY, "HO": HO,
     }
-    waits = {"G": w_ready, "X": o_ready, "WP": angles}
+    waits = {"X": o_ready, "WP": angles}
     for step in ATTENTION_STEPS:
         if step[0] in waits:
             waits.pop(step[0])()
@@ -690,6 +725,8 @@
     ahead.drain()
     for r in range(NX):
         h_out(r).wait()
+    for j in range(NJ):
+        chunk_out(j).wait()
     o_pair.wait_send()
     for half, i in pieces:
         wa_copy(half, i, x).wait_send()
@@ -708,9 +745,9 @@
 
 
 def mlp_kernel(
-    units, h_ref, w_hbm, wdn, hg_hbm, y_ref,
-    xg, wt, raw, wd, ag, ar, act, s1, s2, zb, ya, yb, yfd, yfu, yst,
-    sx, rx, sy, ry, syh, ryh, sa, ra, syr, ryr, sd, rd, lw, lwd, swd, rwd, lh,
+    units, h_hbm, w_hbm, wdn, hg_hbm, y_ref,
+    h_ref, xg, wt, raw, wd, ag, ar, act, s1, s2, zb, ya, yb, yfd, yfu, yst,
+    sx, rx, sy, ry, syh, ryh, sa, ra, syr, ryr, sd, rd, lw, lwd, swd, rwd, lh, lo,
 ):
     at = Place()
     x, c, y = at.x, at.c, at.y
@@ -759,6 +796,8 @@
         return remote(src, dst, swd.at[q, k], rwd.at[q, k], at.partner)
 
     quarters = [(q, k) for q in range(NX) for k in range(2)]
+    h_in_all = pltpu.make_async_copy(h_hbm, h_ref, lo.at[NJ])
+    h_in_all.start()
     for q in range(slots):
         w_in(q).start()
     def h_in(s):
@@ -770,7 +809,7 @@
         d_own(q, k).start()
     for q in range(NX):
         wd[NX * fm + q * 128 + fr : NX * fm + (q + 1) * 128, :] = jnp.zeros((128 - fr, kc), BF16)
-    at.barrier()
+    at.barrier(h_in_all.wait)
     for q, k in quarters:
         d_pair(q, k, c).start()
 
@@ -844,6 +883,9 @@
     def y_copy(j):
         return remote(yst.at[1 - c, j], y_ref.at[y_rows(j, c)], sd.at[j], rd.at[j], at.partner)
 
+    def y_own(j):
+        return pltpu.make_async_copy(yst.at[c, j], y_ref.at[y_rows(j, c)], lo.at[j])
+
     def y_wait(j):
         dst = y_ref.at[y_rows(j, 1 - c)]
         remote(dst, dst, sd.at[j], rd.at[j], at.partner).wait_recv()
@@ -854,7 +896,7 @@
         yst[0, j] = out[:, :kd]
         yst[1, j] = out[:, kd:]
         y_copy(j).start()
-        y_ref[y_rows(j, c), :] = yst[c, j]
+        y_own(j).start()
 
     ops = {"G": G, "P": P, "X": X, "M": reduce.middle, "T": T, "WT": WT}
     for name in ("YR", "YRH", "YH", "XF", "XH", "N"):
@@ -883,6 +925,7 @@
     lax.fori_loop(0, NCH, chunk_sent, 0)
     for j in range(NJ):
         y_copy(j).wait_send()
+        y_own(j).wait()
         y_wait(j)
 
 
@@ -931,10 +974,10 @@
                 jax.ShapeDtypeStruct((2, fc, width), BF16),
                 jax.ShapeDtypeStruct((NX, ch, width), BF16),
             ),
-            in_specs=[vmem_spec] * 3 + [any_spec] * 6,
-            out_specs=(vmem_spec, any_spec, any_spec),
+            in_specs=[any_spec] + [vmem_spec] * 2 + [any_spec] * 6,
+            out_specs=(any_spec, any_spec, any_spec),
             scratch_shapes=[
-                vmem(NJ, ch, kc), vmem(NX, NJ, ch, 2 * kc), vmem(NX, 1, ch, width), vmem(NJ, ch, HEAD_DIM, dtype=F32), vmem(NJ, ch, HEAD_DIM, dtype=F32),
+                vmem(seq, kd), vmem(NJ, ch, kc), vmem(NJ, ch, kc), vmem(NX, NJ, ch, 2 * kc), vmem(NX, 1, ch, width), vmem(NJ, ch, HEAD_DIM, dtype=F32), vmem(NJ, ch, HEAD_DIM, dtype=F32),
                 vmem(NJ, ch // 4, 128, dtype=F32), vmem(NJ, ch // 4, 128, dtype=F32), vmem(ch, 128, dtype=F32), vmem(ch, 128, dtype=F32),
                 vmem(2 * kc, 6 * hc), vmem(row_heads, kc), vmem(NCH, ch, 6 * hc), vmem(NCH, ch, 3 * hc), vmem(NCH, ch, hc),
                 vmem(NX, NJ, ch, 2 * hc), vmem(NX, NJ, ch, 2 * hc), vmem(NCH, ch, row_heads), *reduce_scratch,
@@ -943,7 +986,7 @@
                 sems(NJ), sems(NJ), sems(2, 3), sems(2, 3), sems(2, 3), sems(2, 3), sems(2), sems(2), sems(3, 3), sems(1), sems(1),
                 sems(NCH), sems(NCH), sems(NCH), sems(NCH), sems(4, NCH), sems(4, NCH), sems(4, NJ), sems(4, NJ),
                 sems(2, 2), sems(2, 2, 2), sems(2, 2, 2), sems(2, 2), sems(2, 2), sems(2, 2), sems(2, 2), sems(2, 4), sems(2, 4),
-                sems(4, 1), sems(4, 1), sems(2, 1), sems(2, 1), sems(2, 1), sems(2, 1), sems(NX),
+                sems(4, 1), sems(4, 1), sems(2, 1), sems(2, 1), sems(2, 1), sems(2, 1), sems(NX), sems(1 + NJ),
             ],
             compiler_params=pltpu.CompilerParams(collective_id=0, has_side_effects=True, vmem_limit_bytes=VMEM_LIMIT),
             name="attention_part",
@@ -954,16 +997,17 @@
         y_blk = pl.pallas_call(
             functools.partial(mlp_kernel, units),
             out_shape=jax.ShapeDtypeStruct((seq, kd), BF16),
-            in_specs=[vmem_spec, any_spec, any_spec, any_spec],
-            out_specs=vmem_spec,
+            in_specs=[any_spec] * 4,
+            out_specs=any_spec,
             scratch_shapes=[
+                vmem(NJ, ch, kc),
                 vmem(NX, NJ, ch, width), vmem(width, tiles * 256), vmem(3, 128, width),
                 vmem(NX * tiles * 128, kc), vmem(NCH, ch, NX * tiles * 128), vmem(NCH, h, NX * 128), vmem(2 * ch, tiles * 128),
                 vmem(ch, 128, dtype=F32), vmem(ch, 128, dtype=F32),
                 *reduce_scratch, vmem(2, NJ, ch, kd),
                 sems(4, n_x), sems(4, n_x), sems(2, n_u), sems(2, n_u), sems(2, n_u), sems(2, n_u),
                 sems(4, NCH, 2), sems(4, NCH, 2), sems(4, NJ), sems(4, NJ), sems(NJ), sems(NJ),
-                sems(2 * tiles), sems(NX, 2), sems(NX, 2), sems(NX, 2), sems(NX),
+                sems(2 * tiles), sems(NX, 2), sems(NX, 2), sems(NX, 2), sems(NX), sems(NJ + 1),
             ],
             compiler_params=pltpu.CompilerParams(collective_id=1, has_side_effects=True, vmem_limit_bytes=VMEM_LIMIT),
             name="mlp_part",

time: 334 us -> 331 us (level)
  Pallas kernels: 332 us -> 328 us
where the time goes in v9:
time: 331 us; the launch traced here: 330 us
  Pallas kernels  328 us (99%)
    pallas_call x1, Pallas kernels, layer(): pl.pallas_call(functools.partial(attention_kernel, units), out_shape=(jax...  183 us
    pallas_call x1, Pallas kernels, layer(): pl.pallas_call(functools.partial(mlp_kernel, units), out_shape=jax.ShapeD...  146 us

profile of v9, /device:TPU:97, one launch (start us, length us, event | category | flops | bytes accessed | tf_op | source)
XLA Modules:
  0.0 330.5 jit_solution(15602008884088876862)
XLA Ops:
  0.0 182.6 %attention_part.1 = (bf16[4,128,1024]{2,1,0:T(8,128)(2,1)}, bf16[2,688,4096]{2,1,0:T(8,128)(2,1)}, bf16[4,128,4096]{2,1,0:T(8,128)(2,1)}) custom-call(bf16[1024,512]{1,0:T(8,128)(2,1)} %bitcast.7, f32[2,128,128]{2,1,0:T(8,128)} %constant.4.clone.turn_ref, f32[2,8,128]{2,1,0:T(8,128)} %constant.5.clone.base_ref, bf16[512,1024]{1,0:T(8,128)(2,1)} %wq.1, ...), custom_call_target="tpu_custom_call" | custom-call | tf_op jit(solution)/shard_map/attention_part/pallas_call | solution.py:970
  182.6 145.6 %mlp_part.1 = bf16[1024,512]{1,0:T(8,128)(2,1)} custom-call(bf16[4,128,1024]{2,1,0:T(8,128)(2,1)} %get-tuple-element.8.h_hbm, bf16[2,688,4096]{2,1,0:T(8,128)(2,1)} %get-tuple-element.9.w_hbm, bf16[2752,512]{1,0:T(8,128)(2,1)} %wdn.1, bf16[4,128,4096]{2,1,0:T(8,128)(2,1)} %get-tuple-element.10.hg_hbm), custom_call_target="tpu_custom_call" | custom-call | tf_op jit(solution)/shard_map/mlp_part/pallas_call | solution.py:997
  328.2 2.3 copy.12

commit v10 on v9

--- a/solution.py
+++ b/solution.py
@@ -38,18 +38,18 @@
 
 
 ATTENTION_STEPS = (
-    ("S", "b", 0, 0), ("WA", 0), ("XP", 3), ("XP", 0), ("WOP",), ("XE", 1), ("XE", 0), ("O", "b", 0), ("XP", 1), ("XE", 2),
-    ("XP", 2), ("WA", 1), ("S", "b", 1, 0), ("ST", 1), ("S", "b", 0, 1), ("ST", 0), ("XE", 3), ("O", "b", 1), ("N", 1),
-    ("WP", 0), ("ST", 2), ("N", 0), ("S", "b", 1, 1), ("YH", 1), ("YH", 0), ("G", 0), ("N", 2), ("S", "a", 1, 0), ("WP", 1),
-    ("G", 8), ("G", 4), ("Q", 8), ("ST", 3), ("Q", 0), ("R", 8), ("A", 8), ("O", "a", 1), ("R", 0), ("YH", 2), ("G", 5),
-    ("N", 3), ("R", 4), ("P", 8), ("A", 4), ("G", 9), ("XE", 4), ("A", 0), ("R", 5), ("X", 8), ("P", 4), ("A", 5), ("YH", 3),
-    ("G", 1), ("R", 9), ("P", 0), ("ST", 4), ("A", 9), ("F", "a", 1), ("X", 4), ("M", 0), ("G", 2), ("G", 10), ("N", 4),
-    ("P", 5), ("X", 0), ("P", 9), ("T", 0), ("R", 2), ("HF", 0), ("G", 3), ("X", 9), ("O", "a", 0), ("X", 5), ("YH", 4),
-    ("HH", 0), ("G", 6), ("M", 1), ("S", "a", 1, 1), ("R", 10), ("A", 10), ("F", "a", 0), ("HN", 0), ("G", 11), ("G", 7),
-    ("P", 10), ("R", 6), ("R", 11), ("A", 6), ("A", 11), ("S", "a", 0, 0), ("R", 7), ("F", "b", 1), ("X", 10), ("A", 7),
-    ("P", 6), ("HY", 0), ("R", 1), ("P", 11), ("R", 3), ("A", 1), ("A", 2), ("P", 7), ("S", "a", 0, 1), ("X", 6),
-    ("F", "b", 0), ("DP", 1), ("X", 11), ("A", 3), ("M", 2), ("HO", 0), ("X", 7), ("P", 1), ("P", 2), ("M", 3), ("DP", 0),
-    ("P", 3), ("X", 1), ("T", 1), ("X", 2), ("T", 2), ("X", 3), ("T", 3),
+    ("WA", 0), ("XP", 1), ("S", "b", 0, 1), ("XP", 0), ("XE", 1), ("XE", 0), ("XE", 2), ("XP", 2), ("S", "b", 0, 0), ("XP", 3),
+    ("S", "b", 1, 0), ("ST", 1), ("WP", 0), ("WA", 1), ("O", "b", 1), ("ST", 0), ("N", 1), ("O", "b", 0), ("ST", 2),
+    ("S", "b", 1, 1), ("WOP",), ("N", 0), ("G", 0), ("XE", 3), ("YH", 1), ("YH", 0), ("S", "a", 0, 1), ("N", 2), ("WP", 1),
+    ("G", 8), ("G", 4), ("ST", 3), ("Q", 8), ("Q", 0), ("R", 8), ("XE", 4), ("A", 8), ("F", "a", 1), ("YH", 2), ("G", 5),
+    ("R", 4), ("ST", 4), ("N", 3), ("P", 8), ("G", 9), ("A", 4), ("R", 0), ("S", "a", 1, 1), ("X", 8), ("G", 1), ("N", 4),
+    ("R", 5), ("A", 0), ("R", 9), ("P", 4), ("A", 9), ("A", 5), ("G", 2), ("P", 0), ("X", 4), ("M", 0), ("P", 9),
+    ("S", "a", 1, 0), ("YH", 3), ("G", 6), ("P", 5), ("X", 0), ("T", 0), ("HF", 1), ("HF", 0), ("R", 2), ("X", 9), ("R", 1),
+    ("A", 1), ("YH", 4), ("X", 5), ("M", 1), ("HH", 1), ("O", "a", 0), ("G", 10), ("R", 6), ("HH", 0), ("G", 7), ("O", "a", 1),
+    ("HN", 1), ("R", 10), ("G", 11), ("A", 10), ("A", 6), ("HN", 0), ("R", 7), ("A", 2), ("HY", 1), ("A", 7), ("R", 11),
+    ("P", 10), ("A", 11), ("P", 6), ("G", 3), ("P", 7), ("P", 11), ("F", "b", 1), ("F", "a", 0), ("X", 10), ("HY", 0),
+    ("S", "a", 0, 0), ("F", "b", 0), ("R", 3), ("X", 11), ("A", 3), ("X", 6), ("HO", 1), ("X", 7), ("P", 1), ("P", 2),
+    ("M", 2), ("M", 3), ("DP", 1), ("DP", 0), ("P", 3), ("HO", 0), ("X", 1), ("T", 1), ("X", 2), ("T", 2), ("X", 3), ("T", 3),
 )
 MLP_STEPS = (
     ("XF", 0, 1), ("YR", 0), ("WT", 0), ("XF", 0, 0), ("XH", 0, 1), ("XF", 0, 3), ("YRH", 0), ("XF", 2, 0), ("N", 0, 1),
@@ -325,7 +325,7 @@
     ng = rem(div(x + 1, 2), 2)
     gather = Spread(at, xc, xg, units, (s1, s2), None, None, sy, ry, syh, ryh)
     reduce = Reduce(at, zb, ya, yb, yfd, yfu, syr, ryr)
-    ahead = Spread(at, h_ref, hg, ((0, 0, ch, 0),), (s1, s2), shx, rhx, shy, rhy, shz, rhz)
+    ahead = Spread(at, h_ref, hg, ((0, 0, ch // 2, 0), (0, ch // 2, ch // 2, 0)), (s1, s2), shx, rhx, shy, rhy, shz, rhz)
     weights = (wq, wk, wv)
 
     def half_cols(core):
@@ -653,22 +653,27 @@
     def chunk_out(j):
         return pltpu.make_async_copy(h_ref.at[j], h_hbm.at[j], lx.at[1 + j])
 
-    def h_out(r):
-        return pltpu.make_async_copy(hg.at[ahead.seqs[r], 0], hg_all.at[ahead.seqs[r]], lh.at[r])
+    def h_out(r, u):
+        rows = pl.ds(u * (ch // 2), ch // 2)
+        return pltpu.make_async_copy(hg.at[ahead.seqs[r], 0, rows], hg_all.at[ahead.seqs[r], rows], lh.at[r, u])
+
+    kept = []
 
     def HF(u):
-        ahead.keep_own()
+        if not kept:
+            kept.append(u)
+            ahead.keep_own()
         ahead.XF(0, u)
 
     def HY(u):
         ahead.YH(u)
         for r in (0, 1, 3):
-            h_out(r).start()
+            h_out(r, u).start()
 
     def HO(u):
         for d in range(2):
             ahead.yhalf_wait(d, u)
-        h_out(2).start()
+        h_out(2, u).start()
 
     def own_rows():
         for half, i in pieces:
@@ -697,51 +702,56 @@
         "G": G, "Q": Q, "R": R, "A": A, "P": P, "X": X, "M": reduce.middle, "T": T,
         "HF": HF, "HH": lambda u: ahead.XH(0, u), "HN": lambda u: ahead.N(0, u), "HY": HY, "HO": HO,
     }
+    def sent():
+        for m in range(2):
+            for k in range(4):
+                d_pair(m, k, 1 - c).wait_recv()
+                d_pair(m, k, c).wait_send()
+            d_out(m).wait()
+            for d in range(2):
+                for p in range(2):
+                    s_copy(d, m, p, x).wait_send()
+                o_copy(d, m).wait_send()
+                f_copy(d, m, x).wait_send()
+        for j in range(NJ):
+            x_pair(j).wait_send()
+        for u in range(len(units)):
+            xe_copy(u, x).wait_send()
+            st_copy(u).wait_send()
+            for d in range(2):
+                gather.ycopy(d, u).wait_send()
+                gather.yhalf(d, u).wait_send()
+        reduce.drain()
+        ahead.drain()
+        for r in range(NX):
+            for u in range(2):
+                h_out(r, u).wait()
+        o_pair.wait_send()
+        for half, i in pieces:
+            wa_copy(half, i, x).wait_send()
+            wo_copy(half, i, c).wait_send()
+        for half in range(2):
+            wp_copy(half, c).wait_send()
+
+        def chunk_sent(n, carry):
+            pr_copy(n).wait_send()
+            remote(kvo.at[0, 0], kvp.at[0, 0], skv.at[n], rkv.at[n], at.partner).wait_send()
+            for kind in range(4):
+                og_copy(kind, n).wait_send()
+            return carry
+
+        lax.fori_loop(0, NCH, chunk_sent, 0)
+
     waits = {"X": o_ready, "WP": angles}
-    for step in ATTENTION_STEPS:
+    last = max(i for i, step in enumerate(ATTENTION_STEPS) if step[0] == "X")
+    for i, step in enumerate(ATTENTION_STEPS):
         if step[0] in waits:
             waits.pop(step[0])()
+        if i == last:
+            sent()
         ops[step[0]](*step[1:])
-
-    for m in range(2):
-        for k in range(4):
-            d_pair(m, k, 1 - c).wait_recv()
-            d_pair(m, k, c).wait_send()
-        d_out(m).wait()
-        for d in range(2):
-            for p in range(2):
-                s_copy(d, m, p, x).wait_send()
-            o_copy(d, m).wait_send()
-            f_copy(d, m, x).wait_send()
-    for j in range(NJ):
-        x_pair(j).wait_send()
-    for u in range(len(units)):
-        xe_copy(u, x).wait_send()
-        st_copy(u).wait_send()
-        for d in range(2):
-            gather.ycopy(d, u).wait_send()
-            gather.yhalf(d, u).wait_send()
-    reduce.drain()
-    ahead.drain()
-    for r in range(NX):
-        h_out(r).wait()
     for j in range(NJ):
         chunk_out(j).wait()
-    o_pair.wait_send()
-    for half, i in pieces:
-        wa_copy(half, i, x).wait_send()
-        wo_copy(half, i, c).wait_send()
-    for half in range(2):
-        wp_copy(half, c).wait_send()
-
-    def chunk_sent(n, carry):
-        pr_copy(n).wait_send()
-        remote(kvo.at[0, 0], kvp.at[0, 0], skv.at[n], rkv.at[n], at.partner).wait_send()
-        for kind in range(4):
-            og_copy(kind, n).wait_send()
-        return carry
-
-    lax.fori_loop(0, NCH, chunk_sent, 0)
 
 
 def mlp_kernel(
@@ -906,23 +916,27 @@
         "G": lambda: [h_in(s).wait() for s in range(NX)],
         "X": lambda: [(d_own(q, k).wait(), d_pair(q, k, 1 - c).wait_recv()) for q, k in quarters],
     }
-    for step in MLP_STEPS:
+    def sent():
+        gather.drain()
+        reduce.drain()
+        for q, k in quarters:
+            d_pair(q, k, c).wait_send()
+
+        def chunk_sent(n, carry):
+            for kind in range(4):
+                for copy in a_copies(kind, n):
+                    copy.wait_send()
+            return carry
+
+        lax.fori_loop(0, NCH, chunk_sent, 0)
+
+    last = max(i for i, step in enumerate(MLP_STEPS) if step[0] == "X")
+    for i, step in enumerate(MLP_STEPS):
         if step[0] in waits:
             waits.pop(step[0])()
+        if i == last:
+            sent()
         ops[step[0]](*step[1:])
-
-    gather.drain()
-    reduce.drain()
-    for q, k in quarters:
-        d_pair(q, k, c).wait_send()
-
-    def chunk_sent(n, carry):
-        for kind in range(4):
-            for copy in a_copies(kind, n):
-                copy.wait_send()
-        return carry
-
-    lax.fori_loop(0, NCH, chunk_sent, 0)
     for j in range(NJ):
         y_copy(j).wait_send()
         y_own(j).wait()
@@ -986,7 +1000,7 @@
                 sems(NJ), sems(NJ), sems(2, 3), sems(2, 3), sems(2, 3), sems(2, 3), sems(2), sems(2), sems(3, 3), sems(1), sems(1),
                 sems(NCH), sems(NCH), sems(NCH), sems(NCH), sems(4, NCH), sems(4, NCH), sems(4, NJ), sems(4, NJ),
                 sems(2, 2), sems(2, 2, 2), sems(2, 2, 2), sems(2, 2), sems(2, 2), sems(2, 2), sems(2, 2), sems(2, 4), sems(2, 4),
-                sems(4, 1), sems(4, 1), sems(2, 1), sems(2, 1), sems(2, 1), sems(2, 1), sems(NX), sems(1 + NJ),
+                sems(4, 2), sems(4, 2), sems(2, 2), sems(2, 2), sems(2, 2), sems(2, 2), sems(NX, 2), sems(1 + NJ),
             ],
             compiler_params=pltpu.CompilerParams(collective_id=0, has_side_effects=True, vmem_limit_bytes=VMEM_LIMIT),
             name="attention_part",

time: 331 us -> 331 us (level)
  no operation moved by 1% of the time
where the time goes in v10:
time: 331 us
  Pallas kernels  328 us (99%)
    pallas_call x1, Pallas kernels, layer(): pl.pallas_call(functools.partial(attention_kernel, units), out_shape=(jax...  182 us
    pallas_call x1, Pallas kernels, layer(): pl.pallas_call(functools.partial(mlp_kernel, units), out_shape=jax.ShapeD...  146 us

profile of v10, /device:TPU:97, one launch (start us, length us, event | category | flops | bytes accessed | tf_op | source)
XLA Modules:
  0.0 330.6 jit_solution(6863627687754415893)
XLA Ops:
  0.0 182.2 %attention_part.1 = (bf16[4,128,1024]{2,1,0:T(8,128)(2,1)}, bf16[2,688,4096]{2,1,0:T(8,128)(2,1)}, bf16[4,128,4096]{2,1,0:T(8,128)(2,1)}) custom-call(bf16[1024,512]{1,0:T(8,128)(2,1)} %bitcast.7, f32[2,128,128]{2,1,0:T(8,128)} %constant.4.clone.turn_ref, f32[2,8,128]{2,1,0:T(8,128)} %constant.5.clone.base_ref, bf16[512,1024]{1,0:T(8,128)(2,1)} %wq.1, ...), custom_call_target="tpu_custom_call" | custom-call | tf_op jit(solution)/shard_map/attention_part/pallas_call | solution.py:984
  182.2 146.1 %mlp_part.1 = bf16[1024,512]{1,0:T(8,128)(2,1)} custom-call(bf16[4,128,1024]{2,1,0:T(8,128)(2,1)} %get-tuple-element.8.h_hbm, bf16[2,688,4096]{2,1,0:T(8,128)(2,1)} %get-tuple-element.9.w_hbm, bf16[2752,512]{1,0:T(8,128)(2,1)} %wdn.1, bf16[4,128,4096]{2,1,0:T(8,128)(2,1)} %get-tuple-element.10.hg_hbm), custom_call_target="tpu_custom_call" | custom-call | tf_op jit(solution)/shard_map/mlp_part/pallas_call | solution.py:1011
  328.3 2.3 copy.12

commit v11 on v10

--- a/solution.py
+++ b/solution.py
@@ -308,9 +308,9 @@
 
 
 def attention_kernel(
-    units, x_hbm, turn_ref, base_ref, wq, wk, wv, wo, wg_t, wu_t,
+    units, x_hbm, turn_hbm, base_hbm, wq, wk, wv, wo, wg_t, wu_t,
     h_hbm, w_all, hg_all,
-    x_ref, h_ref, xc, xg, hg, cos_all, sin_all, st_own, st_in, s1, s2, wb, wob, part, precv, qb, kvo, kvp, og, zb, ya, yb, yfd, yfu, own, drel_a, drel_b,
+    x_ref, turn_ref, base_ref, h_ref, xc, xg, hg, cos_all, sin_all, st_own, st_in, s1, s2, wb, wob, part, precv, qb, kvo, kvp, og, zb, ya, yb, yfd, yfu, own, drel_a, drel_b,
     sxe, rxe, sst, rst, sy, ry, syh, ryh, sd, rd, swa, rwa, swo, rwo, swp, rwp, lw, so, ro, spr, rpr, skv, rkv, sog, rog, syr, ryr,
     lg, sds, rds, sdo, rdo, sdf, rdf, sdp, rdp, shx, rhx, shy, rhy, shz, rhz, lh, lx,
 ):
@@ -510,7 +510,7 @@
             d_pair(m, k, c).start()
 
     def pr_copy(n):
-        return remote(part.at[n, :, pl.ds(0, 3 * hc)], precv.at[n], spr.at[n], rpr.at[n], at.pb)
+        return remote(part.at[n, :, pl.ds(0, 3 * hc)], precv.at[n], spr.at[0], rpr.at[n], at.pb)
 
     def project(g, first, size):
         def done(col, step, out):
@@ -540,7 +540,7 @@
 
     def kv_copy(r, j):
         s, n = gather.seqs[r], r * NJ + j
-        return remote(kvo.at[s, j], kvp.at[s, j], skv.at[n], rkv.at[n], at.partner)
+        return remote(kvo.at[s, j], kvp.at[s, j], skv.at[0], rkv.at[n], at.partner)
 
     def rotate(r, j):
         s, n = gather.seqs[r], r * NJ + j
@@ -577,13 +577,13 @@
             ref = og.at[n, pl.ds(0, cut), o_cols(at.xa)]
         else:
             ref = og.at[n, pl.ds(cut, ch - cut), o_cols(at.xb)]
-        return remote(ref, ref, sog.at[kind, n], rog.at[kind, n], at.pa if kind in (0, 3) else at.pb)
+        return remote(ref, ref, sog.at[kind], rog.at[kind, n], at.pa if kind in (0, 3) else at.pb)
 
     def og_wait(kind, n):
         xx = (at.xa, at.xb, at.xo, at.xo)[kind]
         rows = (pl.ds(0, ch), pl.ds(0, ch), pl.ds(0, cut), pl.ds(cut, ch - cut))[kind]
         dst = og.at[n, rows, o_cols(xx)]
-        remote(dst, dst, sog.at[kind, n], rog.at[kind, n], at.pa).wait_recv()
+        remote(dst, dst, sog.at[kind], rog.at[kind, n], at.pa).wait_recv()
 
     def attend(r, j, i):
         s, n = gather.seqs[r], r * NJ + j
@@ -687,9 +687,14 @@
 
     x_in = pltpu.make_async_copy(x_hbm, x_ref, lx.at[0])
     x_in.start()
+    tables = [pltpu.make_async_copy(src, dst, lx.at[1 + NJ + i]) for i, (src, dst) in enumerate(((turn_hbm, turn_ref), (base_hbm, base_ref)))]
+    for copy in tables:
+        copy.start()
     at.barrier(own_rows)
 
     def angles():
+        for copy in tables:
+            copy.wait()
         lane = lax.broadcasted_iota(jnp.int32, (ch, HEAD_DIM), 1)
         for j in range(NJ):
             base_cos, base_sin = base_ref[0, pl.ds(2 * j + c, 1), :], base_ref[1, pl.ds(2 * j + c, 1), :]
@@ -733,14 +738,12 @@
         for half in range(2):
             wp_copy(half, c).wait_send()
 
-        def chunk_sent(n, carry):
-            pr_copy(n).wait_send()
-            remote(kvo.at[0, 0], kvp.at[0, 0], skv.at[n], rkv.at[n], at.partner).wait_send()
-            for kind in range(4):
-                og_copy(kind, n).wait_send()
-            return carry
-
-        lax.fori_loop(0, NCH, chunk_sent, 0)
+        every = part.at[:, :, pl.ds(0, 3 * hc)]
+        remote(every, precv, spr.at[0], rpr.at[0], at.pb).wait_send()
+        remote(kvo, kvp, skv.at[0], rkv.at[0], at.partner).wait_send()
+        for kind, (lo, n) in enumerate(((0, ch), (0, ch), (0, cut), (cut, ch - cut))):
+            every = og.at[:, pl.ds(lo, n), o_cols(x)]
+            remote(every, every, sog.at[kind], rog.at[kind, 0], at.pa).wait_send()
 
     waits = {"X": o_ready, "WP": angles}
     last = max(i for i, step in enumerate(ATTENTION_STEPS) if step[0] == "X")
@@ -832,11 +835,11 @@
 
     def a_copies(kind, n):
         refs = a_refs(kind, n, (x, x, at.xl, at.xr)[kind])
-        return [remote(v, v, sa.at[kind, n, k], ra.at[kind, n, k], at.left if kind % 2 else at.right) for k, v in enumerate(refs)]
+        return [remote(v, v, sa.at[kind, k], ra.at[kind, n, k], at.left if kind % 2 else at.right) for k, v in enumerate(refs)]
 
     def a_wait(kind, n):
         for k, v in enumerate(a_refs(kind, n, (at.xl, at.xr, at.xo, at.xo)[kind])):
-            remote(v, v, sa.at[kind, n, k], ra.at[kind, n, k], at.right).wait_recv()
+            remote(v, v, sa.at[kind, k], ra.at[kind, n, k], at.right).wait_recv()
 
     def a_start(kind, n):
         for copy in a_copies(kind, n):
@@ -922,21 +925,15 @@
         for q, k in quarters:
             d_pair(q, k, c).wait_send()
 
-        def chunk_sent(n, carry):
-            for kind in range(4):
-                for copy in a_copies(kind, n):
-                    copy.wait_send()
-            return carry
-
-        lax.fori_loop(0, NCH, chunk_sent, 0)
-
-    last = max(i for i, step in enumerate(MLP_STEPS) if step[0] == "X")
-    for i, step in enumerate(MLP_STEPS):
+        for kind in range(4):
+            for k, every in enumerate(a_refs(kind, slice(None), x)):
+                remote(every, every, sa.at[kind, k], ra.at[kind, 0, k], at.right).wait_send()
+
+    for step in MLP_STEPS:
         if step[0] in waits:
             waits.pop(step[0])()
-        if i == last:
-            sent()
         ops[step[0]](*step[1:])
+    sent()
     for j in range(NJ):
         y_copy(j).wait_send()
         y_own(j).wait()
@@ -988,19 +985,20 @@
                 jax.ShapeDtypeStruct((2, fc, width), BF16),
                 jax.ShapeDtypeStruct((NX, ch, width), BF16),
             ),
-            in_specs=[any_spec] + [vmem_spec] * 2 + [any_spec] * 6,
+            in_specs=[any_spec] * 9,
             out_specs=(any_spec, any_spec, any_spec),
             scratch_shapes=[
-                vmem(seq, kd), vmem(NJ, ch, kc), vmem(NJ, ch, kc), vmem(NX, NJ, ch, 2 * kc), vmem(NX, 1, ch, width), vmem(NJ, ch, HEAD_DIM, dtype=F32), vmem(NJ, ch, HEAD_DIM, dtype=F32),
+                vmem(seq, kd), vmem(2, ch, HEAD_DIM, dtype=F32), vmem(2, 2 * NJ, HEAD_DIM, dtype=F32),
+                vmem(NJ, ch, kc), vmem(NJ, ch, kc), vmem(NX, NJ, ch, 2 * kc), vmem(NX, 1, ch, width), vmem(NJ, ch, HEAD_DIM, dtype=F32), vmem(NJ, ch, HEAD_DIM, dtype=F32),
                 vmem(NJ, ch // 4, 128, dtype=F32), vmem(NJ, ch // 4, 128, dtype=F32), vmem(ch, 128, dtype=F32), vmem(ch, 128, dtype=F32),
                 vmem(2 * kc, 6 * hc), vmem(row_heads, kc), vmem(NCH, ch, 6 * hc), vmem(NCH, ch, 3 * hc), vmem(NCH, ch, hc),
                 vmem(NX, NJ, ch, 2 * hc), vmem(NX, NJ, ch, 2 * hc), vmem(NCH, ch, row_heads), *reduce_scratch,
                 vmem(2, fc, kd), vmem(2, f_a, kd), vmem(2, fc - f_a, kd),
                 sems(n_u), sems(n_u), sems(n_u), sems(n_u), sems(2, n_u), sems(2, n_u), sems(2, n_u), sems(2, n_u),
                 sems(NJ), sems(NJ), sems(2, 3), sems(2, 3), sems(2, 3), sems(2, 3), sems(2), sems(2), sems(3, 3), sems(1), sems(1),
-                sems(NCH), sems(NCH), sems(NCH), sems(NCH), sems(4, NCH), sems(4, NCH), sems(4, NJ), sems(4, NJ),
+                sems(1), sems(NCH), sems(1), sems(NCH), sems(4), sems(4, NCH), sems(4, NJ), sems(4, NJ),
                 sems(2, 2), sems(2, 2, 2), sems(2, 2, 2), sems(2, 2), sems(2, 2), sems(2, 2), sems(2, 2), sems(2, 4), sems(2, 4),
-                sems(4, 2), sems(4, 2), sems(2, 2), sems(2, 2), sems(2, 2), sems(2, 2), sems(NX, 2), sems(1 + NJ),
+                sems(4, 2), sems(4, 2), sems(2, 2), sems(2, 2), sems(2, 2), sems(2, 2), sems(NX, 2), sems(3 + NJ),
             ],
             compiler_params=pltpu.CompilerParams(collective_id=0, has_side_effects=True, vmem_limit_bytes=VMEM_LIMIT),
             name="attention_part",
@@ -1020,7 +1018,7 @@
                 vmem(ch, 128, dtype=F32), vmem(ch, 128, dtype=F32),
                 *reduce_scratch, vmem(2, NJ, ch, kd),
                 sems(4, n_x), sems(4, n_x), sems(2, n_u), sems(2, n_u), sems(2, n_u), sems(2, n_u),
-                sems(4, NCH, 2), sems(4, NCH, 2), sems(4, NJ), sems(4, NJ), sems(NJ), sems(NJ),
+                sems(4, 2), sems(4, NCH, 2), sems(4, NJ), sems(4, NJ), sems(NJ), sems(NJ),
                 sems(2 * tiles), sems(NX, 2), sems(NX, 2), sems(NX, 2), sems(NX), sems(NJ + 1),
             ],
             compiler_params=pltpu.CompilerParams(collective_id=1, has_side_effects=True, vmem_limit_bytes=VMEM_LIMIT),

time: 331 us -> 328 us (level)
  no operation moved by 1% of the time
where the time goes in v11:
time: 328 us; the launch traced here: 327 us
  Pallas kernels  325 us (99%)
    pallas_call x1, Pallas kernels, layer(): pl.pallas_call(functools.partial(attention_kernel, units), out_shape=(jax...  180 us
    pallas_call x1, Pallas kernels, layer(): pl.pallas_call(functools.partial(mlp_kernel, units), out_shape=jax.ShapeD...  145 us

profile of v11, /device:TPU:97, one launch (start us, length us, event | category | flops | bytes accessed | tf_op | source)
XLA Modules:
  0.0 327.4 jit_solution(6319492762340212655)
XLA Ops:
  0.0 180.3 %attention_part.1 = (bf16[4,128,1024]{2,1,0:T(8,128)(2,1)}, bf16[2,688,4096]{2,1,0:T(8,128)(2,1)}, bf16[4,128,4096]{2,1,0:T(8,128)(2,1)}) custom-call(bf16[1024,512]{1,0:T(8,128)(2,1)} %bitcast.7, f32[2,128,128]{2,1,0:T(8,128)} %constant.4.clone.turn_hbm, f32[2,8,128]{2,1,0:T(8,128)} %constant.5.clone.base_hbm, bf16[512,1024]{1,0:T(8,128)(2,1)} %wq.1, ...), custom_call_target="tpu_custom_call" | custom-call | tf_op jit(solution)/shard_map/attention_part/pallas_call | solution.py:981
  180.3 144.8 %mlp_part.1 = bf16[1024,512]{1,0:T(8,128)(2,1)} custom-call(bf16[4,128,1024]{2,1,0:T(8,128)(2,1)} %get-tuple-element.8.h_hbm, bf16[2,688,4096]{2,1,0:T(8,128)(2,1)} %get-tuple-element.9.w_hbm, bf16[2752,512]{1,0:T(8,128)(2,1)} %wdn.1, bf16[4,128,4096]{2,1,0:T(8,128)(2,1)} %get-tuple-element.10.hg_hbm), custom_call_target="tpu_custom_call" | custom-call | tf_op jit(solution)/shard_map/mlp_part/pallas_call | solution.py:1009
  325.1 2.3 copy.12

commit v12 on v11

--- a/solution.py
+++ b/solution.py
@@ -278,7 +278,7 @@
             lambda: (self.zb.at[1, j], self.yfd.at[j]),
             lambda: (self.zb.at[3, j], self.yfu.at[j]),
         )[kind]()
-        return remote(src, dst, self.ss.at[kind, j], self.rs.at[kind, j], at.down if kind % 2 else at.up)
+        return remote(src, dst, self.ss.at[kind], self.rs.at[kind, j], at.down if kind % 2 else at.up)
 
     def wait(self, kind, j):
         self.copy(kind, j).wait_recv()
@@ -302,9 +302,9 @@
         return self.zb[0, j].astype(F32) + self.yfd[j].astype(F32) + self.yfu[j].astype(F32)
 
     def drain(self):
-        for j in range(NJ):
-            for kind in range(4):
-                self.copy(kind, j).wait_send()
+        h = self.h
+        for kind, every in enumerate((self.zb.at[2, :, 0:h], self.zb.at[2, :, h:], self.zb.at[1], self.zb.at[3])):
+            remote(every, every, self.ss.at[kind], self.rs.at[kind, 0], self.at.up).wait_send()
 
 
 def attention_kernel(
@@ -335,7 +335,7 @@
         return pl.ds(al((2 * j + core) * ch, 8), ch)
 
     def x_pair(j):
-        return remote(x_ref.at[x_rows(j, 1 - c)], xc.at[j, :, half_cols(c)], sd.at[j], rd.at[j], at.partner)
+        return remote(x_ref.at[x_rows(j, 1 - c)], xc.at[j, :, half_cols(c)], sd.at[0], rd.at[j], at.partner)
 
     def pair_cols(xx):
         return pl.ds(al(rem(xx, 2) * kc, 128), kc)
@@ -343,12 +343,12 @@
     def xe_copy(u, xx):
         j, lo, n, _ = units[u]
         rows = pl.ds(lo, n)
-        return remote(xc.at[j, rows], xg.at[y, j, rows, pair_cols(xx)], sxe.at[u], rxe.at[u], at.pa)
+        return remote(xc.at[j, rows], xg.at[y, j, rows, pair_cols(xx)], sxe.at[0], rxe.at[u], at.pa)
 
     def st_copy(u):
         j, lo, n, _ = units[u]
         rows = pl.ds(lo // 4, n // 4)
-        return remote(st_own.at[j, rows], st_in.at[j, rows], sst.at[u], rst.at[u], at.pb)
+        return remote(st_own.at[j, rows], st_in.at[j, rows], sst.at[0], rst.at[u], at.pb)
 
     def XP(j):
         x_pair(j).start()
@@ -360,7 +360,7 @@
         if j not in arrived:
             arrived.append(j)
             dst = xc.at[j, :, half_cols(1 - c)]
-            remote(dst, dst, sd.at[j], rd.at[j], at.partner).wait_recv()
+            remote(dst, dst, sd.at[0], rd.at[j], at.partner).wait_recv()
         xe_copy(u, x).start()
         xg[y, j, lo : lo + n, pair_cols(x)] = xc[j, lo : lo + n]
 
@@ -404,17 +404,17 @@
         return pl.ds(half * 3 * hc + i * hc, hc)
 
     def wa_copy(half, i, xx):
-        return remote(w_part(1 - ng, half, i), wb.at[w_rows(xx, c), w_cols(half, i)], swa.at[half, i], rwa.at[half, i], at.pa)
+        return remote(w_part(1 - ng, half, i), wb.at[w_rows(xx, c), w_cols(half, i)], swa.at[0], rwa.at[half, i], at.pa)
 
     def wo_copy(half, i, core):
-        return remote(w_part(ng, half, i), wb.at[w_rows(x, core), w_cols(half, i)], swo.at[half, i], rwo.at[half, i], at.partner)
+        return remote(w_part(ng, half, i), wb.at[w_rows(x, core), w_cols(half, i)], swo.at[0], rwo.at[half, i], at.partner)
 
     def w_local(half, i):
         return pltpu.make_async_copy(w_part(ng, half, i), wb.at[w_rows(x, c), w_cols(half, i)], lw.at[half, i])
 
     def wp_copy(half, core):
         ref = wb.at[w_rows(at.xa, core), pl.ds(half * 3 * hc, 3 * hc)]
-        return remote(ref, ref, swp.at[half], rwp.at[half], at.partner)
+        return remote(ref, ref, swp.at[0], rwp.at[half], at.partner)
 
     o_local = pltpu.make_async_copy(wo, wob.at[:, half_cols(c)], lw.at[2, 0])
     o_pair = remote(wo, wob.at[:, half_cols(c)], so.at[0], ro.at[0], at.partner)
@@ -469,13 +469,13 @@
 
     def s_copy(d, m, p, xx):
         to, dev = ((at.xa, at.pa), (at.xb, at.pb))[d]
-        return remote(d_src(m, to, p), d_dst(m, xx, p), sds.at[d, m, p], rds.at[d, m, p], dev)
+        return remote(d_src(m, to, p), d_dst(m, xx, p), sds.at[d], rds.at[d, m, p], dev)
 
     def o_copy(d, m):
-        return remote(d_src(m, at.xo, d), (drel_a, drel_b)[d].at[m], sdo.at[d, m], rdo.at[d, m], (at.pa, at.pb)[d])
+        return remote(d_src(m, at.xo, d), (drel_a, drel_b)[d].at[m], sdo.at[d], rdo.at[d, m], (at.pa, at.pb)[d])
 
     def f_copy(d, m, xx):
-        return remote((drel_a, drel_b)[d].at[m], d_dst(m, xx, d), sdf.at[d, m], rdf.at[d, m], (at.pb, at.pa)[d])
+        return remote((drel_a, drel_b)[d].at[m], d_dst(m, xx, d), sdf.at[d], rdf.at[d, m], (at.pb, at.pa)[d])
 
     def d_in(m):
         return pltpu.make_async_copy(mlp_weights[m].at[pl.ds(al(x * fc, 8), fc)], own.at[m], lg.at[0, m])
@@ -488,7 +488,7 @@
 
     def d_pair(m, k, core):
         dst = d_all(m, (at.xa, at.xb, at.xo, x)[k], core)
-        return remote(own.at[m] if k == 3 else dst, dst, sdp.at[m, k], rdp.at[m, k], at.partner)
+        return remote(own.at[m] if k == 3 else dst, dst, sdp.at[0], rdp.at[m, k], at.partner)
 
     def S(link, m, p):
         s_copy("ab".index(link), m, p, x).start()
@@ -707,43 +707,37 @@
         "G": G, "Q": Q, "R": R, "A": A, "P": P, "X": X, "M": reduce.middle, "T": T,
         "HF": HF, "HH": lambda u: ahead.XH(0, u), "HN": lambda u: ahead.N(0, u), "HY": HY, "HO": HO,
     }
+    def all_sent(ref, sem):
+        remote(ref, ref, sem, ro.at[0], at.partner).wait_send()
+
     def sent():
         for m in range(2):
             for k in range(4):
                 d_pair(m, k, 1 - c).wait_recv()
-                d_pair(m, k, c).wait_send()
             d_out(m).wait()
-            for d in range(2):
-                for p in range(2):
-                    s_copy(d, m, p, x).wait_send()
-                o_copy(d, m).wait_send()
-                f_copy(d, m, x).wait_send()
-        for j in range(NJ):
-            x_pair(j).wait_send()
-        for u in range(len(units)):
-            xe_copy(u, x).wait_send()
-            st_copy(u).wait_send()
-            for d in range(2):
+        all_sent(w_all.at[:, :, pl.ds(0, 4 * kd)], sdp.at[0])
+        for d in range(2):
+            all_sent(w_all.at[:, :, pl.ds(0, kd)], sds.at[d])
+            all_sent((drel_a, drel_b)[d], sdo.at[d])
+            all_sent((drel_a, drel_b)[d], sdf.at[d])
+            for u in range(len(units)):
                 gather.ycopy(d, u).wait_send()
                 gather.yhalf(d, u).wait_send()
+        all_sent(x_ref.at[pl.ds(0, NJ * ch)], sd.at[0])
+        all_sent(xc, sxe.at[0])
+        all_sent(st_own, sst.at[0])
         reduce.drain()
         ahead.drain()
         for r in range(NX):
             for u in range(2):
                 h_out(r, u).wait()
         o_pair.wait_send()
-        for half, i in pieces:
-            wa_copy(half, i, x).wait_send()
-            wo_copy(half, i, c).wait_send()
-        for half in range(2):
-            wp_copy(half, c).wait_send()
-
-        every = part.at[:, :, pl.ds(0, 3 * hc)]
-        remote(every, precv, spr.at[0], rpr.at[0], at.pb).wait_send()
-        remote(kvo, kvp, skv.at[0], rkv.at[0], at.partner).wait_send()
+        for sem in (swa, swo, swp):
+            all_sent(wb.at[pl.ds(0, kd)], sem.at[0])
+        all_sent(part.at[:, :, pl.ds(0, 3 * hc)], spr.at[0])
+        all_sent(kvo, skv.at[0])
         for kind, (lo, n) in enumerate(((0, ch), (0, ch), (0, cut), (cut, ch - cut))):
-            every = og.at[:, pl.ds(lo, n), o_cols(x)]
-            remote(every, every, sog.at[kind], rog.at[kind, 0], at.pa).wait_send()
+            all_sent(og.at[:, pl.ds(lo, n), o_cols(x)], sog.at[kind])
 
     waits = {"X": o_ready, "WP": angles}
     last = max(i for i, step in enumerate(ATTENTION_STEPS) if step[0] == "X")
@@ -875,11 +869,12 @@
             n = r * NJ + j
             for kind in (2, 3):
                 a_wait(kind, n)
+            lane = lax.broadcasted_iota(jnp.int32, (h, 128), 1)
             for q in range(NX):
                 cols = pl.ds(NX * fm + q * 128, 128)
-                rest = ar[n, :, q * 128 : (q + 1) * 128]
-                ag[n, 0:h, cols] = rest
-                ag[n, h:, cols] = pltpu.roll(rest.astype(F32), 64, axis=1).astype(BF16)
+                rest = ar[n, :, q * 128 : (q + 1) * 128].astype(F32)
+                ag[n, 0:h, cols] = jnp.where(lane < 64, rest, 0.0).astype(BF16)
+                ag[n, h:, cols] = jnp.where(lane < 64, pltpu.roll(rest, 64, axis=1), 0.0).astype(BF16)
 
         def done(col, size, out):
             for i, (r, j) in enumerate(GROUPS[g]):
@@ -994,10 +989,10 @@
                 vmem(2 * kc, 6 * hc), vmem(row_heads, kc), vmem(NCH, ch, 6 * hc), vmem(NCH, ch, 3 * hc), vmem(NCH, ch, hc),
                 vmem(NX, NJ, ch, 2 * hc), vmem(NX, NJ, ch, 2 * hc), vmem(NCH, ch, row_heads), *reduce_scratch,
                 vmem(2, fc, kd), vmem(2, f_a, kd), vmem(2, fc - f_a, kd),
-                sems(n_u), sems(n_u), sems(n_u), sems(n_u), sems(2, n_u), sems(2, n_u), sems(2, n_u), sems(2, n_u),
-                sems(NJ), sems(NJ), sems(2, 3), sems(2, 3), sems(2, 3), sems(2, 3), sems(2), sems(2), sems(3, 3), sems(1), sems(1),
-                sems(1), sems(NCH), sems(1), sems(NCH), sems(4), sems(4, NCH), sems(4, NJ), sems(4, NJ),
-                sems(2, 2), sems(2, 2, 2), sems(2, 2, 2), sems(2, 2), sems(2, 2), sems(2, 2), sems(2, 2), sems(2, 4), sems(2, 4),
+                sems(1), sems(n_u), sems(1), sems(n_u), sems(2, n_u), sems(2, n_u), sems(2, n_u), sems(2, n_u),
+                sems(1), sems(NJ), sems(1), sems(2, 3), sems(1), sems(2, 3), sems(1), sems(2), sems(3, 3), sems(1), sems(1),
+                sems(1), sems(NCH), sems(1), sems(NCH), sems(4), sems(4, NCH), sems(4), sems(4, NJ),
+                sems(2, 2), sems(2), sems(2, 2, 2), sems(2), sems(2, 2), sems(2), sems(2, 2), sems(1), sems(2, 4),
                 sems(4, 2), sems(4, 2), sems(2, 2), sems(2, 2), sems(2, 2), sems(2, 2), sems(NX, 2), sems(3 + NJ),
             ],
             compiler_params=pltpu.CompilerParams(collective_id=0, has_side_effects=True, vmem_limit_bytes=VMEM_LIMIT),
@@ -1018,7 +1013,7 @@
                 vmem(ch, 128, dtype=F32), vmem(ch, 128, dtype=F32),
                 *reduce_scratch, vmem(2, NJ, ch, kd),
                 sems(4, n_x), sems(4, n_x), sems(2, n_u), sems(2, n_u), sems(2, n_u), sems(2, n_u),
-                sems(4, 2), sems(4, NCH, 2), sems(4, NJ), sems(4, NJ), sems(NJ), sems(NJ),
+                sems(4, 2), sems(4, NCH, 2), sems(4), sems(4, NJ), sems(NJ), sems(NJ),
                 sems(2 * tiles), sems(NX, 2), sems(NX, 2), sems(NX, 2), sems(NX), sems(NJ + 1),
             ],
             compiler_params=pltpu.CompilerParams(collective_id=1, has_side_effects=True, vmem_limit_bytes=VMEM_LIMIT),

time: 328 us -> 327 us (level)
  no operation moved by 1% of the time
where the time goes in v12:
time: 327 us
  Pallas kernels  324 us (99%)
    pallas_call x1, Pallas kernels, layer(): pl.pallas_call(functools.partial(attention_kernel, units), out_shape=(jax...  180 us
    pallas_call x1, Pallas kernels, layer(): pl.pallas_call(functools.partial(mlp_kernel, units), out_shape=jax.ShapeD...  145 us

profile of v12, /device:TPU:97, one launch (start us, length us, event | category | flops | bytes accessed | tf_op | source)
XLA Modules:
  0.0 326.7 jit_solution(7839350237456836502)
XLA Ops:
  0.0 179.8 %attention_part.1 = (bf16[4,128,1024]{2,1,0:T(8,128)(2,1)}, bf16[2,688,4096]{2,1,0:T(8,128)(2,1)}, bf16[4,128,4096]{2,1,0:T(8,128)(2,1)}) custom-call(bf16[1024,512]{1,0:T(8,128)(2,1)} %bitcast.7, f32[2,128,128]{2,1,0:T(8,128)} %constant.4.clone.turn_hbm, f32[2,8,128]{2,1,0:T(8,128)} %constant.5.clone.base_hbm, bf16[512,1024]{1,0:T(8,128)(2,1)} %wq.1, ...), custom_call_target="tpu_custom_call" | custom-call | tf_op jit(solution)/shard_map/attention_part/pallas_call | solution.py:976
  179.8 144.6 %mlp_part.1 = bf16[1024,512]{1,0:T(8,128)(2,1)} custom-call(bf16[4,128,1024]{2,1,0:T(8,128)(2,1)} %get-tuple-element.8.h_hbm, bf16[2,688,4096]{2,1,0:T(8,128)(2,1)} %get-tuple-element.9.w_hbm, bf16[2752,512]{1,0:T(8,128)(2,1)} %wdn.1, bf16[4,128,4096]{2,1,0:T(8,128)(2,1)} %get-tuple-element.10.hg_hbm), custom_call_target="tpu_custom_call" | custom-call | tf_op jit(solution)/shard_map/mlp_part/pallas_call | solution.py:1004
  324.4 2.3 copy.12

commit v13 on v12

--- a/solution.py
+++ b/solution.py
@@ -52,13 +52,13 @@
     ("M", 2), ("M", 3), ("DP", 1), ("DP", 0), ("P", 3), ("HO", 0), ("X", 1), ("T", 1), ("X", 2), ("T", 2), ("X", 3), ("T", 3),
 )
 MLP_STEPS = (
-    ("XF", 0, 1), ("YR", 0), ("WT", 0), ("XF", 0, 0), ("XH", 0, 1), ("XF", 0, 3), ("YRH", 0), ("XF", 2, 0), ("N", 0, 1),
-    ("WT", 1), ("WT", 2), ("XH", 0, 3), ("XF", 0, 2), ("WT", 3), ("XF", 1, 0), ("XF", 3, 0), ("N", 0, 3), ("G", 8), ("YH", 1),
-    ("XH", 2, 0), ("G", 4), ("P", 8), ("XH", 3, 0), ("XH", 0, 0), ("XH", 0, 2), ("G", 3), ("XH", 1, 0), ("YH", 3), ("G", 7),
-    ("N", 2, 0), ("N", 0, 0), ("G", 9), ("N", 0, 2), ("P", 7), ("G", 11), ("P", 4), ("P", 9), ("N", 1, 0), ("N", 3, 0),
-    ("G", 5), ("X", 8), ("G", 1), ("X", 4), ("YH", 2), ("P", 11), ("G", 6), ("X", 9), ("X", 7), ("X", 11), ("P", 5), ("M", 0),
-    ("G", 10), ("G", 0), ("M", 3), ("X", 5), ("P", 10), ("P", 3), ("M", 1), ("P", 6), ("G", 2), ("P", 1), ("X", 10), ("X", 3),
-    ("P", 0), ("X", 6), ("M", 2), ("T", 3), ("P", 2), ("X", 1), ("T", 1), ("X", 0), ("T", 0), ("X", 2), ("T", 2),
+    ("XF", 0, 1), ("XF", 0, 0), ("WT", 0), ("YR", 0), ("WT", 1), ("XH", 0, 1), ("XF", 0, 3), ("YRH", 0), ("XF", 3, 0),
+    ("N", 0, 1), ("XH", 0, 3), ("XF", 1, 0), ("XF", 2, 0), ("WT", 2), ("WT", 3), ("N", 0, 3), ("XF", 0, 2), ("G", 4),
+    ("YH", 1), ("G", 0), ("XH", 2, 0), ("G", 8), ("XH", 1, 0), ("XH", 0, 0), ("XH", 3, 0), ("XH", 0, 2), ("G", 3), ("YH", 3),
+    ("G", 7), ("N", 3, 0), ("N", 0, 2), ("N", 1, 0), ("P", 8), ("N", 2, 0), ("G", 9), ("G", 11), ("P", 4), ("G", 5), ("P", 11),
+    ("X", 8), ("P", 7), ("P", 9), ("X", 4), ("YH", 2), ("G", 6), ("X", 11), ("X", 7), ("P", 5), ("X", 9), ("N", 0, 0),
+    ("M", 0), ("G", 10), ("G", 1), ("M", 3), ("X", 5), ("M", 1), ("P", 10), ("P", 6), ("P", 0), ("G", 2), ("X", 10), ("P", 3),
+    ("P", 1), ("X", 6), ("M", 2), ("P", 2), ("X", 0), ("T", 0), ("X", 3), ("T", 3), ("X", 1), ("T", 1), ("X", 2), ("T", 2),
 )
 
 
@@ -213,9 +213,7 @@
     return refs[0][...] if len(refs) == 1 else jnp.concatenate([ref[...] for ref in refs], axis=0)
 
 
-def product(refs, weight, depth, n_cols, done):
-    step = 256
-
+def product(refs, weight, depth, n_cols, done, step=256):
     def columns(i, carry):
         out = jnp.dot(rows_of(refs), weight[0:depth, pl.ds(al(i * step, 128), step)], preferred_element_type=F32)
         done(i * step, step, out)
@@ -289,17 +287,33 @@
 
     def middle(self, j):
         h = self.h
+
+        def add(r, lo, part):
+            def some_rows(i, carry):
+                rows, src = pl.ds(al(lo + i * 32, 8), 32), pl.ds(al(i * 32, 8), 32)
+                self.zb[r, j, rows, :] = (self.zb[r, j, rows, :].astype(F32) + part[j, src, :].astype(F32)).astype(BF16)
+                return carry
+
+            lax.fori_loop(0, h // 32, some_rows, 0)
+
         self.wait(0, j)
-        self.zb[1, j, 0:h] = (self.zb[1, j, 0:h].astype(F32) + self.ya[j].astype(F32)).astype(BF16)
+        add(1, 0, self.ya)
         self.copy(2, j).start()
         self.wait(1, j)
-        self.zb[3, j, h:] = (self.zb[3, j, h:].astype(F32) + self.yb[j].astype(F32)).astype(BF16)
+        add(3, h, self.yb)
         self.copy(3, j).start()
 
-    def total(self, j):
+    def total(self, j, done):
         self.wait(2, j)
         self.wait(3, j)
-        return self.zb[0, j].astype(F32) + self.yfd[j].astype(F32) + self.yfu[j].astype(F32)
+
+        def some_rows(i, carry):
+            rows = pl.ds(al(i * 32, 8), 32)
+            out = self.zb[0, j, rows, :].astype(F32) + self.yfd[j, rows, :].astype(F32) + self.yfu[j, rows, :].astype(F32)
+            done(rows, out)
+            return carry
+
+        lax.fori_loop(0, self.ch // 32, some_rows, 0)
 
     def drain(self):
         h = self.h
@@ -646,8 +660,10 @@
                 reduce.halves(j)
 
     def T(j):
-        attn = reduce.total(j).astype(BF16)
-        h_ref[j] = (xc[j].astype(F32) + attn.astype(F32)).astype(BF16)
+        def done(rows, attn):
+            h_ref[j, rows, :] = (xc[j, rows, :].astype(F32) + attn.astype(BF16).astype(F32)).astype(BF16)
+
+        reduce.total(j, done)
         chunk_out(j).start()
 
     def chunk_out(j):
@@ -880,7 +896,7 @@
             for i, (r, j) in enumerate(GROUPS[g]):
                 zb[r, j, :, pl.ds(al(col, 128), size)] = out[i * ch : (i + 1) * ch].astype(BF16)
 
-        product([ag.at[r * NJ + j] for r, j in GROUPS[g]], wd, wd.shape[0], kc, done)
+        product([ag.at[r * NJ + j] for r, j in GROUPS[g]], wd, wd.shape[0], kc, done, 512 if len(GROUPS[g]) == 1 else 256)
         for r, j in GROUPS[g]:
             if r == 2:
                 reduce.halves(j)
@@ -899,10 +915,12 @@
         remote(dst, dst, sd.at[j], rd.at[j], at.partner).wait_recv()
 
     def T(j):
-        mlp = reduce.total(j).astype(BF16)
-        out = (h_ref[j].astype(F32) + mlp.astype(F32)).astype(BF16)
-        yst[0, j] = out[:, :kd]
-        yst[1, j] = out[:, kd:]
+        def done(rows, mlp):
+            out = (h_ref[j, rows, :].astype(F32) + mlp.astype(BF16).astype(F32)).astype(BF16)
+            yst[0, j, rows, :] = out[:, :kd]
+            yst[1, j, rows, :] = out[:, kd:]
+
+        reduce.total(j, done)
         y_copy(j).start()
         y_own(j).start()
 

time: 327 us -> 325 us (level)
  no operation moved by 1% of the time
where the time goes in v13:
time: 325 us
  Pallas kernels  323 us (99%)
    pallas_call x1, Pallas kernels, layer(): pl.pallas_call(functools.partial(attention_kernel, units), out_shape=(jax...  180 us
    pallas_call x1, Pallas kernels, layer(): pl.pallas_call(functools.partial(mlp_kernel, units), out_shape=jax.ShapeD...  143 us

profile of v13, /device:TPU:97, one launch (start us, length us, event | category | flops | bytes accessed | tf_op | source)
XLA Modules:
  0.0 325.3 jit_solution(4453705356765764394)
XLA Ops:
  0.0 179.8 %attention_part.1 = (bf16[4,128,1024]{2,1,0:T(8,128)(2,1)}, bf16[2,688,4096]{2,1,0:T(8,128)(2,1)}, bf16[4,128,4096]{2,1,0:T(8,128)(2,1)}) custom-call(bf16[1024,512]{1,0:T(8,128)(2,1)} %bitcast.7, f32[2,128,128]{2,1,0:T(8,128)} %constant.4.clone.turn_hbm, f32[2,8,128]{2,1,0:T(8,128)} %constant.5.clone.base_hbm, bf16[512,1024]{1,0:T(8,128)(2,1)} %wq.1, ...), custom_call_target="tpu_custom_call" | custom-call | tf_op jit(solution)/shard_map/attention_part/pallas_call | solution.py:994
  179.8 143.2 %mlp_part.1 = bf16[1024,512]{1,0:T(8,128)(2,1)} custom-call(bf16[4,128,1024]{2,1,0:T(8,128)(2,1)} %get-tuple-element.8.h_hbm, bf16[2,688,4096]{2,1,0:T(8,128)(2,1)} %get-tuple-element.9.w_hbm, bf16[2752,512]{1,0:T(8,128)(2,1)} %wdn.1, bf16[4,128,4096]{2,1,0:T(8,128)(2,1)} %get-tuple-element.10.hg_hbm), custom_call_target="tpu_custom_call" | custom-call | tf_op jit(solution)/shard_map/mlp_part/pallas_call | solution.py:1022
  323.0 2.3 copy.12

commit v14 on v13

--- a/solution.py
+++ b/solution.py
@@ -214,6 +214,8 @@
 
 
 def product(refs, weight, depth, n_cols, done, step=256):
+    step = 256 if n_cols % step else step
+
     def columns(i, carry):
         out = jnp.dot(rows_of(refs), weight[0:depth, pl.ds(al(i * step, 128), step)], preferred_element_type=F32)
         done(i * step, step, out)
@@ -880,7 +882,7 @@
                 a_wait(kind, r * NJ + j)
                 a_start(kind + 2, r * NJ + j)
 
-    def X(g):
+    def unpack(g):
         for r, j in GROUPS[g]:
             n = r * NJ + j
             for kind in (2, 3):
@@ -892,6 +894,9 @@
                 ag[n, 0:h, cols] = jnp.where(lane < 64, rest, 0.0).astype(BF16)
                 ag[n, h:, cols] = jnp.where(lane < 64, pltpu.roll(rest, 64, axis=1), 0.0).astype(BF16)
 
+    def X(g):
+        unpack(g)
+
         def done(col, size, out):
             for i, (r, j) in enumerate(GROUPS[g]):
                 zb[r, j, :, pl.ds(al(col, 128), size)] = out[i * ch : (i + 1) * ch].astype(BF16)
@@ -900,6 +905,9 @@
         for r, j in GROUPS[g]:
             if r == 2:
                 reduce.halves(j)
+
+    def half_cols(core):
+        return pl.ds(al(core * kd, 128), kd)
 
     def y_rows(j, core):
         return pl.ds(al((2 * j + core) * ch, 8), ch)
@@ -924,7 +932,25 @@
         y_copy(j).start()
         y_own(j).start()
 
-    ops = {"G": G, "P": P, "X": X, "M": reduce.middle, "T": T, "WT": WT}
+    def XT(g):
+        ((_, j),) = GROUPS[g]
+        unpack(g)
+        reduce.wait(2, j)
+        reduce.wait(3, j)
+
+        def half(i, carry):
+            core = 1 - c + i * (2 * c - 1)
+            cols = half_cols(core)
+            out = jnp.dot(ag[j], wd[:, cols], preferred_element_type=F32).astype(BF16).astype(F32)
+            mlp = out + yfd[j, :, cols].astype(F32) + yfu[j, :, cols].astype(F32)
+            yst[core, j] = (h_ref[j, :, cols].astype(F32) + mlp.astype(BF16).astype(F32)).astype(BF16)
+            pl.when(i == 0)(lambda: y_copy(j).start())
+            return carry
+
+        lax.fori_loop(0, 2, half, 0)
+        y_own(j).start()
+
+    ops = {"G": G, "P": P, "X": X, "M": reduce.middle, "T": T, "XT": XT, "WT": WT}
     for name in ("YR", "YRH", "YH", "XF", "XH", "N"):
         ops[name] = getattr(gather, name)
     waits = {
@@ -942,7 +968,9 @@
             for k, every in enumerate(a_refs(kind, slice(None), x)):
                 remote(every, every, sa.at[kind, k], ra.at[kind, 0, k], at.right).wait_send()
 
-    for step in MLP_STEPS:
+    (_, g), (_, j) = MLP_STEPS[-2:]
+    assert MLP_STEPS[-2:] == (("X", g), ("T", j)) and GROUPS[g] == ((0, j),)
+    for step in (*MLP_STEPS[:-2], ("XT", g)):
         if step[0] in waits:
             waits.pop(step[0])()
         ops[step[0]](*step[1:])

time: 325 us -> 325 us (level)
  no operation moved by 1% of the time
where the time goes in v14:
time: 325 us
  Pallas kernels  322 us (99%)
    pallas_call x1, Pallas kernels, layer(): pl.pallas_call(functools.partial(attention_kernel, units), out_shape=(jax...  180 us
    pallas_call x1, Pallas kernels, layer(): pl.pallas_call(functools.partial(mlp_kernel, units), out_shape=jax.ShapeD...  142 us

profile of v14, /device:TPU:97, one launch (start us, length us, event | category | flops | bytes accessed | tf_op | source)
XLA Modules:
  0.0 324.5 jit_solution(14432763665157163450)
XLA Ops:
  0.0 179.8 %attention_part.1 = (bf16[4,128,1024]{2,1,0:T(8,128)(2,1)}, bf16[2,688,4096]{2,1,0:T(8,128)(2,1)}, bf16[4,128,4096]{2,1,0:T(8,128)(2,1)}) custom-call(bf16[1024,512]{1,0:T(8,128)(2,1)} %bitcast.7, f32[2,128,128]{2,1,0:T(8,128)} %constant.4.clone.turn_hbm, f32[2,8,128]{2,1,0:T(8,128)} %constant.5.clone.base_hbm, bf16[512,1024]{1,0:T(8,128)(2,1)} %wq.1, ...), custom_call_target="tpu_custom_call" | custom-call | tf_op jit(solution)/shard_map/attention_part/pallas_call | solution.py:1022
  179.8 142.5 %mlp_part.1 = bf16[1024,512]{1,0:T(8,128)(2,1)} custom-call(bf16[4,128,1024]{2,1,0:T(8,128)(2,1)} %get-tuple-element.8.h_hbm, bf16[2,688,4096]{2,1,0:T(8,128)(2,1)} %get-tuple-element.9.w_hbm, bf16[2752,512]{1,0:T(8,128)(2,1)} %wdn.1, bf16[4,128,4096]{2,1,0:T(8,128)(2,1)} %get-tuple-element.10.hg_hbm), custom_call_target="tpu_custom_call" | custom-call | tf_op jit(solution)/shard_map/mlp_part/pallas_call | solution.py:1050
  322.3 2.3 copy.12

commit v15 on v14

--- a/solution.py
+++ b/solution.py
@@ -656,7 +656,7 @@
             for i, (r, j) in enumerate(GROUPS[g]):
                 zb[r, j, :, pl.ds(al(col, 128), size)] = out[i * ch : (i + 1) * ch].astype(BF16)
 
-        product([og.at[r * NJ + j] for r, j in GROUPS[g]], wob, wob.shape[0], kc, done)
+        product([og.at[r * NJ + j] for r, j in GROUPS[g]], wob, wob.shape[0], kc, done, 512 if GROUPS[g][0][0] == 0 else 256)
         for r, j in GROUPS[g]:
             if r == 2:
                 reduce.halves(j)

time: 325 us -> 324 us (level)
  no operation moved by 1% of the time
where the time goes in v15:
time: 324 us
  Pallas kernels  322 us (99%)
    pallas_call x1, Pallas kernels, layer(): pl.pallas_call(functools.partial(attention_kernel, units), out_shape=(jax...  179 us
    pallas_call x1, Pallas kernels, layer(): pl.pallas_call(functools.partial(mlp_kernel, units), out_shape=jax.ShapeD...  142 us

profile of v15, /device:TPU:97, one launch (start us, length us, event | category | flops | bytes accessed | tf_op | source)
XLA Modules:
  0.0 324.0 jit_solution(18063801678506115476)
XLA Ops:
  0.0 179.4 %attention_part.1 = (bf16[4,128,1024]{2,1,0:T(8,128)(2,1)}, bf16[2,688,4096]{2,1,0:T(8,128)(2,1)}, bf16[4,128,4096]{2,1,0:T(8,128)(2,1)}) custom-call(bf16[1024,512]{1,0:T(8,128)(2,1)} %bitcast.7, f32[2,128,128]{2,1,0:T(8,128)} %constant.4.clone.turn_hbm, f32[2,8,128]{2,1,0:T(8,128)} %constant.5.clone.base_hbm, bf16[512,1024]{1,0:T(8,128)(2,1)} %wq.1, ...), custom_call_target="tpu_custom_call" | custom-call | tf_op jit(solution)/shard_map/attention_part/pallas_call | solution.py:1022
  179.4 142.2 %mlp_part.1 = bf16[1024,512]{1,0:T(8,128)(2,1)} custom-call(bf16[4,128,1024]{2,1,0:T(8,128)(2,1)} %get-tuple-element.8.h_hbm, bf16[2,688,4096]{2,1,0:T(8,128)(2,1)} %get-tuple-element.9.w_hbm, bf16[2752,512]{1,0:T(8,128)(2,1)} %wdn.1, bf16[4,128,4096]{2,1,0:T(8,128)(2,1)} %get-tuple-element.10.hg_hbm), custom_call_target="tpu_custom_call" | custom-call | tf_op jit(solution)/shard_map/mlp_part/pallas_call | solution.py:1050
  321.7 2.3 copy.12

commit v16 on v15

--- a/solution.py
+++ b/solution.py
@@ -823,18 +823,21 @@
     quarters = [(q, k) for q in range(NX) for k in range(2)]
     h_in_all = pltpu.make_async_copy(h_hbm, h_ref, lo.at[NJ])
     h_in_all.start()
-    for q in range(slots):
-        w_in(q).start()
     def h_in(s):
         return pltpu.make_async_copy(hg_hbm.at[s], xg.at[s, 0], lh.at[s])
 
-    for s in range(NX):
-        h_in(s).start()
-    for q, k in quarters:
-        d_own(q, k).start()
-    for q in range(NX):
-        wd[NX * fm + q * 128 + fr : NX * fm + (q + 1) * 128, :] = jnp.zeros((128 - fr, kc), BF16)
-    at.barrier(h_in_all.wait)
+    def local_copies():
+        for q in range(slots):
+            w_in(q).start()
+        for s in range(NX):
+            h_in(s).start()
+        for q, k in quarters:
+            d_own(q, k).start()
+        for q in range(NX):
+            wd[NX * fm + q * 128 + fr : NX * fm + (q + 1) * 128, :] = jnp.zeros((128 - fr, kc), BF16)
+        h_in_all.wait()
+
+    at.barrier(local_copies)
     for q, k in quarters:
         d_pair(q, k, c).start()
 

time: 324 us -> 322 us (level)
  no operation moved by 1% of the time
where the time goes in v16:
time: 322 us
  Pallas kernels  319 us (99%)
    pallas_call x1, Pallas kernels, layer(): pl.pallas_call(functools.partial(attention_kernel, units), out_shape=(jax...  179 us
    pallas_call x1, Pallas kernels, layer(): pl.pallas_call(functools.partial(mlp_kernel, units), out_shape=jax.ShapeD...  140 us

profile of v16, /device:TPU:97, one launch (start us, length us, event | category | flops | bytes accessed | tf_op | source)
XLA Modules:
  0.0 321.6 jit_solution(3408416065504312827)
XLA Ops:
  0.0 179.4 %attention_part.1 = (bf16[4,128,1024]{2,1,0:T(8,128)(2,1)}, bf16[2,688,4096]{2,1,0:T(8,128)(2,1)}, bf16[4,128,4096]{2,1,0:T(8,128)(2,1)}) custom-call(bf16[1024,512]{1,0:T(8,128)(2,1)} %bitcast.7, f32[2,128,128]{2,1,0:T(8,128)} %constant.4.clone.turn_hbm, f32[2,8,128]{2,1,0:T(8,128)} %constant.5.clone.base_hbm, bf16[512,1024]{1,0:T(8,128)(2,1)} %wq.1, ...), custom_call_target="tpu_custom_call" | custom-call | tf_op jit(solution)/shard_map/attention_part/pallas_call | solution.py:1025
  179.4 139.8 %mlp_part.1 = bf16[1024,512]{1,0:T(8,128)(2,1)} custom-call(bf16[4,128,1024]{2,1,0:T(8,128)(2,1)} %get-tuple-element.8.h_hbm, bf16[2,688,4096]{2,1,0:T(8,128)(2,1)} %get-tuple-element.9.w_hbm, bf16[2752,512]{1,0:T(8,128)(2,1)} %wdn.1, bf16[4,128,4096]{2,1,0:T(8,128)(2,1)} %get-tuple-element.10.hg_hbm), custom_call_target="tpu_custom_call" | custom-call | tf_op jit(solution)/shard_map/mlp_part/pallas_call | solution.py:1053
  319.3 2.3 copy.12

commit v17 on v16

--- a/solution.py
+++ b/solution.py
@@ -693,21 +693,23 @@
             ahead.yhalf_wait(d, u)
         h_out(2, u).start()
 
-    def own_rows():
+    def local_weights():
         for half, i in pieces:
             w_local(half, i).start()
         o_local.start()
         for m in range(2):
             d_in(m).start()
+
+    def own_rows():
+        x_in.start()
+        for copy in tables:
+            copy.start()
         x_in.wait()
         for j in range(NJ):
             xc[j, :, half_cols(c)] = x_ref[x_rows(j, c), :]
 
     x_in = pltpu.make_async_copy(x_hbm, x_ref, lx.at[0])
-    x_in.start()
     tables = [pltpu.make_async_copy(src, dst, lx.at[1 + NJ + i]) for i, (src, dst) in enumerate(((turn_hbm, turn_ref), (base_hbm, base_ref)))]
-    for copy in tables:
-        copy.start()
     at.barrier(own_rows)
 
     def angles():
@@ -757,7 +759,7 @@
         for kind, (lo, n) in enumerate(((0, ch), (0, ch), (0, cut), (cut, ch - cut))):
             all_sent(og.at[:, pl.ds(lo, n), o_cols(x)], sog.at[kind])
 
-    waits = {"X": o_ready, "WP": angles}
+    waits = {"X": o_ready, "WP": angles, "ST": local_weights}
     last = max(i for i, step in enumerate(ATTENTION_STEPS) if step[0] == "X")
     for i, step in enumerate(ATTENTION_STEPS):
         if step[0] in waits:

time: 322 us -> 322 us (level)
  no operation moved by 1% of the time
where the time goes in v17:
time: 322 us
  Pallas kernels  319 us (99%)
    pallas_call x1, Pallas kernels, layer(): pl.pallas_call(functools.partial(attention_kernel, units), out_shape=(jax...  179 us
    pallas_call x1, Pallas kernels, layer(): pl.pallas_call(functools.partial(mlp_kernel, units), out_shape=jax.ShapeD...  140 us

profile of v17, /device:TPU:97, one launch (start us, length us, event | category | flops | bytes accessed | tf_op | source)
XLA Modules:
  0.0 321.6 jit_solution(3873508849950897640)
XLA Ops:
  0.0 179.4 %attention_part.1 = (bf16[4,128,1024]{2,1,0:T(8,128)(2,1)}, bf16[2,688,4096]{2,1,0:T(8,128)(2,1)}, bf16[4,128,4096]{2,1,0:T(8,128)(2,1)}) custom-call(bf16[1024,512]{1,0:T(8,128)(2,1)} %bitcast.7, f32[2,128,128]{2,1,0:T(8,128)} %constant.4.clone.turn_hbm, f32[2,8,128]{2,1,0:T(8,128)} %constant.5.clone.base_hbm, bf16[512,1024]{1,0:T(8,128)(2,1)} %wq.1, ...), custom_call_target="tpu_custom_call" | custom-call | tf_op jit(solution)/shard_map/attention_part/pallas_call | solution.py:1027
  179.4 139.9 %mlp_part.1 = bf16[1024,512]{1,0:T(8,128)(2,1)} custom-call(bf16[4,128,1024]{2,1,0:T(8,128)(2,1)} %get-tuple-element.8.h_hbm, bf16[2,688,4096]{2,1,0:T(8,128)(2,1)} %get-tuple-element.9.w_hbm, bf16[2752,512]{1,0:T(8,128)(2,1)} %wdn.1, bf16[4,128,4096]{2,1,0:T(8,128)(2,1)} %get-tuple-element.10.hg_hbm), custom_call_target="tpu_custom_call" | custom-call | tf_op jit(solution)/shard_map/mlp_part/pallas_call | solution.py:1055
  319.3 2.3 copy.12
